TPU v7x, 32 devices: a whole 2x2x4 slice. The times are simulated.
32 devices in a mesh: dp: 2 (over core), row: 4 (over y, x), col: 4 (over z).
Axes of the slice: x: 2, y: 2, z: 4, core: 2. Of those that a mesh axis runs over, the one named last changes fastest.
Arguments:
- tokens: bfloat16 [8, 257, 1408], P(('dp', 'col'), None, 'row'), may hold values from -6 to 6
- cotangent: bfloat16 [8, 257, 1408], P(('dp', 'col'), None, 'row'), may hold values from -6 to 6
- qkv_weight: bfloat16 [2, 1408, 3, 1408], P(None, 'row', None, 'col'), may hold values from -0.15625 to 0.15625
- qv_bias: float32 [2, 2, 1408], P(None, None, 'col'), may hold values from -3 to 3
- proj_weight: bfloat16 [2, 1408, 1408], P(None, 'col', 'row'), may hold values from -0.625 to 0.625
- proj_bias: float32 [2, 1408], P(None, 'row'), may hold values from -3 to 3
- up_weight: bfloat16 [2, 1408, 6144], P(None, 'row', 'col'), may hold values from -0.15625 to 0.15625
- up_bias: float32 [2, 6144], P(None, 'col'), may hold values from -3 to 3
- down_weight: bfloat16 [2, 6144, 1408], P(None, 'col', 'row'), may hold values from -0.078125 to 0.078125
- down_bias: float32 [2, 1408], P(None, 'row'), may hold values from -3 to 3
- norm_gain: float32 [2, 2, 1408], P(None, None, 'row'), may hold values from 0.25 to 1.75
- norm_shift: float32 [2, 2, 1408], P(None, None, 'row'), may hold values from -3 to 3
Outputs:
- out: float32 [8, 257, 1408], P(('dp', 'col'), None, 'row')
- tokens_grad: float32 [8, 257, 1408], P(('dp', 'col'), None, 'row')
- qkv_weight_grad: float32 [2, 1408, 3, 1408], P('dp', 'row', None, 'col')
- qv_bias_grad: float32 [2, 2, 1408], P('dp', None, 'col')
- proj_weight_grad: float32 [2, 1408, 1408], P('dp', 'col', 'row')
- proj_bias_grad: float32 [2, 1408], P('dp', 'row')
- up_weight_grad: float32 [2, 1408, 6144], P('dp', 'row', 'col')
- up_bias_grad: float32 [2, 6144], P('dp', 'col')
- down_weight_grad: float32 [2, 6144, 1408], P('dp', 'col', 'row')
- down_bias_grad: float32 [2, 1408], P('dp', 'row')
- norm_gain_grad: float32 [2, 2, 1408], P(None, None, 'row')
- norm_shift_grad: float32 [2, 2, 1408], P(None, None, 'row')
All inputs are finite; a program needn't handle non-finite values.
Results may differ from a plain program's by a relative error of at most 0.03.
Values may be sent and summed in bfloat16 or wider, within the bound.
A program may use at most 128 MiB of HBM per device.

v0:
```python
from functools import partial

import jax
import jax.numpy as jnp
from jax import lax
from jax.sharding import PartitionSpec as P

D = 1408
HEAD_DIM = 88
SEQ = 257
LAYERS = 2


EPSILON = 1e-06
NORMAL = (((1,), (0,)), ((), ()))
LAST_BOTH = (((1,), (1,)), ((), ()))
FIRST_BOTH = (((0,), (0,)), ((), ()))


def gather_tokens(values):
    return lax.all_gather(values, "col", axis=0, tiled=True)


def gather_blocks(values):
    return lax.all_gather(values, "row", axis=0, tiled=True)


def gather_grad_blocks(values):
    return lax.all_gather(values, "row", axis=0, tiled=True)


def width_totals(first_sum, second_sum):
    return lax.psum((first_sum, second_sum), "row")


def gather_whole(triple_w, up_w, proj_w, down_w):
    row_whole = (triple_w, up_w, proj_w, down_w)
    col_whole = (proj_w, down_w, triple_w, up_w)
    return (row_whole, col_whole)


def row_product(gathered, matrix, contract):
    return lax.psum_scatter(
        lax.dot_general(gathered, matrix, contract, preferred_element_type=jnp.float32).astype(
            jnp.bfloat16
        ),
        "row",
        scatter_dimension=0,
        tiled=True,
    ).astype(jnp.float32)


def col_product(gathered, matrix, contract):
    return lax.psum_scatter(
        lax.dot_general(gathered, matrix, contract, preferred_element_type=jnp.float32).astype(
            jnp.bfloat16
        ),
        "col",
        scatter_dimension=0,
        tiled=True,
    ).astype(jnp.float32)


def norm_forward(stream, factor, shift):
    totals, squares = width_totals(jnp.sum(stream, axis=1), jnp.sum(stream * stream, axis=1))
    centre = totals / D
    spread = squares / D - centre * centre
    centred = stream - centre[:, None]
    scaling = lax.rsqrt(spread + EPSILON)
    standard = centred * scaling[:, None]
    return (standard * factor + shift, standard, scaling)


def norm_backward(grad_norm, standard, scaling, factor):
    factor_grad = jnp.sum(grad_norm * standard, axis=0)
    shift_grad = jnp.sum(grad_norm, axis=0)
    grad_standard = grad_norm * factor
    first_sum, second_sum = width_totals(
        jnp.sum(grad_standard, axis=1), jnp.sum(grad_standard * standard, axis=1)
    )
    grad_stream = scaling[:, None] * (
        grad_standard - first_sum[:, None] / D - standard * (second_sum[:, None] / D)
    )
    return (grad_stream, factor_grad, shift_grad)


def split_triple(triple_out, width):
    images = triple_out.shape[0] // SEQ
    head_count = width // HEAD_DIM
    pieces = triple_out.reshape(images, SEQ, 3, head_count, HEAD_DIM)
    return (pieces[:, :, 0], pieces[:, :, 1], pieces[:, :, 2])


def attend_forward(triple_out, width):
    queries, key_rows, values = split_triple(triple_out, width)
    scaling = HEAD_DIM ** (-0.5)
    scores = (
        jnp.einsum("bqhd,bkhd->bhqk", queries, key_rows, preferred_element_type=jnp.float32)
        * scaling
    )
    row_peak = jnp.max(scores, axis=-1, keepdims=True)
    log_totals = row_peak + jnp.log(jnp.sum(jnp.exp(scores - row_peak), axis=-1, keepdims=True))
    probs_low = jnp.exp(scores - log_totals).astype(jnp.bfloat16)
    attended = jnp.einsum("bhqk,bkhd->bqhd", probs_low, values, preferred_element_type=jnp.float32)
    return (attended.reshape(triple_out.shape[0], width).astype(jnp.bfloat16), log_totals)


def attend_backward(triple_out, log_totals, grad_attended, width):
    queries, key_rows, values = split_triple(triple_out, width)
    scaling = HEAD_DIM ** (-0.5)
    scores = (
        jnp.einsum("bqhd,bkhd->bhqk", queries, key_rows, preferred_element_type=jnp.float32)
        * scaling
    )
    probs = jnp.exp(scores - log_totals)
    probs_low = probs.astype(jnp.bfloat16)
    grad_heads = grad_attended.reshape(values.shape)
    grad_values = jnp.einsum(
        "bhqk,bqhd->bkhd", probs_low, grad_heads, preferred_element_type=jnp.float32
    )
    grad_probs = jnp.einsum(
        "bqhd,bkhd->bhqk", grad_heads, values, preferred_element_type=jnp.float32
    )
    grad_scores = (
        probs * (grad_probs - jnp.sum(grad_probs * probs, axis=-1, keepdims=True))
    ).astype(jnp.bfloat16)
    grad_queries = (
        jnp.einsum("bhqk,bkhd->bqhd", grad_scores, key_rows, preferred_element_type=jnp.float32)
        * scaling
    )
    grad_keys = (
        jnp.einsum("bhqk,bqhd->bkhd", grad_scores, queries, preferred_element_type=jnp.float32)
        * scaling
    )
    stacked = jnp.stack([grad_queries, grad_keys, grad_values], axis=2)
    return stacked.reshape(triple_out.shape[0], 3 * width).astype(jnp.bfloat16)


def layer_forward(stream, weights):
    qkv_w, qv_b, proj_w, proj_b, up_w, up_b, down_w, down_b, factors, shifts = weights
    width = qkv_w.shape[2]
    triple_w = qkv_w.reshape(qkv_w.shape[0], 3 * width)
    row_whole, col_whole = gather_whole(triple_w, up_w, proj_w, down_w)
    first_norm, first_standard, first_scaling = norm_forward(stream, factors[0], shifts[0])
    first_rows = gather_tokens(first_norm.astype(jnp.bfloat16))
    offsets = jnp.concatenate([qv_b[0], jnp.zeros_like(qv_b[0]), qv_b[1]])
    triple_out = (row_product(first_rows, triple_w, NORMAL) + offsets).astype(jnp.bfloat16)
    attended, log_totals = attend_forward(triple_out, width)
    head_rows = gather_blocks(attended)
    stream_mid = stream + col_product(head_rows, proj_w, NORMAL) + proj_b
    second_norm, second_standard, second_scaling = norm_forward(stream_mid, factors[1], shifts[1])
    second_rows = gather_tokens(second_norm.astype(jnp.bfloat16))
    before = row_product(second_rows, up_w, NORMAL) + up_b
    activated = jax.nn.gelu(before, approximate=False).astype(jnp.bfloat16)
    hidden_rows = gather_blocks(activated)
    branch_out = col_product(hidden_rows, down_w, NORMAL)
    stream_out = stream_mid + branch_out + down_b
    saved = (
        first_rows,
        first_standard,
        first_scaling,
        triple_out,
        log_totals,
        head_rows,
        second_rows,
        second_standard,
        second_scaling,
        before,
        hidden_rows,
        row_whole,
        col_whole,
    )
    return (stream_out, saved)


def layer_backward(grad_out, saved, weights):
    qkv_w, qv_b, proj_w, proj_b, up_w, up_b, down_w, down_b, factors, shifts = weights
    (
        first_rows,
        first_standard,
        first_scaling,
        triple_out,
        log_totals,
        head_rows,
        second_rows,
        second_standard,
        second_scaling,
        before,
        hidden_rows,
        row_whole,
        col_whole,
    ) = saved
    width = qkv_w.shape[2]
    triple_w = qkv_w.reshape(qkv_w.shape[0], 3 * width)
    grad_rows = gather_tokens(grad_out.astype(jnp.bfloat16))
    down_grad = lax.dot_general(
        hidden_rows, grad_rows, FIRST_BOTH, preferred_element_type=jnp.float32
    )
    down_off_grad = jnp.sum(grad_rows, axis=0, dtype=jnp.float32)
    grad_active = row_product(grad_rows, down_w, LAST_BOTH)
    _, slope_pull = jax.vjp(partial(jax.nn.gelu, approximate=False), before)
    grad_before = slope_pull(grad_active)[0].astype(jnp.bfloat16)
    before_rows = gather_grad_blocks(grad_before)
    up_grad = lax.dot_general(
        second_rows, before_rows, FIRST_BOTH, preferred_element_type=jnp.float32
    )
    up_off_grad = jnp.sum(before_rows, axis=0, dtype=jnp.float32)
    grad_second = col_product(before_rows, up_w, LAST_BOTH)
    grad_mid, second_factor_grad, second_shift_grad = norm_backward(
        grad_second, second_standard, second_scaling, factors[1]
    )
    grad_mid = grad_mid + grad_out
    mid_rows = gather_tokens(grad_mid.astype(jnp.bfloat16))
    proj_grad = lax.dot_general(head_rows, mid_rows, FIRST_BOTH, preferred_element_type=jnp.float32)
    proj_off_grad = jnp.sum(mid_rows, axis=0, dtype=jnp.float32)
    grad_attended = row_product(mid_rows, proj_w, LAST_BOTH).astype(jnp.bfloat16)
    grad_triple = attend_backward(triple_out, log_totals, grad_attended, width)
    triple_rows = gather_grad_blocks(grad_triple)
    triple_grad = lax.dot_general(
        first_rows, triple_rows, FIRST_BOTH, preferred_element_type=jnp.float32
    )
    column_sums = jnp.sum(triple_rows, axis=0, dtype=jnp.float32).reshape(3, width)
    qv_grad = jnp.stack([column_sums[0], column_sums[2]])
    grad_first = col_product(triple_rows, triple_w, LAST_BOTH)
    grad_in, first_factor_grad, first_shift_grad = norm_backward(
        grad_first, first_standard, first_scaling, factors[0]
    )
    grad_in = grad_in + grad_mid
    factor_grads = jnp.stack([first_factor_grad, second_factor_grad])
    shift_grads = jnp.stack([first_shift_grad, second_shift_grad])
    layer_grads = (
        triple_grad.reshape(qkv_w.shape),
        qv_grad,
        proj_grad,
        proj_off_grad,
        up_grad,
        up_off_grad,
        down_grad,
        down_off_grad,
        factor_grads,
        shift_grads,
    )
    return (grad_in, layer_grads)


def per_device(
    tokens,
    cotangent,
    qkv_weight,
    qv_bias,
    proj_weight,
    proj_bias,
    up_weight,
    up_bias,
    down_weight,
    down_bias,
    norm_gain,
    norm_shift,
):
    image_count, seq_len, width_row = tokens.shape
    stream = tokens.reshape(image_count * seq_len, width_row).astype(jnp.float32)
    layer_params = []
    saved_list = []
    for layer_index in range(LAYERS):
        params = (
            qkv_weight[layer_index],
            qv_bias[layer_index],
            proj_weight[layer_index],
            proj_bias[layer_index],
            up_weight[layer_index],
            up_bias[layer_index],
            down_weight[layer_index],
            down_bias[layer_index],
            norm_gain[layer_index],
            norm_shift[layer_index],
        )
        layer_params.append(params)
        stream, saved = layer_forward(stream, params)
        saved_list.append(saved)
    grad_stream = cotangent.reshape(image_count * seq_len, width_row).astype(jnp.float32)
    per_layer = [None] * LAYERS
    for layer_index in reversed(range(LAYERS)):
        grad_stream, layer_grads = layer_backward(
            grad_stream, saved_list[layer_index], layer_params[layer_index]
        )
        per_layer[layer_index] = layer_grads
    stacked = tuple(
        (jnp.stack([layer_grads[position] for layer_grads in per_layer]) for position in range(10))
    )
    summed = (
        lax.psum_scatter(
            stacked[0].astype(jnp.bfloat16), "dp", scatter_dimension=0, tiled=True
        ).astype(jnp.float32),
        lax.psum_scatter(
            stacked[1].astype(jnp.bfloat16), "dp", scatter_dimension=0, tiled=True
        ).astype(jnp.float32),
        lax.psum_scatter(
            stacked[2].astype(jnp.bfloat16), "dp", scatter_dimension=0, tiled=True
        ).astype(jnp.float32),
        lax.psum_scatter(
            stacked[3].astype(jnp.bfloat16), "dp", scatter_dimension=0, tiled=True
        ).astype(jnp.float32),
        lax.psum_scatter(
            stacked[4].astype(jnp.bfloat16), "dp", scatter_dimension=0, tiled=True
        ).astype(jnp.float32),
        lax.psum_scatter(
            stacked[5].astype(jnp.bfloat16), "dp", scatter_dimension=0, tiled=True
        ).astype(jnp.float32),
        lax.psum_scatter(
            stacked[6].astype(jnp.bfloat16), "dp", scatter_dimension=0, tiled=True
        ).astype(jnp.float32),
        lax.psum_scatter(
            stacked[7].astype(jnp.bfloat16), "dp", scatter_dimension=0, tiled=True
        ).astype(jnp.float32),
    )
    norm_sums = lax.psum((stacked[8], stacked[9]), ("dp", "col"))
    result = stream.reshape(image_count, seq_len, width_row)
    tokens_grad = grad_stream.reshape(image_count, seq_len, width_row)
    return (
        result,
        tokens_grad,
        summed[0],
        summed[1],
        summed[2],
        summed[3],
        summed[4],
        summed[5],
        summed[6],
        summed[7],
        norm_sums[0],
        norm_sums[1],
    )


def solution(mesh):
    placed = (
        P(("dp", "col"), None, "row"),
        P(("dp", "col"), None, "row"),
        P(None, "row", None, "col"),
        P(None, None, "col"),
        P(None, "col", "row"),
        P(None, "row"),
        P(None, "row", "col"),
        P(None, "col"),
        P(None, "col", "row"),
        P(None, "row"),
        P(None, None, "row"),
        P(None, None, "row"),
    )
    return jax.shard_map(
        per_device,
        mesh=mesh,
        in_specs=placed,
        out_specs=(
            P(("dp", "col"), None, "row"),
            P(("dp", "col"), None, "row"),
            P("dp", "row", None, "col"),
            P("dp", None, "col"),
            P("dp", "col", "row"),
            P("dp", "row"),
            P("dp", "row", "col"),
            P("dp", "col"),
            P("dp", "col", "row"),
            P("dp", "row"),
            P(None, None, "row"),
            P(None, None, "row"),
        ),
        check_vma=False,
    )
```

profile of v0, /device:TPU:0, one launch (start us, length us, event | category | flops | bytes accessed | tf_op | source)
XLA Modules:
  0.0 1328.5 jit_solution(15089566230927576608)
XLA Ops:
  9.5 11.4 all-reduce.44
  23.4 19.1 %all-gather.1 = bf16[4,257,352]{2,1,0:T(8,128)(2,1)S(1)} all-gather(bf16[1,257,352]{2,1,0:T(8,128)(2,1)S(1)} %fusion.160), channel_id=1, replica_groups=mesh['dp'=2,'row'=4,'col'=4] {'col'}, dimensions={0}, use_global_device_ids=true | all-gather | bytes 904640 | tf_op jit(solution)/shard_map/all_gather | solution.py:21
  49.1 40.1 %fusion = bf16[288,1056]{1,0:T(8,128)(2,1)S(1)} fusion(bf16[1028,1056]{1,0:T(8,128)(2,1)} %convolution_convert_fusion.5), kind=kCustom, calls=%all-reduce-scatter | all-reduce-scatter fusion | flops 1216513 | bytes 2779904
  101.2 13.9 %all-gather.2 = bf16[4,257,352]{2,1,0:T(8,128)(2,1)S(1)} all-gather(bf16[1,257,352]{2,1,0:T(8,128)(2,1)S(1)} %copy.122), channel_id=1, replica_groups=mesh['dp'=2,'row'=4,'col'=4] {'row'}, dimensions={0}, use_global_device_ids=true | all-gather | bytes 904640 | tf_op jit(solution)/shard_map/all_gather | solution.py:25
  117.4 19.6 %fusion.1 = bf16[272,352]{1,0:T(8,128)(2,1)} fusion(bf16[1028,352]{1,0:T(8,128)(2,1)S(1)} %convolution_convert_fusion.15), kind=kCustom, calls=%all-reduce-scatter.1 | all-reduce-scatter fusion | flops 382977 | bytes 915712
  143.5 8.9 all-reduce.43
  152.6 15.8 %all-gather.3 = bf16[4,257,352]{2,1,0:T(8,128)(2,1)S(1)} all-gather(bf16[1,257,352]{2,1,0:T(8,128)(2,1)S(1)} %fusion.157), channel_id=1, replica_groups=mesh['dp'=2,'row'=4,'col'=4] {'col'}, dimensions={0}, use_global_device_ids=true | all-gather | bytes 904640 | tf_op jit(solution)/shard_map/all_gather | solution.py:21
  169.6 5.0 convolution_convert_fusion.4
  174.6 47.1 %fusion.2 = bf16[272,1536]{1,0:T(8,128)(2,1)S(1)} fusion(bf16[1028,1536]{1,0:T(8,128)(2,1)} %convolution_convert_fusion.4), kind=kCustom, calls=%all-reduce-scatter.2 | all-reduce-scatter fusion | flops 1671169 | bytes 3994112
  236.5 46.7 %all-gather.23.cloned.1.call-done = bf16[4,257,1536]{2,1,0:T(8,128)(2,1)} async-done(((bf16[1,257,1536]{2,1,0:T(8,128)(2,1)}), bf16[4,257,1536]{2,1,0:T(8,128)(2,1)}) %all-gather.23.cloned.1.call-update) | async-done | bytes 3158032 | tf_op jit(solution)/shard_map/all_gather | solution.py:25
  287.6 4.9 convolution_convert_fusion.14
  292.5 22.6 %fusion.3 = bf16[272,352]{1,0:T(8,128)(2,1)S(1)} fusion(bf16[1028,352]{1,0:T(8,128)(2,1)} %convolution_convert_fusion.14), kind=kCustom, calls=%all-reduce-scatter.3 | all-reduce-scatter fusion | flops 382977 | bytes 915712
  323.3 8.9 all-reduce.42
  332.5 17.7 %all-gather.5 = bf16[4,257,352]{2,1,0:T(8,128)(2,1)S(1)} all-gather(bf16[1,257,352]{2,1,0:T(8,128)(2,1)S(1)} %fusion.158), channel_id=1, replica_groups=mesh['dp'=2,'row'=4,'col'=4] {'col'}, dimensions={0}, use_global_device_ids=true | all-gather | bytes 904640 | tf_op jit(solution)/shard_map/all_gather | solution.py:21
  355.7 39.8 %fusion.4 = bf16[288,1056]{1,0:T(8,128)(2,1)S(1)} fusion(bf16[1028,1056]{1,0:T(8,128)(2,1)} %convolution_convert_fusion.3), kind=kCustom, calls=%all-reduce-scatter.4 | all-reduce-scatter fusion | flops 1216513 | bytes 2779904
  398.7 29.0 %all-gather = bf16[1,1028,352]{2,0,1:T(2,128)(2,1)} all-gather(bf16[1,257,352]{2,0,1:T(2,128)(2,1)S(1)} %copy.129), channel_id=2, replica_groups=mesh['dp'=2,'row'=4,'col'=4] {'col'}, dimensions={1}, use_global_device_ids=true | all-gather | bytes 904640 | tf_op jit(solution)/shard_map/all_gather | solution.py:21
  441.3 13.7 %all-gather.6 = bf16[4,257,352]{2,1,0:T(8,128)(2,1)} all-gather(bf16[1,257,352]{2,1,0:T(8,128)(2,1)} %copy.128), channel_id=1, replica_groups=mesh['dp'=2,'row'=4,'col'=4] {'row'}, dimensions={0}, use_global_device_ids=true | all-gather | bytes 904640 | tf_op jit(solution)/shard_map/all_gather | solution.py:25
  460.2 19.7 %fusion.5 = bf16[272,352]{1,0:T(8,128)(2,1)} fusion(bf16[1028,352]{1,0:T(8,128)(2,1)} %convolution_convert_fusion.13), kind=kCustom, calls=%all-reduce-scatter.5 | all-reduce-scatter fusion | flops 382977 | bytes 915712
  483.4 5.2 convolution_convert_fusion.1
  493.7 8.9 all-reduce.41
  503.8 16.5 %all-gather.7 = bf16[4,257,352]{2,1,0:T(8,128)(2,1)} all-gather(bf16[1,257,352]{2,1,0:T(8,128)(2,1)S(1)} %fusion.159), channel_id=1, replica_groups=mesh['dp'=2,'row'=4,'col'=4] {'col'}, dimensions={0}, use_global_device_ids=true | all-gather | bytes 904640 | tf_op jit(solution)/shard_map/all_gather | solution.py:21
  522.6 5.0 convolution_convert_fusion.2
  527.6 103.6 %fusion.165 = (bf16[272,1536]{1,0:T(8,128)(2,1)}, bf16[272,1536]{1,0:T(8,128)(2,1)}) fusion(bf16[1028,1536]{1,0:T(8,128)(2,1)} %convolution_convert_fusion.2, bf16[1028,1536]{1,0:T(8,128)(2,1)} %convolution_convert_fusion.1), kind=kCustom, calls=%all-reduce-scatter.17 | all-reduce-scatter fusion | flops 3342337 | bytes 7987712
  632.1 5.0 collective-permute-start.8
  643.1 6.9 concatenate.16
  650.0 7.0 concatenate.14
  657.0 6.4 fusion.91
  663.8 41.0 %all-gather.27.cloned.1.call-done = bf16[4,257,1536]{2,1,0:T(8,128)(2,1)} async-done(((bf16[1,257,1536]{2,1,0:T(8,128)(2,1)}), bf16[4,257,1536]{2,1,0:T(8,128)(2,1)}) %all-gather.27.cloned.1.call-update) | async-done | bytes 3158032 | tf_op jit(solution)/shard_map/all_gather | solution.py:29
  714.1 23.1 %fusion.9 = bf16[272,352]{1,0:T(8,128)(2,1)} fusion(bf16[1028,352]{1,0:T(8,128)(2,1)} %convolution_convert_fusion.11), kind=kCustom, calls=%all-reduce-scatter.9 | all-reduce-scatter fusion | flops 382977 | bytes 915712
  747.2 8.9 all-reduce.40
  758.3 18.1 %all-gather.10 = bf16[4,257,352]{2,1,0:T(8,128)(2,1)} all-gather(bf16[1,257,352]{2,1,0:T(8,128)(2,1)S(1)} %get-tuple-element.134), channel_id=1, replica_groups=mesh['dp'=2,'row'=4,'col'=4] {'col'}, dimensions={0}, use_global_device_ids=true | all-gather | bytes 904640 | tf_op jit(solution)/shard_map/all_gather | solution.py:21
  781.6 27.9 %fusion.10 = bf16[288,352]{1,0:T(8,128)(2,1)} fusion(bf16[1028,352]{1,0:T(8,128)(2,1)} %convolution_convert_fusion.10), kind=kCustom, calls=%all-reduce-scatter.10 | all-reduce-scatter fusion | flops 405505 | bytes 926976
  831.6 37.2 %all-gather.29.cloned.1.call-done = bf16[4,257,1056]{2,1,0:T(8,128)(2,1)} async-done(((bf16[1,257,1056]{2,1,0:T(8,128)(2,1)}), bf16[4,257,1056]{2,1,0:T(8,128)(2,1)}) %all-gather.29.cloned.1.call-update) | async-done | bytes 2171152 | tf_op jit(solution)/shard_map/all_gather | solution.py:29
  877.3 22.6 %fusion.11 = bf16[272,352]{1,0:T(8,128)(2,1)S(1)} fusion(bf16[1028,352]{1,0:T(8,128)(2,1)} %convolution_convert_fusion.7), kind=kCustom, calls=%all-reduce-scatter.11 | all-reduce-scatter fusion | flops 382977 | bytes 915712
  905.7 9.4 all-reduce.39
  916.1 17.6 %all-gather.12 = bf16[4,257,352]{2,1,0:T(8,128)(2,1)S(1)} all-gather(bf16[1,257,352]{2,1,0:T(8,128)(2,1)S(1)} %get-tuple-element.132), channel_id=1, replica_groups=mesh['dp'=2,'row'=4,'col'=4] {'col'}, dimensions={0}, use_global_device_ids=true | all-gather | bytes 904640 | tf_op jit(solution)/shard_map/all_gather | solution.py:21
  939.8 47.7 %fusion.12 = bf16[272,1536]{1,0:T(8,128)(2,1)S(1)} fusion(bf16[1028,1536]{1,0:T(8,128)(2,1)} %convolution_convert_fusion), kind=kCustom, calls=%all-reduce-scatter.12 | all-reduce-scatter fusion | flops 1671169 | bytes 3994112
  992.7 6.1 concatenate.20
  1014.5 35.0 %all-gather.31.cloned.1.call-done = bf16[4,257,1536]{2,1,0:T(8,128)(2,1)} async-done(((bf16[1,257,1536]{2,1,0:T(8,128)(2,1)}), bf16[4,257,1536]{2,1,0:T(8,128)(2,1)}) %all-gather.31.cloned.1.call-update) | async-done | bytes 3158032 | tf_op jit(solution)/shard_map/all_gather | solution.py:29
  1058.9 22.5 %fusion.13 = bf16[272,352]{1,0:T(8,128)(2,1)S(1)} fusion(bf16[1028,352]{1,0:T(8,128)(2,1)} %convolution_convert_fusion.9), kind=kCustom, calls=%all-reduce-scatter.13 | all-reduce-scatter fusion | flops 382977 | bytes 915712
  1091.2 9.6 all-reduce.38
  1103.9 17.9 %all-gather.14 = bf16[4,257,352]{2,1,0:T(8,128)(2,1)S(1)} all-gather(bf16[1,257,352]{2,1,0:T(8,128)(2,1)S(1)} %get-tuple-element.130), channel_id=1, replica_groups=mesh['dp'=2,'row'=4,'col'=4] {'col'}, dimensions={0}, use_global_device_ids=true | all-gather | bytes 904640 | tf_op jit(solution)/shard_map/all_gather | solution.py:21
  1125.8 26.2 %fusion.14 = bf16[288,352]{1,0:T(8,128)(2,1)} fusion(bf16[1028,352]{1,0:T(8,128)(2,1)} %convolution_convert_fusion.8), kind=kCustom, calls=%all-reduce-scatter.14 | all-reduce-scatter fusion | flops 405505 | bytes 926976
  1183.7 5.0 convolution_convert_fusion.12
  1203.6 5.8 all-gather.33.cloned.1.call-done
  1227.1 34.2 %fusion.164 = (bf16[272,352]{1,0:T(8,128)(2,1)S(1)}, bf16[272,352]{1,0:T(8,128)(2,1)S(1)}) fusion(bf16[1028,352]{1,0:T(8,128)(2,1)S(1)} %copy-done.41, bf16[1028,352]{1,0:T(8,128)(2,1)} %convolution_convert_fusion.6), kind=kCustom, calls=%all-reduce-scatter.16 | all-reduce-scatter fusion | flops 765953 | bytes 1830912
  1276.4 8.8 all-reduce.37
  1288.8 27.1 %all-reduce.36 = (f32[2,2,352]{2,1,0:T(2,128)}, f32[2,2,352]{2,1,0:T(2,128)}) all-reduce(f32[2,2,352]{2,1,0:T(2,128)S(1)} %pad_maximum_fusion.7, f32[2,2,352]{2,1,0:T(2,128)S(1)} %pad_maximum_fusion.8), channel_id=1, replica_groups=mesh['dp'=2,'row'=4,'col'=4] {'dp','col'}, use_global_device_ids=true, to_apply=%region_74.0 | all-reduce | flops 2816 | bytes 22528 | tf_op jit(solution)/shard_map/psum | solution.py:316
  (398 shorter events, 310.2 us)
Async XLA Ops:
  7.2 276.0 %all-gather.23.cloned.1.call-start = ((), (), s32[]{:S(2)}) async-start(), calls=%async_computation.8 | async-start | bytes 4055040 | tf_op jit(solution)/shard_map/all_gather | solution.py:25
  8.3 34.6 %copy-start.29 = (bf16[2,352,3,352]{3,1,2,0:T(8,128)(2,1)S(1)}, bf16[2,352,3,352]{3,1,2,0:T(8,128)(2,1)}, u32[]{:S(2)}) copy-start(bf16[2,352,3,352]{3,1,2,0:T(8,128)(2,1)} %param.14) | copy-start | bytes 4460548
  20.9 23.1 %copy-start.45 = (f32[257]{0:T(512)}, f32[257]{0:T(512)S(1)}, u32[]{:S(2)}) copy-start(f32[257]{0:T(512)S(1)} %get-tuple-element.161) | copy-start | bytes 3088
  49.1 42.6 %copy-start.67 = (u32[32]{0:T(128)S(1)}, u32[32]{0:T(128)}, u32[]{:S(2)}) copy-start(u32[32]{0:T(128)} %constant.102) | copy-start | bytes 388
  49.1 43.9 %copy-start.63 = (f32[2,2,352]{2,1,0:T(2,128)S(1)}, f32[2,2,352]{2,1,0:T(2,128)}, u32[]{:S(2)}) copy-start(f32[2,2,352]{2,1,0:T(2,128)} %param.15) | copy-start | bytes 16900
  89.3 5.9 collective-permute-start
  115.4 26.5 %copy-start.12 = (bf16[1028,352]{1,0:T(8,128)(2,1)}, bf16[1028,352]{1,0:T(8,128)(2,1)S(1)}, u32[]{:S(2)}) copy-start(bf16[1028,352]{1,0:T(8,128)(2,1)S(1)} %reshape.293) | copy-start | bytes 2171140
  115.4 24.7 %copy-start.64 = (f32[2,352]{1,0:T(2,128)S(1)}, f32[2,352]{1,0:T(2,128)}, u32[]{:S(2)}) copy-start(f32[2,352]{1,0:T(2,128)} %param.17) | copy-start | bytes 8452
  115.4 25.3 %copy-start.66 = (u32[32]{0:T(128)S(1)}, u32[32]{0:T(128)}, u32[]{:S(2)}) copy-start(u32[32]{0:T(128)} %constant.106) | copy-start | bytes 388
  115.4 27.8 %copy-start = (bf16[1,257,352]{2,1,0:T(8,128)(2,1)S(1)}, bf16[1,257,352]{2,1,0:T(8,128)(2,1)}, u32[]{:S(2)}) copy-start(bf16[1,257,352]{2,1,0:T(8,128)(2,1)} %param.12) | copy-start | bytes 542788
  137.8 4.1 collective-permute-start.1
  143.2 179.8 %copy-start.7 = (bf16[317,352]{1,0:T(8,128)(2,1)}, bf16[317,352]{1,0:T(8,128)(2,1)S(1)}, u32[]{:S(2)}) copy-start(bf16[317,352]{1,0:T(8,128)(2,1)S(1)} %concatenate.9) | copy-start | bytes 669508
  174.6 50.3 %copy-start.51 = (f32[2,1536]{1,0:T(2,128)S(1)}, f32[2,1536]{1,0:T(2,128)}, u32[]{:S(2)}) copy-start(f32[2,1536]{1,0:T(2,128)} %param.19) | copy-start | bytes 36868
  221.8 5.1 collective-permute-start.2
  236.4 468.4 %all-gather.27.cloned.1.call-start = ((), (), s32[]{:S(2)}) async-start(), calls=%async_computation.10 | async-start | bytes 4055040 | tf_op jit(solution)/shard_map/all_gather | solution.py:29
  287.6 30.1 %copy-start.65 = (f32[2,352]{1,0:T(2,128)S(1)}, f32[2,352]{1,0:T(2,128)}, u32[]{:S(2)}) copy-start(f32[2,352]{1,0:T(2,128)} %param.21) | copy-start | bytes 8452
  292.5 27.1 %copy-start.11 = (bf16[1,352,3,352]{3,1,2,0:T(8,128)(2,1)S(1)}, bf16[1,352,3,352]{3,1,2,0:T(8,128)(2,1)}, u32[]{:S(2)}) copy-start(bf16[1,352,3,352]{3,1,2,0:T(8,128)(2,1)} %get-tuple-element.142) | copy-start | bytes 2230276
  292.5 29.1 %copy-start.50 = (f32[352]{0:T(512)S(1)}, f32[352]{0:T(512)}, u32[]{:S(2)}) copy-start(f32[352]{0:T(512)} %copy-done.49) | copy-start | bytes 4228
  292.5 29.1 %copy-start.61 = (f32[352]{0:T(512)S(1)}, f32[352]{0:T(512)}, u32[]{:S(2)}) copy-start(f32[352]{0:T(512)} %get-tuple-element.92) | copy-start | bytes 4228
  292.5 29.1 %copy-start.62 = (f32[352]{0:T(512)S(1)}, f32[352]{0:T(512)}, u32[]{:S(2)}) copy-start(f32[352]{0:T(512)} %get-tuple-element.95) | copy-start | bytes 4228
  315.2 6.5 collective-permute-start.3
  323.3 28.1 %copy-start.2 = (f32[257,352]{1,0:T(8,128)}, f32[257,352]{1,0:T(8,128)S(1)}, u32[]{:S(2)}) copy-start(f32[257,352]{1,0:T(8,128)S(1)} %get-tuple-element.139) | copy-start | bytes 1085572
  395.6 32.1 %collective-permute-start.4 = (bf16[93,1056]{1,0:T(8,128)(2,1)S(1)}, bf16[93,1056]{1,0:T(8,128)(2,1)}, u32[]{:S(2)}, u32[]{:S(2)}) collective-permute-start(bf16[93,1056]{1,0:T(8,128)(2,1)S(1)} %slice.218), channel_id=1, source_target_pairs={{0,4},{4,8},{8,12},{1,5},{5,9},{9,13},{2,6},{6,10},{10,14},{3,7},{... | collective-permute-start | bytes 589256
  480.7 7.9 collective-permute-start.5
  632.1 10.9 collective-permute-start.8
  638.8 11.2 collective-permute-start.6
  663.4 205.5 %all-gather.29.cloned.1.call-start = ((), (), s32[]{:S(2)}) async-start(), calls=%async_computation.11 | async-start | bytes 3041280 | tf_op jit(solution)/shard_map/all_gather | solution.py:29
  738.0 4.2 collective-permute-start.9
  810.4 4.4 collective-permute-start.10
  828.8 173.9 %all-gather.25.cloned.1.call-start = ((), (), s32[]{:S(2)}) async-start(), calls=%async_computation.9 | async-start | bytes 4055040 | tf_op jit(solution)/shard_map/all_gather | solution.py:25
  831.6 41.6 %copy-start.37 = (bf16[1,352,3,352]{1,3,2,0:T(8,128)(2,1)S(1)}, bf16[1,352,3,352]{1,3,2,0:T(8,128)(2,1)}, u32[]{:S(2)}) copy-start(bf16[1,352,3,352]{1,3,2,0:T(8,128)(2,1)} %copy.172) | copy-start | bytes 2230276
  831.6 217.9 %all-gather.31.cloned.1.call-start = ((), (), s32[]{:S(2)}) async-start(), calls=%async_computation.12 | async-start | bytes 4055040 | tf_op jit(solution)/shard_map/all_gather | solution.py:29
  877.3 27.6 %copy-start.3 = (f32[257,352]{1,0:T(8,128)S(1)}, f32[257,352]{1,0:T(8,128)}, u32[]{:S(2)}) copy-start(f32[257,352]{1,0:T(8,128)} %copy-done.2) | copy-start | bytes 1085572
  877.3 37.9 %copy-start.31 = (f32[257,352]{1,0:T(8,128)S(1)}, f32[257,352]{1,0:T(8,128)}, u32[]{:S(2)}) copy-start(f32[257,352]{1,0:T(8,128)} %get-tuple-element.135) | copy-start | bytes 1085572
  899.9 4.1 collective-permute-start.11
  987.6 5.1 collective-permute-start.12
  1002.6 193.6 %reduce-scatter.43.cloned.1.call-start = ((), (), s32[]{:S(2)}) async-start(), calls=%async_computation.7 | async-start | bytes 3244032 | tf_op jit(solution)/shard_map/reduce_scatter | solution.py:309
  1014.4 187.4 %reduce-scatter.39.cloned.1.call-start = ((), (), s32[]{:S(2)}) async-start(), calls=%async_computation.5 | async-start | bytes 811008 | tf_op jit(solution)/shard_map/reduce_scatter | solution.py:297
  1081.4 6.0 collective-permute-start.13
  1153.6 5.5 collective-permute-start.14
  1159.1 50.3 %all-gather.33.cloned.1.call-start = ((), (), s32[]{:S(2)}) async-start(), calls=%async_computation.13 | async-start | bytes 3041280 | tf_op jit(solution)/shard_map/all_gather | solution.py:29
  1170.2 145.7 %reduce-scatter.41.cloned.1.call-start = ((), (), s32[]{:S(2)}) async-start(), calls=%async_computation.6 | async-start | bytes 3244032 | tf_op jit(solution)/shard_map/reduce_scatter | solution.py:303
  1177.4 141.4 %reduce-scatter.37.cloned.1.call-start = ((), (), s32[]{:S(2)}) async-start(), calls=%async_computation.4 | async-start | bytes 2433024 | tf_op jit(solution)/shard_map/reduce_scatter | solution.py:291
  1227.1 48.9 %copy-start.44 = (f32[257]{0:T(512)S(1)}, f32[257]{0:T(512)}, u32[]{:S(2)}) copy-start(f32[257]{0:T(512)} %copy-done.43) | copy-start | bytes 3088
  1227.1 48.9 %copy-start.46 = (f32[257]{0:T(512)S(1)}, f32[257]{0:T(512)}, u32[]{:S(2)}) copy-start(f32[257]{0:T(512)} %copy-done.45) | copy-start | bytes 3088
  1227.1 58.2 %copy-start.30 = (f32[257,352]{1,0:T(8,128)S(1)}, f32[257,352]{1,0:T(8,128)}, u32[]{:S(2)}) copy-start(f32[257,352]{1,0:T(8,128)} %get-tuple-element.131) | copy-start | bytes 1085572
  1261.3 13.9 %collective-permute-start.15 = (bf16[45,352]{1,0:T(8,128)(2,1)S(1)}, bf16[45,352]{1,0:T(8,128)(2,1)S(1)}, u32[]{:S(2)}, u32[]{:S(2)}) collective-permute-start(bf16[45,352]{1,0:T(8,128)(2,1)S(1)} %slice.229), channel_id=1, source_target_pairs={{0,1},{1,2},{2,3},{4,5},{5,6},{6,7},{8,9},{9,10},{10,11},{12,13},{... | collective-permute-start | bytes 95048
  1273.1 13.6 %collective-permute-start.7 = (bf16[45,352]{1,0:T(8,128)(2,1)S(1)}, bf16[45,352]{1,0:T(8,128)(2,1)S(1)}, u32[]{:S(2)}, u32[]{:S(2)}) collective-permute-start(bf16[45,352]{1,0:T(8,128)(2,1)S(1)} %slice.221), channel_id=1, source_target_pairs={{0,1},{1,2},{2,3},{4,5},{5,6},{6,7},{8,9},{9,10},{10,11},{12,13},{... | collective-permute-start | bytes 95048
  (47 other events, 256.5 us)
Sparse Core Ops, SparseCore 0:
  236.5 46.5 all-gather.22
  663.5 41.2 all-gather.26
  829.0 39.8 all-gather.28
  871.2 44.9 all-gather.24
  1002.7 46.7 all-gather.30
  1052.2 9.8 reduce-scatter.42
  1159.2 7.9 reduce-scatter.38
  1170.4 38.9 all-gather.32
  1212.2 9.7 reduce-scatter.40
  1226.1 9.3 reduce-scatter.36
where the time goes:
time: 1340 us; the launch traced here: 1330 us
  blocking collectives  781 us (58%)
  waiting for transfers between devices  175 us (13%)
  local copies, waits for them, and re-layouts  138 us (10%)
  matrix products  97 us (7%)
  other arithmetic  69.6 us (5%)
  starting transfers between devices  49.1 us (4%)
  between operations  18.1 us (1%)
    unnamed x15, blocking collectives  500 us
    all_gather x8, blocking collectives, gather_tokens(): return lax.all_gather(values, 'col', axis=0, tiled=True)  152 us
    unnamed x202, local copies, waits for them, and re-layouts  122 us
    all_gather x4, waiting for transfers between devices, gather_grad_blocks(): return lax.all_gather(values, 'row', axis=0, tiled=True)  119 us
    psum x8, blocking collectives, width_totals(): return lax.psum((first_sum, second_sum), 'row')  74.9 us
    unnamed x16, starting transfers between devices  48.1 us
    all_gather x2, waiting for transfers between devices, gather_blocks(): return lax.all_gather(values, 'row', axis=0, tiled=True)  46.7 us
    dot_general x8, matrix products, row_product(): lax.dot_general(gathered, matrix, contract, preferred_element_type=jnp.fl...  32.8 us
  transfers between devices with their start and end apart: 26, of which 11 were waited for; matrix products, arithmetic and copies ran while one was open for 23% of the time, Pallas kernels for 0%

commit v1 on v0

--- a/solution.py
+++ b/solution.py
@@ -3,15 +3,776 @@
 import jax
 import jax.numpy as jnp
 from jax import lax
+from jax.experimental import pallas as pl
+from jax.experimental.pallas import tpu as pltpu
 from jax.sharding import PartitionSpec as P
 
 D = 1408
 HEAD_DIM = 88
 SEQ = 257
 LAYERS = 2
-
-
 EPSILON = 1e-06
+MESH = pl.DeviceIdType.MESH
+BF = jnp.bfloat16
+F32 = jnp.float32
+
+ROWS = 272
+STEP = 64
+CHUNK = 80
+BLK = 352
+PAD = 384
+HALF = 768
+N = 4
+
+
+def dot(a, b):
+    return jnp.dot(a, b, preferred_element_type=F32)
+
+
+def dot_t(a, b):
+    return lax.dot_general(a, b, (((1,), (1,)), ((), ())), preferred_element_type=F32)
+
+
+def t_dot(a, b):
+    return lax.dot_general(a, b, (((0,), (0,)), ((), ())), preferred_element_type=F32)
+
+
+def span(index):
+    return pl.ds(STEP * index, STEP if index < N - 1 else CHUNK)
+
+
+def head_span(head):
+    low, high = HEAD_DIM * head, HEAD_DIM * (head + 1)
+    return low, high, low // 128 * 128, -(-high // 128) * 128
+
+
+def kernel(
+    tok_hbm, cot_hbm, w_hbm, vec_ref, qb_ref, ub_ref,
+    out_hbm, tg_hbm, g_hbm, vsum, csum,
+    w, x1, x2, triple, att, lse, hid, slope, std, inv,
+    gtop, gmid, lt, part, recv, st, gst, tmp, tin, cin, oblk, pin, pv,
+    gb, da, g3, acc, sbuf, prx, keep, ici, fin,
+    wloc, wsend, wrecv, psend, precv, vs, vr, toks, tokr, cots, cotr,
+    zs, zr, rss, rsr, outs, outr, tgs, tgr, cs_s, cs_r, credit, gis, gir, fins, finr,
+):
+    d, r, c = lax.axis_index("dp"), lax.axis_index("row"), lax.axis_index("col")
+    other = 1 - d
+    near = (r + 1 - 2 * lax.rem(r, 2), lax.rem(r + 2, N), N - 1 - r)
+    last = c == N - 1
+
+    def remote(src, dst, ssem, rsem, dev):
+        return pltpu.make_async_remote_copy(
+            src, dst, ssem, rsem, device_id=dev, device_id_type=MESH
+        )
+
+    def rblk(index):
+        return pl.ds(pl.multiple_of(index * BLK, 16), BLK)
+
+    recv[...] = jnp.zeros_like(recv)
+    tin[...] = jnp.zeros_like(tin)
+    cin[...] = jnp.zeros_like(cin)
+    vsum[...] = jnp.zeros_like(vsum)
+    barrier = pltpu.get_barrier_semaphore()
+    for k in range(N * N):
+        pl.semaphore_signal(
+            barrier, inc=1,
+            device_id=(d, lax.rem(r + k // N, N), lax.rem(c + k % N, N)), device_id_type=MESH,
+        )
+    pl.semaphore_signal(barrier, inc=1, device_id=(other, r, c), device_id_type=MESH)
+    pl.semaphore_wait(barrier, N * N + 1)
+
+    for k in range(3):
+        remote(vec_ref, pin.at[r], vs.at[k], vr.at[k], (d, near[k], c)).start()
+    own_vec = pltpu.make_async_copy(vec_ref, pin.at[r], vr.at[3])
+    own_vec.start()
+
+    def spread(src, dst, ssem, rsem, start):
+        for ct in range(N):
+            mine = jnp.logical_and(r == c, c == ct)
+            size = STEP if ct < N - 1 else CHUNK
+            source, target = src.at[span(ct)], dst.at[r, pl.ds(0, size)]
+
+            @pl.when(mine)
+            def _():
+                if start:
+                    pltpu.make_async_copy(source, target, rsem.at[r]).start()
+
+            @pl.when(jnp.logical_not(mine))
+            def _():
+                copy = remote(source, target, ssem.at[ct], rsem.at[r], (d, c, ct))
+                if start:
+                    copy.start()
+                else:
+                    copy.wait_send()
+
+    def spread_wait(src, dst, rsem):
+        def at_size(ct):
+            size = STEP if ct < N - 1 else CHUNK
+            for rs in range(N):
+                pltpu.make_async_copy(
+                    src.at[span(ct)], dst.at[rs, pl.ds(0, size)], rsem.at[rs]
+                ).wait()
+
+        @pl.when(last)
+        def _():
+            at_size(N - 1)
+
+        @pl.when(jnp.logical_not(last))
+        def _():
+            at_size(0)
+
+    spread(tok_hbm, tin, toks, tokr, True)
+
+    def local_w(l, b):
+        return pltpu.make_async_copy(w_hbm.at[l, b], w.at[l, b, rblk(r)], wloc.at[l, b])
+
+    def send_w(l, i, k):
+        b = 2 * i + d
+        return remote(
+            w_hbm.at[l, b], w.at[l, b, rblk(r)], wsend.at[l, i, k], wrecv.at[l, i, k],
+            (d, near[k], c),
+        )
+
+    def share_w(l, i, k):
+        b = 2 * i + d
+        rows = w.at[l, b, rblk(near[k])]
+        return remote(rows, rows, psend.at[l, i, k], precv.at[l, i, k], (other, r, c))
+
+    for b in range(6):
+        local_w(0, b).start()
+    for l in range(LAYERS):
+        for i in range(3):
+            for k in range(3):
+                send_w(l, i, k).start()
+            if l == 0 and i == 0:
+                spread(cot_hbm, cin, cots, cotr, True)
+    for b in range(6):
+        local_w(1, b).start()
+
+    def forward_w(l, i):
+        for k in range(3):
+            send_w(l, i, k).wait_recv()
+            share_w(l, i, k).start()
+
+    def need_w(l, i):
+        local_w(l, 2 * i).wait()
+        local_w(l, 2 * i + 1).wait()
+        for k in range(3):
+            b = 2 * i + other
+            rows = w.at[l, b, rblk(near[k])]
+            pltpu.make_async_copy(rows, rows, precv.at[l, i, k]).wait()
+
+    def gather_start(x):
+        for cs in range(N):
+
+            @pl.when(c == cs)
+            def _():
+                for ct in range(N):
+                    if ct != cs:
+                        rows = x.at[span(cs)]
+                        remote(rows, rows, zs.at[ct], zr.at[cs], (d, r, ct)).start()
+
+    def gather_wait(x):
+        for cs in range(N):
+            rows = x.at[span(cs)]
+
+            @pl.when(c != cs)
+            def _():
+                pltpu.make_async_copy(rows, rows, zr.at[cs]).wait()
+
+            @pl.when(c == cs)
+            def _():
+                for ct in range(N):
+                    if ct != cs:
+                        remote(rows, rows, zs.at[ct], zr.at[cs], (d, r, ct)).wait_send()
+
+    def scatter_copy(ct):
+        size = STEP if ct < N - 1 else CHUNK
+        return remote(
+            part.at[span(ct)], recv.at[c, pl.ds(0, size)], rss.at[ct], rsr.at[c], (d, r, ct)
+        )
+
+    def scatter_start():
+        for ct in range(N):
+
+            @pl.when(c != ct)
+            def _():
+                scatter_copy(ct).start()
+
+            @pl.when(c == ct)
+            def _():
+                size = STEP if ct < N - 1 else CHUNK
+                recv[ct, 0:size, :] = part[span(ct), :]
+
+    def scatter_wait():
+        for cs in range(N):
+            for big in (False, True):
+                size = CHUNK if big else STEP
+                rows = recv.at[cs, pl.ds(0, size)]
+
+                @pl.when(jnp.logical_and(c != cs, last if big else jnp.logical_not(last)))
+                def _():
+                    pltpu.make_async_copy(rows, rows, rsr.at[cs]).wait()
+
+            @pl.when(c != cs)
+            def _():
+                scatter_copy(cs).wait_send()
+
+    def received(rows):
+        total = recv[0, rows, :].astype(F32)
+        for cs in range(1, N):
+            total = total + recv[cs, rows, :].astype(F32)
+        return total
+
+    def vector(row):
+        return pv[pl.ds(row, 1), :]
+
+    def own_rows(x, t, value):
+        @pl.when(jnp.logical_or(t < 4, last))
+        def _():
+            x[pl.ds(pl.multiple_of(STEP * c + 16 * t, 16), 16), :] = value
+
+    valid = jnp.where(last, SEQ - STEP * (N - 1), STEP)
+
+    def masked(t, value):
+        index = lax.broadcasted_iota(jnp.int32, (16, 1), 0) + 16 * t
+        return jnp.where(index < valid, value, 0.0)
+
+    def norm_forward(l, j, x, extra):
+        def body(t, _):
+            rows = pl.ds(pl.multiple_of(16 * t, 16), 16)
+            v = extra(rows)
+            st[rows, :] = v
+            centre = jnp.sum(v, axis=1, keepdims=True) / D
+            spread_ = jnp.sum(v * v, axis=1, keepdims=True) / D - centre * centre
+            scale = lax.rsqrt(spread_ + EPSILON)
+            standard = (v - centre) * scale
+            std[l, j, rows, :] = standard
+            inv[l, j, rows, :] = jnp.broadcast_to(scale, (16, 128))
+            value = standard * vector(6 * l + j) + vector(6 * l + 2 + j)
+            own_rows(x, t, value.astype(BF))
+            return 0
+
+        lax.fori_loop(0, CHUNK // 16, body, 0)
+
+    def norm_backward(l, j, x, bias_row):
+        def body(t, _):
+            rows = pl.ds(pl.multiple_of(16 * t, 16), 16)
+            e = received(rows)
+            standard = std[l, j, rows, :]
+            gain_term = masked(t, e * standard)
+            vsum[pl.ds(6 * l + j, 1), :] += jnp.sum(gain_term, axis=0, keepdims=True)
+            vsum[pl.ds(6 * l + 2 + j, 1), :] += jnp.sum(masked(t, e), axis=0, keepdims=True)
+            f = e * vector(6 * l + j)
+            first = jnp.sum(f, axis=1, keepdims=True) / D
+            second = jnp.sum(f * standard, axis=1, keepdims=True) / D
+            scale = inv[l, j, rows, 0:1]
+            grad = gst[rows, :] + scale * (f - first - standard * second)
+            gst[rows, :] = grad
+            if x is not None:
+                low = grad.astype(BF)
+                own_rows(x, t, low)
+                vsum[pl.ds(bias_row, 1), :] += jnp.sum(
+                    masked(t, low.astype(F32)), axis=0, keepdims=True
+                )
+            return 0
+
+        lax.fori_loop(0, CHUNK // 16, body, 0)
+
+    def tiles(count, body):
+        lax.fori_loop(0, count, lambda n, _: (body(n), 0)[1], 0)
+
+    def features(body):
+        tiles(5, lambda n: body(pl.multiple_of(n * 256, 256), 256))
+        body(1280, 128)
+
+    def assemble(src, dst):
+        for k in range(N):
+            dst[:, BLK * k : BLK * (k + 1)] = src[k, :, 0:BLK].astype(F32)
+
+    for k in range(3):
+        remote(vec_ref, pin.at[r], vs.at[k], vr.at[k], (d, near[k], c)).wait_recv()
+    own_vec.wait()
+    assemble(pin, pv)
+    spread_wait(tok_hbm, tin, tokr)
+    assemble(tin, st)
+
+    lane = lax.broadcasted_iota(jnp.int32, (1, PAD), 1)
+    key_ok = lax.broadcasted_iota(jnp.int32, (1, ROWS), 1) < SEQ
+    scaling = HEAD_DIM**-0.5
+
+    def head_mask(head):
+        low, high, s0, s1 = head_span(head)
+        lanes = lane[:, s0:s1]
+        return jnp.logical_and(lanes >= low, lanes < high).astype(BF), s0, s1
+
+    def attend(l):
+        acc[0] = jnp.zeros((ROWS, PAD), F32)
+        for head in range(4):
+            mask, s0, s1 = head_mask(head)
+            q = triple[l, 0, :, s0:s1] * mask
+            scores = dot_t(q, triple[l, 1, :, s0:s1]) * scaling
+            scores = jnp.where(key_ok, scores, -1e30)
+            peak = jnp.max(scores, axis=1, keepdims=True)
+            total = peak + jnp.log(jnp.sum(jnp.exp(scores - peak), axis=1, keepdims=True))
+            lse[l, :, head : head + 1] = total
+            probs = jnp.exp(scores - total).astype(BF)
+            acc[0, :, s0:s1] += dot(probs, triple[l, 2, :, s0:s1] * mask)
+        att[l] = acc[0].astype(BF)
+
+    def forward(l, _):
+        def take(rows):
+            return st[rows, :]
+
+        norm_forward(l, 0, x1.at[l], take)
+        gather_start(x1.at[l])
+
+        @pl.when(l == 0)
+        def _():
+            forward_w(0, 0)
+
+        gather_wait(x1.at[l])
+        need_w(l, 0)
+
+        def qkv(s):
+            lanes = pl.ds(pl.multiple_of(lax.rem(s, 2) * PAD, 128), PAD)
+            value = dot(x1[l], w[l, s // 2, :, lanes]) + qb_ref[l, pl.ds(s, 1), :]
+            triple[l, s] = value.astype(BF)
+
+        tiles(3, qkv)
+        attend(l)
+
+        def proj(start, size):
+            value = dot_t(att[l], w[l, 1, pl.ds(start, size), PAD : 2 * PAD])
+            part[:, pl.ds(start, size)] = value.astype(BF)
+
+        features(proj)
+        scatter_start()
+        forward_w(l, 1)
+        scatter_wait()
+        norm_forward(
+            l, 1, x2.at[l], lambda rows: st[rows, :] + received(rows) + vector(6 * l + 4)
+        )
+        gather_start(x2.at[l])
+        forward_w(l, 2)
+        need_w(l, 1)
+        gather_wait(x2.at[l])
+
+        for h in range(2):
+
+            def up(n):
+                lanes = pl.ds(pl.multiple_of(n * 256, 256), 256)
+                before = dot(x2[l], w[l, 2 + h, :, lanes]) + ub_ref[l, pl.ds(h, 1), lanes]
+                half = before * (0.5**0.5)
+                cdf = 0.5 + 0.5 * lax.erf(half)
+                hid[l, h, :, lanes] = (before * cdf).astype(BF)
+                density = jnp.exp(-half * half) * 0.3989422804014327
+                slope[l, h, :, lanes] = (cdf + before * density).astype(slope.dtype)
+
+            tiles(3, up)
+        need_w(l, 2)
+
+        def down(start, size):
+            rows = pl.ds(start, size)
+            value = dot_t(hid[l, 0], w[l, 4, rows, :]) + dot_t(hid[l, 1], w[l, 5, rows, :])
+            part[:, pl.ds(start, size)] = value.astype(BF)
+
+        features(down)
+        scatter_start()
+
+        @pl.when(l == 0)
+        def _():
+            forward_w(1, 0)
+
+        scatter_wait()
+        def settle(t, _):
+            rows = pl.ds(pl.multiple_of(16 * t, 16), 16)
+            st[rows, :] = st[rows, :] + received(rows) + vector(6 * l + 5)
+            return 0
+
+        lax.fori_loop(0, CHUNK // 16, settle, 0)
+        return 0
+
+    lax.fori_loop(0, LAYERS, forward, 0)
+
+    def give(src, dst, ssem, rsem, start):
+        for k in range(N):
+            for cs in range(N):
+                size = STEP if cs < N - 1 else CHUNK
+                source, target = src.at[k, pl.ds(0, size)], dst.at[span(cs)]
+                mine = jnp.logical_and(r == k, c == r)
+
+                @pl.when(jnp.logical_and(c == cs, mine))
+                def _():
+                    if start:
+                        pltpu.make_async_copy(source, target, rsem.at[cs]).start()
+
+                @pl.when(jnp.logical_and(c == cs, jnp.logical_not(mine)))
+                def _():
+                    copy = remote(source, target, ssem.at[k], rsem.at[cs], (d, k, r))
+                    if start:
+                        copy.start()
+                    else:
+                        copy.wait_send()
+
+    def give_wait(dst, rsem):
+        for cs in range(N):
+            rows = dst.at[span(cs)]
+            pltpu.make_async_copy(rows, rows, rsem.at[cs]).wait()
+
+    for k in range(N):
+        oblk[k] = st[:, BLK * k : BLK * (k + 1)]
+    give(oblk, out_hbm, outs, outr, True)
+
+    spread_wait(cot_hbm, cin, cotr)
+    assemble(cin, gst)
+
+    def top_rows(t, _):
+        rows = pl.ds(pl.multiple_of(16 * t, 16), 16)
+        low = gst[rows, :].astype(BF)
+        own_rows(gtop, t, low)
+        vsum[pl.ds(6 * (LAYERS - 1) + 5, 1), :] += jnp.sum(
+            masked(t, low.astype(F32)), axis=0, keepdims=True
+        )
+        return 0
+
+    lax.fori_loop(0, CHUNK // 16, top_rows, 0)
+
+    def transpose(src, index):
+        def body(n):
+            lanes = pl.ds(pl.multiple_of(n * 128, 128), 128)
+            lt[index, lanes, :] = src[:, lanes].T
+
+        tiles(D // 128, body)
+
+    def piece(k):
+        return remote(sbuf.at[k], prx.at[k], cs_s.at[k], cs_r.at[k], (other, r, c))
+
+    def block_tile(i, b, k, left, right):
+        rows = rblk(k)
+        if i == 0:
+            lanes = []
+            for j in range(2):
+                s = 2 * b + j
+                lanes.append(dot(lt[left(s), rows, :], right(s)))
+            return lanes
+        return [dot(lt[left(b), rows, :], right(b))]
+
+    def store_tile(ref, values):
+        start = 0
+        for value in values:
+            ref[:, start : start + value.shape[1]] = value.astype(BF)
+            start += value.shape[1]
+
+    def pair(i, slot, left, right, wait_credit):
+        if wait_credit is not None:
+
+            @pl.when(wait_credit)
+            def _():
+                pl.semaphore_wait(credit, 1)
+
+        def send_tile(k):
+            store_tile(sbuf.at[k], block_tile(i, other, k, left, right))
+            piece(k).start()
+
+        tiles(N, send_tile)
+
+        def keep_tile(k):
+            store_tile(keep.at[slot, k], block_tile(i, d, k, left, right))
+
+        tiles(N, keep_tile)
+
+        def out_copy(k):
+            return remote(
+                keep.at[slot, near[k]], ici.at[i, k], gis.at[i, k], gir.at[i, k], (d, near[k], c)
+            )
+
+        def add(k):
+            rows = prx.at[k]
+            pltpu.make_async_copy(rows, rows, cs_r.at[k]).wait()
+            keep[slot, k] = (keep[slot, k].astype(F32) + prx[k].astype(F32)).astype(BF)
+
+        for k in range(3):
+            add(near[k])
+            out_copy(k).start()
+        add(r)
+        for k in range(N):
+            piece(k).wait_send()
+        pl.semaphore_signal(credit, inc=1, device_id=(other, r, c), device_id_type=MESH)
+
+    def finish(l, i, slot):
+        for k in range(3):
+            arrived = ici.at[i, k]
+            pltpu.make_async_copy(arrived, arrived, gir.at[i, k]).wait()
+
+        def body(t, _):
+            rows = pl.ds(pl.multiple_of(16 * t, 16), 16)
+            total = keep[slot, r, rows, :].astype(F32)
+            for k in range(3):
+                total = total + ici[i, k, rows, :].astype(F32)
+            fin[rows, :] = total
+            return 0
+
+        lax.fori_loop(0, BLK // 16, body, 0)
+        target = g_hbm.at[2 * i + d]
+
+        @pl.when(l == d)
+        def _():
+            copy = pltpu.make_async_copy(fin, target, fins.at[0])
+            copy.start()
+            copy.wait()
+
+        @pl.when(l != d)
+        def _():
+            copy = remote(fin, target, fins.at[0], finr.at[i], (other, r, c))
+            copy.start()
+            copy.wait_send()
+
+        for k in range(3):
+            remote(
+                keep.at[slot, near[k]], ici.at[i, k], gis.at[i, k], gir.at[i, k], (d, near[k], c)
+            ).wait_send()
+
+    def attend_back(l):
+        for s in range(3):
+            acc[s] = jnp.zeros((ROWS, PAD), F32)
+        for head in range(4):
+            mask, s0, s1 = head_mask(head)
+            q = triple[l, 0, :, s0:s1] * mask
+            keys = triple[l, 1, :, s0:s1]
+            scores = dot_t(q, keys) * scaling
+            scores = jnp.where(key_ok, scores, -1e30)
+            probs = jnp.exp(scores - lse[l, :, head : head + 1])
+            probs_low = probs.astype(BF)
+            grad_heads = da[:, s0:s1] * mask
+            acc[2, :, s0:s1] += t_dot(probs_low, grad_heads)
+            grad_probs = dot_t(grad_heads, triple[l, 2, :, s0:s1])
+            inner = jnp.sum(grad_probs * probs, axis=1, keepdims=True)
+            grad_scores = (probs * (grad_probs - inner)).astype(BF)
+            acc[0, :, s0:s1] += dot(grad_scores, keys * mask)
+            acc[1, :, s0:s1] += t_dot(grad_scores, q)
+        for s in range(3):
+            value = acc[s] * scaling if s < 2 else acc[s]
+            g3[s] = value.astype(BF)
+        g3[3] = att[l]
+
+    def backward(step, _):
+        l = LAYERS - 1 - step
+        gather_start(gtop)
+
+        @pl.when(step > 0)
+        def _():
+            finish(l + 1, 0, 0)
+
+        gather_wait(gtop)
+
+        for h in range(2):
+
+            def hidden(n):
+                lanes = pl.ds(pl.multiple_of(n * 256, 256), 256)
+                value = dot(gtop[...], w[l, 4 + h, :, lanes]) * slope[l, h, :, lanes].astype(F32)
+                low = value.astype(BF)
+                gb[h, :, lanes] = low
+                csum[l, pl.ds(2 + h, 1), lanes] = jnp.sum(
+                    low.astype(F32), axis=0, keepdims=True
+                )
+
+            tiles(3, hidden)
+
+        def back_up(start, size):
+            rows = pl.ds(start, size)
+            value = dot_t(gb[0], w[l, 2, rows, :]) + dot_t(gb[1], w[l, 3, rows, :])
+            part[:, pl.ds(start, size)] = value.astype(BF)
+
+        features(back_up)
+        scatter_start()
+        transpose(gtop, 0)
+        pair(2, 0, lambda b: 0, lambda b: hid[l, b], step > 0)
+        scatter_wait()
+        norm_backward(l, 1, gmid, 6 * l + 4)
+        gather_start(gmid)
+        transpose(x2.at[l], 1)
+        pair(1, 1, lambda b: 1, lambda b: gb[b], step >= 0)
+        gather_wait(gmid)
+        da[...] = dot(gmid[...], w[l, 1, :, PAD : 2 * PAD]).astype(BF)
+        attend_back(l)
+        for s in range(3):
+            row, start = (0, PAD * s) if s < 2 else (1, 0)
+            csum[l, row : row + 1, start : start + PAD] = jnp.sum(
+                g3[s].astype(F32), axis=0, keepdims=True
+            )
+
+        def back_qkv(start, size):
+            rows = pl.ds(start, size)
+            value = dot_t(g3[0], w[l, 0, rows, 0:PAD])
+            value = value + dot_t(g3[1], w[l, 0, rows, PAD : 2 * PAD])
+            value = value + dot_t(g3[2], w[l, 1, rows, 0:PAD])
+            part[:, pl.ds(start, size)] = value.astype(BF)
+
+        features(back_qkv)
+        scatter_start()
+        finish(l, 2, 0)
+        finish(l, 1, 1)
+        transpose(x1.at[l], 0)
+        transpose(gmid, 1)
+        pair(0, 0, lambda s: s // 3, lambda s: g3[s], step >= 0)
+        scatter_wait()
+        norm_backward(l, 0, gtop, jnp.where(l > 0, 6 * l - 1, 12))
+        return 0
+
+    lax.fori_loop(0, LAYERS, backward, 0)
+
+    for k in range(N):
+        tmp[k] = gst[:, BLK * k : BLK * (k + 1)]
+    give(tmp, tg_hbm, tgs, tgr, True)
+    finish(0, 0, 0)
+
+    pl.semaphore_wait(credit, 1)
+    give(oblk, out_hbm, outs, outr, False)
+    give_wait(out_hbm, outr)
+    give(tmp, tg_hbm, tgs, tgr, False)
+    give_wait(tg_hbm, tgr)
+    spread(tok_hbm, tin, toks, tokr, False)
+    spread(cot_hbm, cin, cots, cotr, False)
+    for i in range(3):
+        arrived = g_hbm.at[2 * i + other]
+        pltpu.make_async_copy(arrived, arrived, finr.at[i]).wait()
+    for k in range(3):
+        remote(vec_ref, pin.at[r], vs.at[k], vr.at[k], (d, near[k], c)).wait_send()
+    for l in range(LAYERS):
+        for i in range(3):
+            for k in range(3):
+                send_w(l, i, k).wait_send()
+                share_w(l, i, k).wait_send()
+
+
+def fused(tok, cot, wcat, vec, qb, ub):
+    dma = pltpu.SemaphoreType.DMA
+    vmem = pltpu.VMEM
+    whole = pl.BlockSpec(memory_space=pltpu.VMEM)
+    anywhere = pl.BlockSpec(memory_space=pl.ANY)
+    scratch = [
+        vmem((LAYERS, 6, D, HALF), BF),
+        vmem((LAYERS, ROWS, D), BF),
+        vmem((LAYERS, ROWS, D), BF),
+        vmem((LAYERS, 3, ROWS, PAD), BF),
+        vmem((LAYERS, ROWS, PAD), BF),
+        vmem((LAYERS, ROWS, 128), F32),
+        vmem((LAYERS, 2, ROWS, HALF), BF),
+        vmem((LAYERS, 2, ROWS, HALF), BF),
+        vmem((LAYERS, 2, CHUNK, D), F32),
+        vmem((LAYERS, 2, CHUNK, 128), F32),
+        vmem((ROWS, D), BF),
+        vmem((ROWS, D), BF),
+        vmem((2, D, ROWS), BF),
+        vmem((ROWS, D), BF),
+        vmem((N, CHUNK, D), BF),
+        vmem((CHUNK, D), F32),
+        vmem((CHUNK, D), F32),
+        vmem((N, CHUNK, BLK), F32),
+        vmem((N, CHUNK, BLK), BF),
+        vmem((N, CHUNK, BLK), BF),
+        vmem((N, CHUNK, BLK), F32),
+        vmem((N, 16, BLK), F32),
+        vmem((16, D), F32),
+        vmem((2, ROWS, HALF), BF),
+        vmem((ROWS, PAD), BF),
+        vmem((4, ROWS, PAD), BF),
+        vmem((3, ROWS, PAD), F32),
+        vmem((N, BLK, HALF), BF),
+        vmem((N, BLK, HALF), BF),
+        vmem((2, N, BLK, HALF), BF),
+        vmem((3, 3, BLK, HALF), BF),
+        vmem((BLK, HALF), F32),
+        dma((LAYERS, 6)),
+        dma((LAYERS, 3, 3)), dma((LAYERS, 3, 3)),
+        dma((LAYERS, 3, 3)), dma((LAYERS, 3, 3)),
+        dma((3,)), dma((4,)),
+        dma((N,)), dma((N,)), dma((N,)), dma((N,)),
+        dma((N,)), dma((N,)), dma((N,)), dma((N,)),
+        dma((N,)), dma((N,)), dma((N,)), dma((N,)),
+        dma((N,)), dma((N,)), pltpu.SemaphoreType.REGULAR,
+        dma((3, 3)), dma((3, 3)), dma((1,)), dma((3,)),
+    ]
+    shape = jax.ShapeDtypeStruct
+    return pl.pallas_call(
+        kernel,
+        out_shape=(
+            shape((ROWS, BLK), F32),
+            shape((ROWS, BLK), F32),
+            shape((6, BLK, HALF), F32),
+            shape((16, D), F32),
+            shape((LAYERS, 4, HALF), F32),
+        ),
+        in_specs=[anywhere, anywhere, anywhere, whole, whole, whole],
+        out_specs=(anywhere, anywhere, anywhere, whole, whole),
+        scratch_shapes=scratch,
+        compiler_params=pltpu.CompilerParams(
+            collective_id=0, has_side_effects=True, vmem_limit_bytes=67_043_328
+        ),
+    )(tok, cot, wcat, vec, qb, ub)
+
+
+def widen(values, axis=-1, to=PAD):
+    axis = axis % values.ndim
+    pads = [(0, 0)] * values.ndim
+    pads[axis] = (0, to - values.shape[axis])
+    return jnp.pad(values, pads)
+
+
+def per_device_fused(
+    tokens, cotangent, qkv_weight, qv_bias, proj_weight, proj_bias,
+    up_weight, up_bias, down_weight, down_bias, norm_gain, norm_shift,
+):
+    row, dp = lax.axis_index("row"), lax.axis_index("dp")
+    tok = widen(tokens[0], 0, ROWS)
+    cot = widen(cotangent[0], 0, ROWS)
+    q, k, v = (widen(qkv_weight[:, :, s]) for s in range(3))
+    proj = widen(proj_weight.transpose(0, 2, 1))
+    down = down_weight.transpose(0, 2, 1)
+    wcat = jnp.stack(
+        [
+            jnp.concatenate([q, k], 2),
+            jnp.concatenate([v, proj], 2),
+            up_weight[:, :, :HALF],
+            up_weight[:, :, HALF:],
+            down[:, :, :HALF],
+            down[:, :, HALF:],
+        ],
+        axis=1,
+    )
+    vec = jnp.concatenate(
+        [norm_gain, norm_shift, proj_bias[:, None], down_bias[:, None]], axis=1
+    ).reshape(12, BLK)
+    vec = widen(vec, 0, 16)
+    zero = jnp.zeros_like(qv_bias[:, 0])
+    qb = widen(jnp.stack([qv_bias[:, 0], zero, qv_bias[:, 1]], axis=1))
+    ub = up_bias.reshape(LAYERS, 2, HALF)
+    out, tg, grads, vsum, csum = fused(tok, cot, wcat, vec, qb, ub)
+    vsum = lax.psum(vsum, ("dp", "row", "col"))
+    csum = lax.psum(csum, ("dp", "row"))
+    mine = lax.dynamic_slice(vsum[:12], (0, row * BLK), (12, BLK)).reshape(LAYERS, 6, BLK)
+    layer = lax.dynamic_slice(mine, (dp, 0, 0), (1, 6, BLK))
+    cols = lax.dynamic_slice(csum, (dp, 0, 0), (1, 4, HALF))
+    qkv_grad = jnp.stack(
+        [grads[0, :, :BLK], grads[0, :, PAD : PAD + BLK], grads[1, :, :BLK]], axis=1
+    )
+    return (
+        out[None, :SEQ],
+        tg[None, :SEQ],
+        qkv_grad[None],
+        jnp.stack([cols[:, 0, :BLK], cols[:, 1, :BLK]], axis=1),
+        grads[1, :, PAD : PAD + BLK].T[None],
+        layer[:, 4],
+        jnp.concatenate([grads[2], grads[3]], axis=1)[None],
+        cols[:, 2:].reshape(1, 2 * HALF),
+        jnp.concatenate([grads[4].T, grads[5].T], axis=0)[None],
+        layer[:, 5],
+        mine[:, 0:2],
+        mine[:, 2:4],
+    )
+
+
 NORMAL = (((1,), (0,)), ((), ()))
 LAST_BOTH = (((1,), (1,)), ((), ()))
 FIRST_BOTH = (((0,), (0,)), ((), ()))
@@ -243,7 +1004,7 @@
     return (grad_in, layer_grads)
 
 
-def per_device(
+def per_device_plain(
     tokens,
     cotangent,
     qkv_weight,
@@ -347,8 +1108,9 @@
         P(None, None, "row"),
         P(None, None, "row"),
     )
+    sizes = (mesh.shape["dp"], mesh.shape["row"], mesh.shape["col"])
     return jax.shard_map(
-        per_device,
+        per_device_fused if sizes == (2, N, N) else per_device_plain,
         mesh=mesh,
         in_specs=placed,
         out_specs=(

time: 1340 us -> 589 us (0.44)
  blocking collectives: 781 us -> 27.6 us
  Pallas kernels: 0 us -> 431 us
  local copies, waits for them, and re-layouts: 138 us -> 23.9 us
  matrix products: 97 us -> 0 us
  waiting for transfers between devices: 175 us -> 82 us
  other arithmetic: 69.6 us -> 9.17 us
  starting transfers between devices: 49.1 us -> 0.04 us
    unnamed x15 -> x0, blocking collectives: 500 us -> none
    pallas_call x0 -> x1, Pallas kernels: none -> 431 us  [fused(): pl.pallas_call(kernel, out_shape=(shape((ROWS, BLK), F32), shape((ROWS, B...]
    all_gather x10 -> x0, blocking collectives: 179 us -> none  [the longest x8 152 us: gather_tokens(): return lax.all_gather(values, 'col', axis=0, tiled=True)]
    all_gather x6 -> x0, waiting for transfers between devices: 166 us -> none  [the longest x4 119 us: gather_grad_blocks(): return lax.all_gather(values, 'row', axis=0, tiled=True)]
    unnamed x202 -> x39, local copies, waits for them, and re-layouts: 122 us -> 7.51 us
    dot_general x36 -> x0, matrix products: 97 us -> none  [the longest x8 32.8 us: row_product(): lax.dot_general(gathered, matrix, contract, preferred_element_type=jnp.fl...]
    psum x0 -> x1, waiting for transfers between devices: none -> 82 us  [per_device_fused(): vsum = lax.psum(vsum, ('dp', 'row', 'col'))]
    psum x9 -> x1, blocking collectives: 102 us -> 27.6 us  [per_device_fused(): csum = lax.psum(csum, ('dp', 'row'))]
  transfers between devices with their start and end apart: 26 -> 1, of which waited for: 11 -> 1; matrix products, arithmetic and copies ran while one was open for 23% -> 3% of each run, Pallas kernels for 0% -> 0%
where the time goes in v1:
time: 589 us; the launch traced here: 588 us
  Pallas kernels  431 us (73%)
  waiting for transfers between devices  82 us (14%)
  blocking collectives  27.6 us (5%)
  local copies, waits for them, and re-layouts  23.9 us (4%)
  between operations  14.2 us (2%)
  other arithmetic  9.17 us (2%)
    pallas_call x1, Pallas kernels, fused(): pl.pallas_call(kernel, out_shape=(shape((ROWS, BLK), F32), shape((ROWS, B...  431 us
    psum x1, waiting for transfers between devices, per_device_fused(): vsum = lax.psum(vsum, ('dp', 'row', 'col'))  82 us
    psum x1, blocking collectives, per_device_fused(): csum = lax.psum(csum, ('dp', 'row'))  27.6 us
  transfers between devices with their start and end apart: 1, of which 1 were waited for; matrix products, arithmetic and copies ran while one was open for 3% of the time, Pallas kernels for 0%

profile of v1, /device:TPU:0, one launch (start us, length us, event | category | flops | bytes accessed | tf_op | source)
XLA Modules:
  0.0 587.5 jit_solution(16796527379174334237)
XLA Ops:
  7.2 0.0 all-reduce.10.cloned.1.call-start
  7.2 1.6 slice_bitcast_fusion.10
  8.8 0.3 copy.35
  9.1 0.0 copy-start.3
  9.2 1.1 fusion.6
  10.3 1.1 fusion.9
  11.4 1.1 bitcast_dynamic-update-slice_fusion.1
  12.5 1.0 bitcast_dynamic-update-slice_fusion
  13.5 0.0 copy-done.4
  13.5 0.0 copy-start.13
  13.6 0.0 copy-start.14
  13.6 0.0 copy-start.11
  13.6 0.0 copy-start.12
  13.6 0.0 copy-start.9
  13.6 1.1 fusion.11
  14.7 1.1 fusion.10.w_hbm
  15.8 0.1 pad.44.clone
  15.8 0.1 pad_maximum_fusion.1
  15.9 0.6 pad.35.qb_ref
  16.5 0.7 pad.28.tok_hbm
  17.2 0.7 pad.29.cot_hbm
  17.9 0.0 copy-done.13
  18.0 0.0 copy-done.11
  18.0 0.0 copy-done.12
  18.0 0.6 pad.34.vec_ref
  18.6 0.6 reshape.37.ub_ref
  19.3 430.7 %shard_map.211 = (f32[272,352]{1,0:T(8,128)}, f32[272,352]{1,0:T(8,128)}, f32[6,352,768]{2,1,0:T(8,128)}, f32[16,1408]{1,0:T(8,128)}, f32[2,4,768]{2,1,0:T(4,128)}) custom-call(bf16[272,352]{1,0:T(8,128)(2,1)} %pad.28.tok_hbm, bf16[272,352]{1,0:T(8,128)(2,1)} %pad.29.cot_hbm, bf16[2,6,352,768]{3,2,1,0:T(8,128)(2,1)} %fusion.10.w_hbm, ...), custom_call_target="tpu_custom_call" | custom-call | tf_op jit(solution)/shard_map/pallas_call | solution.py:698
  449.9 0.0 all-reduce.10.cloned.1.call-update
  450.0 3.0 slice_bitcast_fusion.6
  452.9 3.6 slice_bitcast_fusion.3
  456.5 0.0 copy-done.8
  456.5 27.6 %psum.14 = f32[2,4,768]{2,1,0:T(4,128)S(1)} all-reduce(f32[2,4,768]{2,1,0:T(4,128)S(1)} %copy-done.8), channel_id=1, replica_groups=mesh['dp'=2,'row'=4,'col'=4] {'dp','row'}, use_global_device_ids=true, to_apply=%region_0.1 | all-reduce | flops 6144 | bytes 49152 | tf_op jit(solution)/shard_map/psum | solution.py:753
  484.1 2.8 maximum_bitcast_fusion.1
  486.9 1.6 maximum_bitcast_fusion
  488.6 1.2 slice_bitcast_fusion.13
  489.8 0.0 copy-done
  489.8 0.0 copy-done.1
  489.8 0.0 copy-start.2
  489.8 2.4 maximum_bitcast_fusion.2
  492.2 0.6 constant_dynamic-slice_fusion
  492.7 1.2 copy.39
  493.9 1.2 copy.40
  495.0 0.6 copy.45
  495.7 1.0 copy.41
  496.7 82.0 %all-reduce.10.cloned.1.call-done = f32[16,1408]{1,0:T(8,128)} async-done(((f32[16,1408]{1,0:T(8,128)}), f32[16,1408]{1,0:T(8,128)}) %all-reduce.10.cloned.1.call-update) | async-done | bytes 90128 | tf_op jit(solution)/shard_map/psum | solution.py:752
  578.7 0.8 constant_dynamic-slice_fusion.1
  579.5 0.6 fusion.12
  580.1 0.6 dynamic-slice_bitcast_fusion.1
  (23 shorter events, 0.1 us)
Async XLA Ops:
  7.2 1.7 copy-start.5
  7.2 571.5 %all-reduce.10.cloned.1.call-start = ((), (), s32[]{:S(2)}) async-start(), calls=%async_computation | async-start | bytes 180224 | tf_op jit(solution)/shard_map/psum | solution.py:752
  9.1 2.3 copy-start.3
  11.4 2.1 copy-start.4
  13.5 2.2 copy-start.10
  13.5 3.0 copy-start.6
  13.5 3.7 copy-start.7
  13.5 4.4 copy-start.13
  13.6 4.4 copy-start.14
  13.6 4.4 copy-start.11
  13.6 4.4 copy-start.12
  13.6 5.0 copy-start.9
  452.9 3.6 copy-start.8
  486.9 2.8 copy-start
  486.9 2.8 copy-start.1
  489.8 5.9 %copy-start.2 = (f32[1,352,352]{1,2,0:T(8,128)S(1)}, f32[1,352,352]{1,2,0:T(8,128)}, u32[]{:S(2)}) copy-start(f32[1,352,352]{1,2,0:T(8,128)} %get-tuple-element.50) | copy-start | bytes 1486852
Sparse Core Ops, SparseCore 0:
  450.1 128.5 all-reduce.9

commit v2 on v1

--- a/solution.py
+++ b/solution.py
@@ -47,13 +47,15 @@
 
 
 def kernel(
-    tok_hbm, cot_hbm, w_hbm, vec_ref, qb_ref, ub_ref,
-    out_hbm, tg_hbm, g_hbm, vsum, csum,
-    w, x1, x2, triple, att, lse, hid, slope, std, inv,
-    gtop, gmid, lt, part, recv, st, gst, tmp, tin, cin, oblk, pin, pv,
-    gb, da, g3, acc, sbuf, prx, keep, ici, fin,
+    tok_hbm, cot_hbm, wa_hbm, up_hbm, down_hbm, vec_ref, qb_ref, ub_ref,
+    out_hbm, tg_hbm, ga_hbm, gu_hbm, gd_hbm, vout, cout,
+    wa, wm, x1, x2, triple, att, lse, hid, slope, std, inv,
+    gtop, gmid, lt, part, recv, st, gst, tin, cin, oblk, pin, pv,
+    gb, da, g3, acc, sbuf, prx, keep, ici, fin, part2, recv2,
+    vsum, csum, vb, vx, vz, vd, cx, cd,
     wloc, wsend, wrecv, psend, precv, vs, vr, toks, tokr, cots, cotr,
     zs, zr, rss, rsr, outs, outr, tgs, tgr, cs_s, cs_r, credit, gis, gir, fins, finr,
+    zs2, zr2, rss2, rsr2, vxs, vxr, vzs, vzr, vds, cxs, cxr, cds,
 ):
     d, r, c = lax.axis_index("dp"), lax.axis_index("row"), lax.axis_index("col")
     other = 1 - d
@@ -69,9 +71,11 @@
         return pl.ds(pl.multiple_of(index * BLK, 16), BLK)
 
     recv[...] = jnp.zeros_like(recv)
+    recv2[...] = jnp.zeros_like(recv2)
     tin[...] = jnp.zeros_like(tin)
     cin[...] = jnp.zeros_like(cin)
     vsum[...] = jnp.zeros_like(vsum)
+    csum[...] = jnp.zeros_like(csum)
     barrier = pltpu.get_barrier_semaphore()
     for k in range(N * N):
         pl.semaphore_signal(
@@ -123,31 +127,40 @@
 
     spread(tok_hbm, tin, toks, tokr, True)
 
-    def local_w(l, b):
-        return pltpu.make_async_copy(w_hbm.at[l, b], w.at[l, b, rblk(r)], wloc.at[l, b])
+    def source_w(l, i, which):
+        if i == 0:
+            return wa_hbm.at[l, pl.ds(2 * which, 2)]
+        lanes = pl.ds(pl.multiple_of(HALF * which, 128), HALF)
+        return (up_hbm if i == 1 else down_hbm).at[l, :, lanes]
+
+    def rows_w(l, i, which, block):
+        if i == 0:
+            return wa.at[l, pl.ds(2 * which, 2), rblk(block), :]
+        return wm.at[l, 2 * (i - 1) + which, rblk(block), :]
+
+    def local_w(l, i, which):
+        return pltpu.make_async_copy(
+            source_w(l, i, which), rows_w(l, i, which, r), wloc.at[l, i, which]
+        )
 
     def send_w(l, i, k):
-        b = 2 * i + d
         return remote(
-            w_hbm.at[l, b], w.at[l, b, rblk(r)], wsend.at[l, i, k], wrecv.at[l, i, k],
+            source_w(l, i, d), rows_w(l, i, d, r), wsend.at[l, i, k], wrecv.at[l, i, k],
             (d, near[k], c),
         )
 
     def share_w(l, i, k):
-        b = 2 * i + d
-        rows = w.at[l, b, rblk(near[k])]
+        rows = rows_w(l, i, d, near[k])
         return remote(rows, rows, psend.at[l, i, k], precv.at[l, i, k], (other, r, c))
 
-    for b in range(6):
-        local_w(0, b).start()
     for l in range(LAYERS):
         for i in range(3):
             for k in range(3):
                 send_w(l, i, k).start()
+            for which in range(2):
+                local_w(l, i, which).start()
             if l == 0 and i == 0:
                 spread(cot_hbm, cin, cots, cotr, True)
-    for b in range(6):
-        local_w(1, b).start()
 
     def forward_w(l, i):
         for k in range(3):
@@ -155,14 +168,13 @@
             share_w(l, i, k).start()
 
     def need_w(l, i):
-        local_w(l, 2 * i).wait()
-        local_w(l, 2 * i + 1).wait()
+        for which in range(2):
+            local_w(l, i, which).wait()
         for k in range(3):
-            b = 2 * i + other
-            rows = w.at[l, b, rblk(near[k])]
+            rows = rows_w(l, i, other, near[k])
             pltpu.make_async_copy(rows, rows, precv.at[l, i, k]).wait()
 
-    def gather_start(x):
+    def gather_start(x, zs=zs, zr=zr):
         for cs in range(N):
 
             @pl.when(c == cs)
@@ -172,7 +184,7 @@
                         rows = x.at[span(cs)]
                         remote(rows, rows, zs.at[ct], zr.at[cs], (d, r, ct)).start()
 
-    def gather_wait(x):
+    def gather_wait(x, zs=zs, zr=zr):
         for cs in range(N):
             rows = x.at[span(cs)]
 
@@ -186,39 +198,42 @@
                     if ct != cs:
                         remote(rows, rows, zs.at[ct], zr.at[cs], (d, r, ct)).wait_send()
 
-    def scatter_copy(ct):
+    def scatter_copy(ct, part, recv, rss, rsr):
         size = STEP if ct < N - 1 else CHUNK
         return remote(
             part.at[span(ct)], recv.at[c, pl.ds(0, size)], rss.at[ct], rsr.at[c], (d, r, ct)
         )
 
-    def scatter_start():
+    main = (part, recv, rss, rsr)
+    side = (part2, recv2, rss2, rsr2)
+
+    def scatter_start(path=main):
         for ct in range(N):
 
             @pl.when(c != ct)
             def _():
-                scatter_copy(ct).start()
+                scatter_copy(ct, *path).start()
 
             @pl.when(c == ct)
             def _():
                 size = STEP if ct < N - 1 else CHUNK
-                recv[ct, 0:size, :] = part[span(ct), :]
-
-    def scatter_wait():
+                path[1][ct, 0:size, :] = path[0][span(ct), :]
+
+    def scatter_wait(path=main):
         for cs in range(N):
             for big in (False, True):
                 size = CHUNK if big else STEP
-                rows = recv.at[cs, pl.ds(0, size)]
+                rows = path[1].at[cs, pl.ds(0, size)]
 
                 @pl.when(jnp.logical_and(c != cs, last if big else jnp.logical_not(last)))
                 def _():
-                    pltpu.make_async_copy(rows, rows, rsr.at[cs]).wait()
+                    pltpu.make_async_copy(rows, rows, path[3].at[cs]).wait()
 
             @pl.when(c != cs)
             def _():
-                scatter_copy(cs).wait_send()
-
-    def received(rows):
+                scatter_copy(cs, *path).wait_send()
+
+    def received(rows, recv=recv):
         total = recv[0, rows, :].astype(F32)
         for cs in range(1, N):
             total = total + recv[cs, rows, :].astype(F32)
@@ -320,6 +335,31 @@
             acc[0, :, s0:s1] += dot(probs, triple[l, 2, :, s0:s1] * mask)
         att[l] = acc[0].astype(BF)
 
+    def down(l, target):
+        def body(start, size):
+            rows = pl.ds(start, size)
+            value = dot_t(hid[l, 0], wm[l, 2, rows, :]) + dot_t(hid[l, 1], wm[l, 3, rows, :])
+            target[:, rows] = value.astype(BF)
+
+        return body
+
+    def settle(l, recv):
+        def body(t, _):
+            rows = pl.ds(pl.multiple_of(16 * t, 16), 16)
+            st[rows, :] = st[rows, :] + received(rows, recv) + vector(6 * l + 5)
+            return 0
+
+        return body
+
+    def top_rows(t, _):
+        rows = pl.ds(pl.multiple_of(16 * t, 16), 16)
+        low = gst[rows, :].astype(BF)
+        own_rows(gtop, t, low)
+        vsum[pl.ds(6 * (LAYERS - 1) + 5, 1), :] += jnp.sum(
+            masked(t, low.astype(F32)), axis=0, keepdims=True
+        )
+        return 0
+
     def forward(l, _):
         def take(rows):
             return st[rows, :]
@@ -332,18 +372,25 @@
             forward_w(0, 0)
 
         gather_wait(x1.at[l])
+
+        @pl.when(l == 0)
+        def _():
+            spread_wait(cot_hbm, cin, cotr)
+            assemble(cin, gst)
+            lax.fori_loop(0, CHUNK // 16, top_rows, 0)
+            gather_start(gtop, zs2, zr2)
+
         need_w(l, 0)
 
         def qkv(s):
-            lanes = pl.ds(pl.multiple_of(lax.rem(s, 2) * PAD, 128), PAD)
-            value = dot(x1[l], w[l, s // 2, :, lanes]) + qb_ref[l, pl.ds(s, 1), :]
+            value = dot(x1[l], wa[l, s]) + qb_ref[l, pl.ds(s, 1), :]
             triple[l, s] = value.astype(BF)
 
         tiles(3, qkv)
         attend(l)
 
         def proj(start, size):
-            value = dot_t(att[l], w[l, 1, pl.ds(start, size), PAD : 2 * PAD])
+            value = dot_t(att[l], wa[l, 3, pl.ds(start, size), :])
             part[:, pl.ds(start, size)] = value.astype(BF)
 
         features(proj)
@@ -362,7 +409,7 @@
 
             def up(n):
                 lanes = pl.ds(pl.multiple_of(n * 256, 256), 256)
-                before = dot(x2[l], w[l, 2 + h, :, lanes]) + ub_ref[l, pl.ds(h, 1), lanes]
+                before = dot(x2[l], wm[l, h, :, lanes]) + ub_ref[l, pl.ds(h, 1), lanes]
                 half = before * (0.5**0.5)
                 cdf = 0.5 + 0.5 * lax.erf(half)
                 hid[l, h, :, lanes] = (before * cdf).astype(BF)
@@ -372,25 +419,14 @@
             tiles(3, up)
         need_w(l, 2)
 
-        def down(start, size):
-            rows = pl.ds(start, size)
-            value = dot_t(hid[l, 0], w[l, 4, rows, :]) + dot_t(hid[l, 1], w[l, 5, rows, :])
-            part[:, pl.ds(start, size)] = value.astype(BF)
-
-        features(down)
-        scatter_start()
-
         @pl.when(l == 0)
         def _():
+            features(down(l, part))
+            scatter_start()
             forward_w(1, 0)
-
-        scatter_wait()
-        def settle(t, _):
-            rows = pl.ds(pl.multiple_of(16 * t, 16), 16)
-            st[rows, :] = st[rows, :] + received(rows) + vector(6 * l + 5)
-            return 0
-
-        lax.fori_loop(0, CHUNK // 16, settle, 0)
+            scatter_wait()
+            lax.fori_loop(0, CHUNK // 16, settle(l, recv), 0)
+
         return 0
 
     lax.fori_loop(0, LAYERS, forward, 0)
@@ -419,24 +455,6 @@
         for cs in range(N):
             rows = dst.at[span(cs)]
             pltpu.make_async_copy(rows, rows, rsem.at[cs]).wait()
-
-    for k in range(N):
-        oblk[k] = st[:, BLK * k : BLK * (k + 1)]
-    give(oblk, out_hbm, outs, outr, True)
-
-    spread_wait(cot_hbm, cin, cotr)
-    assemble(cin, gst)
-
-    def top_rows(t, _):
-        rows = pl.ds(pl.multiple_of(16 * t, 16), 16)
-        low = gst[rows, :].astype(BF)
-        own_rows(gtop, t, low)
-        vsum[pl.ds(6 * (LAYERS - 1) + 5, 1), :] += jnp.sum(
-            masked(t, low.astype(F32)), axis=0, keepdims=True
-        )
-        return 0
-
-    lax.fori_loop(0, CHUNK // 16, top_rows, 0)
 
     def transpose(src, index):
         def body(n):
@@ -500,6 +518,12 @@
             piece(k).wait_send()
         pl.semaphore_signal(credit, inc=1, device_id=(other, r, c), device_id_type=MESH)
 
+    def result(i, which, j):
+        if i == 0:
+            return ga_hbm.at[2 * which + j]
+        lanes = pl.ds(pl.multiple_of(HALF * which + PAD * j, 128), PAD)
+        return (gu_hbm if i == 1 else gd_hbm).at[:, lanes]
+
     def finish(l, i, slot):
         for k in range(3):
             arrived = ici.at[i, k]
@@ -510,23 +534,32 @@
             total = keep[slot, r, rows, :].astype(F32)
             for k in range(3):
                 total = total + ici[i, k, rows, :].astype(F32)
-            fin[rows, :] = total
+            fin[0, rows, :] = total[:, 0:PAD]
+            fin[1, rows, :] = total[:, PAD : 2 * PAD]
             return 0
 
         lax.fori_loop(0, BLK // 16, body, 0)
-        target = g_hbm.at[2 * i + d]
 
         @pl.when(l == d)
         def _():
-            copy = pltpu.make_async_copy(fin, target, fins.at[0])
-            copy.start()
-            copy.wait()
+            copies = [
+                pltpu.make_async_copy(fin.at[j], result(i, d, j), fins.at[j]) for j in range(2)
+            ]
+            for copy in copies:
+                copy.start()
+            for copy in copies:
+                copy.wait()
 
         @pl.when(l != d)
         def _():
-            copy = remote(fin, target, fins.at[0], finr.at[i], (other, r, c))
-            copy.start()
-            copy.wait_send()
+            copies = [
+                remote(fin.at[j], result(i, d, j), fins.at[j], finr.at[i, j], (other, r, c))
+                for j in range(2)
+            ]
+            for copy in copies:
+                copy.start()
+            for copy in copies:
+                copy.wait_send()
 
         for k in range(3):
             remote(
@@ -558,19 +591,22 @@
 
     def backward(step, _):
         l = LAYERS - 1 - step
-        gather_start(gtop)
+
+        @pl.when(step == 0)
+        def _():
+            gather_wait(gtop, zs2, zr2)
 
         @pl.when(step > 0)
         def _():
+            gather_start(gtop)
             finish(l + 1, 0, 0)
-
-        gather_wait(gtop)
+            gather_wait(gtop)
 
         for h in range(2):
 
             def hidden(n):
                 lanes = pl.ds(pl.multiple_of(n * 256, 256), 256)
-                value = dot(gtop[...], w[l, 4 + h, :, lanes]) * slope[l, h, :, lanes].astype(F32)
+                value = dot(gtop[...], wm[l, 2 + h, :, lanes]) * slope[l, h, :, lanes].astype(F32)
                 low = value.astype(BF)
                 gb[h, :, lanes] = low
                 csum[l, pl.ds(2 + h, 1), lanes] = jnp.sum(
@@ -581,7 +617,7 @@
 
         def back_up(start, size):
             rows = pl.ds(start, size)
-            value = dot_t(gb[0], w[l, 2, rows, :]) + dot_t(gb[1], w[l, 3, rows, :])
+            value = dot_t(gb[0], wm[l, 0, rows, :]) + dot_t(gb[1], wm[l, 1, rows, :])
             part[:, pl.ds(start, size)] = value.astype(BF)
 
         features(back_up)
@@ -593,20 +629,29 @@
         gather_start(gmid)
         transpose(x2.at[l], 1)
         pair(1, 1, lambda b: 1, lambda b: gb[b], step >= 0)
+        @pl.when(step == 0)
+        def _():
+            features(down(l, part2))
+
         gather_wait(gmid)
-        da[...] = dot(gmid[...], w[l, 1, :, PAD : 2 * PAD]).astype(BF)
+
+        @pl.when(step == 0)
+        def _():
+            scatter_start(side)
+
+        da[...] = dot(gmid[...], wa[l, 3]).astype(BF)
         attend_back(l)
         for s in range(3):
-            row, start = (0, PAD * s) if s < 2 else (1, 0)
-            csum[l, row : row + 1, start : start + PAD] = jnp.sum(
-                g3[s].astype(F32), axis=0, keepdims=True
-            )
+            if s != 1:
+                csum[l, s // 2 : s // 2 + 1, 0:PAD] = jnp.sum(
+                    g3[s].astype(F32), axis=0, keepdims=True
+                )
 
         def back_qkv(start, size):
             rows = pl.ds(start, size)
-            value = dot_t(g3[0], w[l, 0, rows, 0:PAD])
-            value = value + dot_t(g3[1], w[l, 0, rows, PAD : 2 * PAD])
-            value = value + dot_t(g3[2], w[l, 1, rows, 0:PAD])
+            value = dot_t(g3[0], wa[l, 0, rows, :])
+            value = value + dot_t(g3[1], wa[l, 1, rows, :])
+            value = value + dot_t(g3[2], wa[l, 2, rows, :])
             part[:, pl.ds(start, size)] = value.astype(BF)
 
         features(back_qkv)
@@ -618,25 +663,84 @@
         pair(0, 0, lambda s: s // 3, lambda s: g3[s], step >= 0)
         scatter_wait()
         norm_backward(l, 0, gtop, jnp.where(l > 0, 6 * l - 1, 12))
+
+        @pl.when(step == 0)
+        def _():
+            scatter_wait(side)
+            lax.fori_loop(0, CHUNK // 16, settle(l, recv2), 0)
+            for k in range(N):
+                oblk[k] = st[:, BLK * k : BLK * (k + 1)]
+            give(oblk, out_hbm, outs, outr, True)
+
         return 0
 
     lax.fori_loop(0, LAYERS, backward, 0)
 
-    for k in range(N):
-        tmp[k] = gst[:, BLK * k : BLK * (k + 1)]
-    give(tmp, tg_hbm, tgs, tgr, True)
-    finish(0, 0, 0)
-
-    pl.semaphore_wait(credit, 1)
     give(oblk, out_hbm, outs, outr, False)
     give_wait(out_hbm, outr)
-    give(tmp, tg_hbm, tgs, tgr, False)
+    for k in range(N):
+        oblk[k] = gst[:, BLK * k : BLK * (k + 1)]
+    give(oblk, tg_hbm, tgs, tgr, True)
+
+    def c_copy(k):
+        return remote(csum, cx.at[k], cxs.at[k], cxr.at[k], (d, near[k], c))
+
+    def v_copy(k):
+        return remote(vb.at[near[k]], vx.at[k], vxs.at[k], vxr.at[k], (d, near[k], c))
+
+    def z_copy(k):
+        return remote(
+            vz.at[c], vz.at[c], vzs.at[k], vzr.at[c], (d, r, lax.rem(c + k + 1, N))
+        )
+
+    for k in range(N):
+        vb[k] = vsum[:, BLK * k : BLK * (k + 1)]
+    for k in range(3):
+        v_copy(k).start()
+        c_copy(k).start()
+    total = vb[r]
+    for k in range(3):
+        v_copy(k).wait_recv()
+        total = total + vx[k]
+    vz[c] = total
+    for k in range(3):
+        z_copy(k).start()
+    for k in range(3):
+        c_copy(k).wait()
+    for l in range(LAYERS):
+        csum[l] = csum[l] + cx[0, l] + cx[1, l] + cx[2, l]
+    c_half = remote(csum.at[other], cd, cds.at[0], cds.at[1], (other, r, c))
+    c_half.start()
+    for cs in range(N):
+
+        @pl.when(c != cs)
+        def _():
+            pltpu.make_async_copy(vz.at[cs], vz.at[cs], vzr.at[cs]).wait()
+
+    total = vz[0]
+    for cs in range(1, N):
+        total = total + vz[cs]
+    vd[0] = total
+    v_half = remote(vd.at[0], vd.at[1], vds.at[0], vds.at[1], (other, r, c))
+    v_half.start()
+    finish(0, 0, 0)
+    c_half.wait()
+    cout[...] = csum[d] + cd[...]
+    v_half.wait()
+    vout[...] = vd[0] + vd[1]
+    for k in range(3):
+        v_copy(k).wait_send()
+        z_copy(k).wait_send()
+
+    pl.semaphore_wait(credit, 1)
+    give(oblk, tg_hbm, tgs, tgr, False)
     give_wait(tg_hbm, tgr)
     spread(tok_hbm, tin, toks, tokr, False)
     spread(cot_hbm, cin, cots, cotr, False)
     for i in range(3):
-        arrived = g_hbm.at[2 * i + other]
-        pltpu.make_async_copy(arrived, arrived, finr.at[i]).wait()
+        for j in range(2):
+            arrived = result(i, other, j)
+            pltpu.make_async_copy(arrived, arrived, finr.at[i, j]).wait()
     for k in range(3):
         remote(vec_ref, pin.at[r], vs.at[k], vr.at[k], (d, near[k], c)).wait_send()
     for l in range(LAYERS):
@@ -646,13 +750,14 @@
                 share_w(l, i, k).wait_send()
 
 
-def fused(tok, cot, wcat, vec, qb, ub):
+def fused(*operands):
     dma = pltpu.SemaphoreType.DMA
     vmem = pltpu.VMEM
     whole = pl.BlockSpec(memory_space=pltpu.VMEM)
     anywhere = pl.BlockSpec(memory_space=pl.ANY)
     scratch = [
-        vmem((LAYERS, 6, D, HALF), BF),
+        vmem((LAYERS, 4, D, PAD), BF),
+        vmem((LAYERS, 4, D, HALF), BF),
         vmem((LAYERS, ROWS, D), BF),
         vmem((LAYERS, ROWS, D), BF),
         vmem((LAYERS, 3, ROWS, PAD), BF),
@@ -669,7 +774,6 @@
         vmem((N, CHUNK, D), BF),
         vmem((CHUNK, D), F32),
         vmem((CHUNK, D), F32),
-        vmem((N, CHUNK, BLK), F32),
         vmem((N, CHUNK, BLK), BF),
         vmem((N, CHUNK, BLK), BF),
         vmem((N, CHUNK, BLK), F32),
@@ -683,8 +787,18 @@
         vmem((N, BLK, HALF), BF),
         vmem((2, N, BLK, HALF), BF),
         vmem((3, 3, BLK, HALF), BF),
-        vmem((BLK, HALF), F32),
-        dma((LAYERS, 6)),
+        vmem((2, BLK, PAD), F32),
+        vmem((ROWS, D), BF),
+        vmem((N, CHUNK, D), BF),
+        vmem((16, D), F32),
+        vmem((LAYERS, 4, HALF), F32),
+        vmem((N, 16, BLK), F32),
+        vmem((3, 16, BLK), F32),
+        vmem((N, 16, BLK), F32),
+        vmem((2, 16, BLK), F32),
+        vmem((3, LAYERS, 4, HALF), F32),
+        vmem((4, HALF), F32),
+        dma((LAYERS, 3, 2)),
         dma((LAYERS, 3, 3)), dma((LAYERS, 3, 3)),
         dma((LAYERS, 3, 3)), dma((LAYERS, 3, 3)),
         dma((3,)), dma((4,)),
@@ -692,7 +806,10 @@
         dma((N,)), dma((N,)), dma((N,)), dma((N,)),
         dma((N,)), dma((N,)), dma((N,)), dma((N,)),
         dma((N,)), dma((N,)), pltpu.SemaphoreType.REGULAR,
-        dma((3, 3)), dma((3, 3)), dma((1,)), dma((3,)),
+        dma((3, 3)), dma((3, 3)), dma((2,)), dma((3, 2)),
+        dma((N,)), dma((N,)), dma((N,)), dma((N,)),
+        dma((3,)), dma((3,)), dma((3,)), dma((N,)), dma((2,)),
+        dma((3,)), dma((3,)), dma((2,)),
     ]
     shape = jax.ShapeDtypeStruct
     return pl.pallas_call(
@@ -700,17 +817,19 @@
         out_shape=(
             shape((ROWS, BLK), F32),
             shape((ROWS, BLK), F32),
-            shape((6, BLK, HALF), F32),
-            shape((16, D), F32),
-            shape((LAYERS, 4, HALF), F32),
+            shape((4, BLK, PAD), F32),
+            shape((BLK, 2 * HALF), F32),
+            shape((BLK, 2 * HALF), F32),
+            shape((16, BLK), F32),
+            shape((4, HALF), F32),
         ),
-        in_specs=[anywhere, anywhere, anywhere, whole, whole, whole],
-        out_specs=(anywhere, anywhere, anywhere, whole, whole),
+        in_specs=[anywhere] * 5 + [whole] * 3,
+        out_specs=(anywhere,) * 5 + (whole, whole),
         scratch_shapes=scratch,
         compiler_params=pltpu.CompilerParams(
             collective_id=0, has_side_effects=True, vmem_limit_bytes=67_043_328
         ),
-    )(tok, cot, wcat, vec, qb, ub)
+    )(*operands)
 
 
 def widen(values, axis=-1, to=PAD):
@@ -724,22 +843,11 @@
     tokens, cotangent, qkv_weight, qv_bias, proj_weight, proj_bias,
     up_weight, up_bias, down_weight, down_bias, norm_gain, norm_shift,
 ):
-    row, dp = lax.axis_index("row"), lax.axis_index("dp")
+    dp = lax.axis_index("dp")
     tok = widen(tokens[0], 0, ROWS)
     cot = widen(cotangent[0], 0, ROWS)
-    q, k, v = (widen(qkv_weight[:, :, s]) for s in range(3))
-    proj = widen(proj_weight.transpose(0, 2, 1))
-    down = down_weight.transpose(0, 2, 1)
-    wcat = jnp.stack(
-        [
-            jnp.concatenate([q, k], 2),
-            jnp.concatenate([v, proj], 2),
-            up_weight[:, :, :HALF],
-            up_weight[:, :, HALF:],
-            down[:, :, :HALF],
-            down[:, :, HALF:],
-        ],
-        axis=1,
+    heads = jnp.concatenate(
+        [qkv_weight.transpose(0, 2, 1, 3), proj_weight.transpose(0, 2, 1)[:, None]], axis=1
     )
     vec = jnp.concatenate(
         [norm_gain, norm_shift, proj_bias[:, None], down_bias[:, None]], axis=1
@@ -748,28 +856,23 @@
     zero = jnp.zeros_like(qv_bias[:, 0])
     qb = widen(jnp.stack([qv_bias[:, 0], zero, qv_bias[:, 1]], axis=1))
     ub = up_bias.reshape(LAYERS, 2, HALF)
-    out, tg, grads, vsum, csum = fused(tok, cot, wcat, vec, qb, ub)
-    vsum = lax.psum(vsum, ("dp", "row", "col"))
-    csum = lax.psum(csum, ("dp", "row"))
-    mine = lax.dynamic_slice(vsum[:12], (0, row * BLK), (12, BLK)).reshape(LAYERS, 6, BLK)
-    layer = lax.dynamic_slice(mine, (dp, 0, 0), (1, 6, BLK))
-    cols = lax.dynamic_slice(csum, (dp, 0, 0), (1, 4, HALF))
-    qkv_grad = jnp.stack(
-        [grads[0, :, :BLK], grads[0, :, PAD : PAD + BLK], grads[1, :, :BLK]], axis=1
-    )
+    down = down_weight.transpose(0, 2, 1)
+    out, tg, ga, gu, gd, vout, cout = fused(tok, cot, widen(heads), up_weight, down, vec, qb, ub)
+    both = vout[:12].reshape(LAYERS, 6, BLK)
+    layer = lax.dynamic_slice(both, (dp, 0, 0), (1, 6, BLK))
     return (
         out[None, :SEQ],
         tg[None, :SEQ],
-        qkv_grad[None],
-        jnp.stack([cols[:, 0, :BLK], cols[:, 1, :BLK]], axis=1),
-        grads[1, :, PAD : PAD + BLK].T[None],
+        ga[:3, :, :BLK].transpose(1, 0, 2)[None],
+        cout[None, 0:2, :BLK],
+        ga[3, :, :BLK].T[None],
         layer[:, 4],
-        jnp.concatenate([grads[2], grads[3]], axis=1)[None],
-        cols[:, 2:].reshape(1, 2 * HALF),
-        jnp.concatenate([grads[4].T, grads[5].T], axis=0)[None],
+        gu[None],
+        cout[2:].reshape(1, 2 * HALF),
+        gd.T[None],
         layer[:, 5],
-        mine[:, 0:2],
-        mine[:, 2:4],
+        both[:, 0:2],
+        both[:, 2:4],
     )
 
 

time: 589 us -> 426 us (0.72)
  waiting for transfers between devices: 82 us -> 0 us
  Pallas kernels: 431 us -> 401 us
  blocking collectives: 27.6 us -> 0 us
  between operations: 14.2 us -> 0.79 us
    psum x1 -> x0, waiting for transfers between devices: 82 us -> none  [per_device_fused(): vsum = lax.psum(vsum, ('dp', 'row', 'col'))]
    pallas_call x1, Pallas kernels: 431 us -> 401 us  [fused(): pl.pallas_call(kernel, out_shape=(shape((ROWS, BLK), F32), shape((ROWS, B...]
    psum x1 -> x0, blocking collectives: 27.6 us -> none  [per_device_fused(): csum = lax.psum(csum, ('dp', 'row'))]
    broadcast_in_dim x3 -> x0, other arithmetic: 6.82 us -> none  [the longest x1 2.8 us: per_device_fused(): jnp.concatenate([grads[4].T, grads[5].T], axis=0)[None]]
  transfers between devices with their start and end apart: 1 -> 0, of which waited for: 1 -> 0; matrix products, arithmetic and copies ran while one was open for 3% -> 0% of each run, Pallas kernels for 0% -> 0%
where the time goes in v2:
time: 426 us
  Pallas kernels  401 us (94%)
  local copies, waits for them, and re-layouts  20 us (5%)
    pallas_call x1, Pallas kernels, fused(): pl.pallas_call(kernel, out_shape=(shape((ROWS, BLK), F32), shape((ROWS, B...  401 us
    unnamed x30, local copies, waits for them, and re-layouts  9.06 us

profile of v2, /device:TPU:0, one launch (start us, length us, event | category | flops | bytes accessed | tf_op | source)
XLA Modules:
  0.0 425.7 jit_solution(13452590100189433123)
XLA Ops:
  0.6 0.8 fusion.4
  1.4 0.1 pad.25.clone
  1.5 0.1 pad_maximum_fusion.1
  1.6 0.6 pad.23.qb_ref
  2.2 1.3 copy.28
  3.5 0.0 copy-start.2
  3.5 0.0 copy-start.3
  3.5 0.0 copy-start.9
  3.6 0.0 copy-start.10
  3.6 0.0 copy-start.7
  3.6 0.0 copy-start.8
  3.6 0.0 copy-start.5
  3.6 3.3 fusion.2.wa_hbm
  6.9 0.0 copy-done.2
  6.9 0.7 pad.19.tok_hbm
  7.6 0.0 copy-done.3
  7.6 0.7 pad.20.cot_hbm
  8.3 0.0 copy-done.9
  8.3 0.0 copy-done.10
  8.3 0.0 copy-done.7
  8.3 0.0 copy-done.8
  8.4 0.6 pad.22.vec_ref
  9.0 0.0 copy-done.5
  9.0 0.6 reshape.37.ub_ref
  9.6 401.5 %shard_map.211 = (f32[272,352]{1,0:T(8,128)}, f32[272,352]{1,0:T(8,128)}, f32[4,352,384]{2,1,0:T(8,128)}, f32[352,1536]{1,0:T(8,128)}, f32[352,1536]{1,0:T(8,128)}, /*index=5*/f32[16,352]{1,0:T(8,128)}, f32[4,768]{1,0:T(4,128)}) custom-call(bf16[272,352]{1,0:T(8,128)(2,1)} %pad.19.tok_hbm, bf16[272,352]{1,0:T(8,128)(2,1)} %pad.20.cot_hbm, ...), custom_call_target="tpu_custom_call" | custom-call | tf_op jit(solution)/shard_map/pallas_call | solution.py:815
  411.1 0.0 copy-start.4
  411.1 1.2 slice_bitcast_fusion.2
  412.3 1.2 copy.31
  413.5 1.2 copy.32
  414.6 0.0 copy-done.4
  414.6 0.6 dynamic-slice_bitcast_fusion
  415.2 0.6 fusion.3
  415.8 0.0 copy-start.6
  415.8 0.0 copy-start.1
  415.8 2.8 slice_bitcast_fusion
  418.6 1.1 slice_bitcast_fusion.1
  419.7 1.0 copy.33
  420.7 0.0 copy-done.6
  420.8 0.6 copy.34
  421.4 0.6 slice_bitcast_fusion.5
  421.9 0.0 copy-done.1
  421.9 0.0 copy-start
  421.9 1.3 copy.37
  423.3 1.0 copy-done
  424.3 1.3 copy.38
  (6 shorter events, 0.0 us)
Async XLA Ops:
  3.5 3.4 copy-start.2
  3.5 4.1 copy-start.3
  3.5 4.8 %copy-start.9 = (f32[2,352]{1,0:T(2,128)S(1)}, f32[2,352]{1,0:T(2,128)}, u32[]{:S(2)}) copy-start(f32[2,352]{1,0:T(2,128)} %param.17) | copy-start | bytes 8452
  3.6 4.8 %copy-start.10 = (f32[2,352]{1,0:T(2,128)S(1)}, f32[2,352]{1,0:T(2,128)}, u32[]{:S(2)}) copy-start(f32[2,352]{1,0:T(2,128)} %param.21) | copy-start | bytes 8452
  3.6 4.8 %copy-start.7 = (f32[2,2,352]{2,1,0:T(2,128)S(1)}, f32[2,2,352]{2,1,0:T(2,128)}, u32[]{:S(2)}) copy-start(f32[2,2,352]{2,1,0:T(2,128)} %param.23) | copy-start | bytes 16900
  3.6 4.8 %copy-start.8 = (f32[2,2,352]{2,1,0:T(2,128)S(1)}, f32[2,2,352]{2,1,0:T(2,128)}, u32[]{:S(2)}) copy-start(f32[2,2,352]{2,1,0:T(2,128)} %param.22) | copy-start | bytes 16900
  3.6 5.4 %copy-start.5 = (f32[2,1536]{1,0:T(2,128)S(1)}, f32[2,1536]{1,0:T(2,128)}, u32[]{:S(2)}) copy-start(f32[2,1536]{1,0:T(2,128)} %param.19) | copy-start | bytes 36868
  411.1 3.5 copy-start.4
  415.8 5.0 %copy-start.6 = (f32[4,768]{1,0:T(4,128)S(1)}, f32[4,768]{1,0:T(4,128)}, u32[]{:S(2)}) copy-start(f32[4,768]{1,0:T(4,128)} %get-tuple-element.22) | copy-start | bytes 36868
  415.8 6.1 %copy-start.1 = (f32[352,1536]{1,0:T(8,128)S(1)}, f32[352,1536]{1,0:T(8,128)}, u32[]{:S(2)}) copy-start(f32[352,1536]{1,0:T(8,128)} %get-tuple-element.24) | copy-start | bytes 6488068
  421.9 2.4 copy-start

commit v3 on v2

--- a/solution.py
+++ b/solution.py
@@ -19,6 +19,7 @@
 ROWS = 272
 STEP = 64
 CHUNK = 80
+LAST = 72
 BLK = 352
 PAD = 384
 HALF = 768
@@ -38,7 +39,7 @@
 
 
 def span(index):
-    return pl.ds(STEP * index, STEP if index < N - 1 else CHUNK)
+    return pl.ds(STEP * index, STEP if index < N - 1 else LAST)
 
 
 def head_span(head):
@@ -50,11 +51,11 @@
     tok_hbm, cot_hbm, wa_hbm, up_hbm, down_hbm, vec_ref, qb_ref, ub_ref,
     out_hbm, tg_hbm, ga_hbm, gu_hbm, gd_hbm, vout, cout,
     wa, wm, x1, x2, triple, att, lse, hid, slope, std, inv,
-    gtop, gmid, lt, part, recv, st, gst, tin, cin, oblk, pin, pv,
-    gb, da, g3, acc, sbuf, prx, keep, ici, fin, part2, recv2,
+    gtop, gmid, lt, part, recv, st, gst, tin, cin, oblk, mid, pin, pv,
+    gb, da, g3, acc, sbuf, prx, keep, ici, fin, hop, recv2,
     vsum, csum, vb, vx, vz, vd, cx, cd,
-    wloc, wsend, wrecv, psend, precv, vs, vr, toks, tokr, cots, cotr,
-    zs, zr, rss, rsr, outs, outr, tgs, tgr, cs_s, cs_r, credit, gis, gir, fins, finr,
+    wloc, wsend, wrecv, fsend, frecv, psend, precv, vs, vr, m1s, m1r, m2s, m2r,
+    zs, zr, rss, rsr, cs_s, cs_r, credit, gis, gir, fins, finr, hs, hr,
     zs2, zr2, rss2, rsr2, vxs, vxr, vzs, vzr, vds, cxs, cxr, cds,
 ):
     d, r, c = lax.axis_index("dp"), lax.axis_index("row"), lax.axis_index("col")
@@ -70,8 +71,13 @@
     def rblk(index):
         return pl.ds(pl.multiple_of(index * BLK, 16), BLK)
 
+    def rhalf(index, part_):
+        return pl.ds(pl.multiple_of(index * BLK + part_ * (BLK // 2), 16), BLK // 2)
+
     recv[...] = jnp.zeros_like(recv)
     recv2[...] = jnp.zeros_like(recv2)
+    for array in (x1.at[0], x1.at[1], x2.at[0], x2.at[1], gtop, gmid):
+        array[ROWS - 16 :, :] = jnp.zeros((16, D), BF)
     tin[...] = jnp.zeros_like(tin)
     cin[...] = jnp.zeros_like(cin)
     vsum[...] = jnp.zeros_like(vsum)
@@ -90,42 +96,119 @@
     own_vec = pltpu.make_async_copy(vec_ref, pin.at[r], vr.at[3])
     own_vec.start()
 
-    def spread(src, dst, ssem, rsem, start):
+    def by_size(body):
+        @pl.when(last)
+        def _():
+            body(LAST)
+
+        @pl.when(jnp.logical_not(last))
+        def _():
+            body(STEP)
+
+    def come_start(u, src):
         for ct in range(N):
-            mine = jnp.logical_and(r == c, c == ct)
-            size = STEP if ct < N - 1 else CHUNK
-            source, target = src.at[span(ct)], dst.at[r, pl.ds(0, size)]
-
-            @pl.when(mine)
+            size = STEP if ct < N - 1 else LAST
+            source, target = src.at[span(ct)], mid.at[u, c, pl.ds(0, size)]
+
+            @pl.when(c == ct)
             def _():
-                if start:
-                    pltpu.make_async_copy(source, target, rsem.at[r]).start()
-
-            @pl.when(jnp.logical_not(mine))
+                pltpu.make_async_copy(source, target, m1r.at[u, c]).start()
+
+            @pl.when(c != ct)
             def _():
-                copy = remote(source, target, ssem.at[ct], rsem.at[r], (d, c, ct))
-                if start:
-                    copy.start()
-                else:
-                    copy.wait_send()
-
-    def spread_wait(src, dst, rsem):
-        def at_size(ct):
-            size = STEP if ct < N - 1 else CHUNK
+                remote(source, target, m1s.at[u, ct], m1r.at[u, c], (d, r, ct)).start()
+
+    def come_pass(u, dst):
+        def sized(size):
+            rows = pl.ds(0, size)
+            for p in range(N):
+                source, target = mid.at[u, p, rows], dst.at[r, rows]
+                pltpu.make_async_copy(source, source, m1r.at[u, p]).wait()
+
+                @pl.when(r == p)
+                def _():
+                    pltpu.make_async_copy(source, target, m2r.at[u, r]).start()
+
+                @pl.when(r != p)
+                def _():
+                    remote(source, target, m2s.at[u, p], m2r.at[u, r], (d, p, c)).start()
+
+        by_size(sized)
+
+    def come_wait(u, dst):
+        def sized(size):
             for rs in range(N):
-                pltpu.make_async_copy(
-                    src.at[span(ct)], dst.at[rs, pl.ds(0, size)], rsem.at[rs]
-                ).wait()
-
-        @pl.when(last)
-        def _():
-            at_size(N - 1)
-
-        @pl.when(jnp.logical_not(last))
-        def _():
-            at_size(0)
-
-    spread(tok_hbm, tin, toks, tokr, True)
+                rows = dst.at[rs, pl.ds(0, size)]
+                pltpu.make_async_copy(rows, rows, m2r.at[u, rs]).wait()
+
+        by_size(sized)
+
+    def go_start(u):
+        def sized(size):
+            rows = pl.ds(0, size)
+            for k in range(N):
+                source, target = oblk.at[k, rows], mid.at[u, r, rows]
+
+                @pl.when(r == k)
+                def _():
+                    pltpu.make_async_copy(source, target, m1r.at[u, r]).start()
+
+                @pl.when(r != k)
+                def _():
+                    remote(source, target, m1s.at[u, k], m1r.at[u, r], (d, k, c)).start()
+
+        by_size(sized)
+
+    def go_pass(u, dst):
+        def sized(size):
+            for p in range(N):
+                source = mid.at[u, p, pl.ds(0, size)]
+                target = dst.at[pl.ds(pl.multiple_of(STEP * c, 16), size)]
+                pltpu.make_async_copy(source, source, m1r.at[u, p]).wait()
+
+                @pl.when(c == p)
+                def _():
+                    pltpu.make_async_copy(source, target, m2r.at[u, c]).start()
+
+                @pl.when(c != p)
+                def _():
+                    remote(source, target, m2s.at[u, p], m2r.at[u, c], (d, r, p)).start()
+
+        by_size(sized)
+
+    def go_wait(u, dst):
+        for cs in range(N):
+            rows = dst.at[span(cs)]
+            pltpu.make_async_copy(rows, rows, m2r.at[u, cs]).wait()
+
+    def sent(u):
+        for ct in range(N):
+            size = STEP if ct < N - 1 else LAST
+            rows = mid.at[u, 0, pl.ds(0, size)]
+
+            if u < 2:
+
+                @pl.when(c != ct)
+                def _():
+                    remote(rows, rows, m1s.at[u, ct], m1r.at[u, 0], (d, r, ct)).wait_send()
+
+            def second(size):
+                rows = mid.at[u, 0, pl.ds(0, size)]
+                first_row = u < 2
+
+                @pl.when((r != ct) if first_row else (c != ct))
+                def _():
+                    remote(rows, rows, m2s.at[u, ct], m2r.at[u, 0], (d, r, c)).wait_send()
+
+                if not first_row:
+
+                    @pl.when(r != ct)
+                    def _():
+                        remote(rows, rows, m1s.at[u, ct], m1r.at[u, 0], (d, ct, c)).wait_send()
+
+            by_size(second)
+
+    come_start(0, tok_hbm)
 
     def source_w(l, i, which):
         if i == 0:
@@ -135,44 +218,59 @@
 
     def rows_w(l, i, which, block):
         if i == 0:
-            return wa.at[l, pl.ds(2 * which, 2), rblk(block), :]
-        return wm.at[l, 2 * (i - 1) + which, rblk(block), :]
+            return wa.at[l, pl.ds(2 * which, 2), block, :]
+        return wm.at[l, 2 * (i - 1) + which, block, :]
 
     def local_w(l, i, which):
         return pltpu.make_async_copy(
-            source_w(l, i, which), rows_w(l, i, which, r), wloc.at[l, i, which]
+            source_w(l, i, which), rows_w(l, i, which, rblk(r)), wloc.at[l, i, which]
         )
 
     def send_w(l, i, k):
         return remote(
-            source_w(l, i, d), rows_w(l, i, d, r), wsend.at[l, i, k], wrecv.at[l, i, k],
+            source_w(l, i, d), rows_w(l, i, d, rblk(r)), wsend.at[l, i, k], wrecv.at[l, i, k],
             (d, near[k], c),
         )
 
+    def pass_w(l, i, k):
+        rows = rows_w(l, i, d, rhalf(near[k], k))
+        return remote(rows, rows, fsend.at[l, i, k], frecv.at[l, i, k], (d, near[1 - k], c))
+
     def share_w(l, i, k):
-        rows = rows_w(l, i, d, near[k])
+        rows = rows_w(l, i, d, rblk(near[k]))
         return remote(rows, rows, psend.at[l, i, k], precv.at[l, i, k], (other, r, c))
 
-    for l in range(LAYERS):
-        for i in range(3):
-            for k in range(3):
-                send_w(l, i, k).start()
-            for which in range(2):
-                local_w(l, i, which).start()
-            if l == 0 and i == 0:
-                spread(cot_hbm, cin, cots, cotr, True)
-
-    def forward_w(l, i):
-        for k in range(3):
+    def direct_w(l, i):
+        for k in range(2):
+            send_w(l, i, k).start()
+
+    def stage_w(l, i):
+        for k in range(2):
             send_w(l, i, k).wait_recv()
+            pass_w(l, i, k).start()
+        for k in range(2):
             share_w(l, i, k).start()
+
+    def close_w(l, i):
+        for k in range(2):
+            rows = rows_w(l, i, d, rhalf(near[2], k))
+            pltpu.make_async_copy(rows, rows, frecv.at[l, i, k]).wait()
+        share_w(l, i, 2).start()
 
     def need_w(l, i):
         for which in range(2):
             local_w(l, i, which).wait()
         for k in range(3):
-            rows = rows_w(l, i, other, near[k])
+            rows = rows_w(l, i, other, rblk(near[k]))
             pltpu.make_async_copy(rows, rows, precv.at[l, i, k]).wait()
+
+    direct_w(0, 0)
+    come_start(1, cot_hbm)
+    come_pass(0, tin)
+    for l in range(LAYERS):
+        for i in range(3):
+            for which in range(2):
+                local_w(l, i, which).start()
 
     def gather_start(x, zs=zs, zr=zr):
         for cs in range(N):
@@ -199,13 +297,13 @@
                         remote(rows, rows, zs.at[ct], zr.at[cs], (d, r, ct)).wait_send()
 
     def scatter_copy(ct, part, recv, rss, rsr):
-        size = STEP if ct < N - 1 else CHUNK
+        size = STEP if ct < N - 1 else LAST
         return remote(
             part.at[span(ct)], recv.at[c, pl.ds(0, size)], rss.at[ct], rsr.at[c], (d, r, ct)
         )
 
     main = (part, recv, rss, rsr)
-    side = (part2, recv2, rss2, rsr2)
+    side = (x2.at[LAYERS - 1], recv2, rss2, rsr2)
 
     def scatter_start(path=main):
         for ct in range(N):
@@ -216,13 +314,13 @@
 
             @pl.when(c == ct)
             def _():
-                size = STEP if ct < N - 1 else CHUNK
+                size = STEP if ct < N - 1 else LAST
                 path[1][ct, 0:size, :] = path[0][span(ct), :]
 
     def scatter_wait(path=main):
         for cs in range(N):
             for big in (False, True):
-                size = CHUNK if big else STEP
+                size = LAST if big else STEP
                 rows = path[1].at[cs, pl.ds(0, size)]
 
                 @pl.when(jnp.logical_and(c != cs, last if big else jnp.logical_not(last)))
@@ -309,7 +407,8 @@
         remote(vec_ref, pin.at[r], vs.at[k], vr.at[k], (d, near[k], c)).wait_recv()
     own_vec.wait()
     assemble(pin, pv)
-    spread_wait(tok_hbm, tin, tokr)
+    come_wait(0, tin)
+    come_pass(1, cin)
     assemble(tin, st)
 
     lane = lax.broadcasted_iota(jnp.int32, (1, PAD), 1)
@@ -369,13 +468,16 @@
 
         @pl.when(l == 0)
         def _():
-            forward_w(0, 0)
-
+            stage_w(0, 0)
+            direct_w(0, 1)
+            direct_w(0, 2)
+
+        close_w(l, 0)
         gather_wait(x1.at[l])
 
         @pl.when(l == 0)
         def _():
-            spread_wait(cot_hbm, cin, cotr)
+            come_wait(1, cin)
             assemble(cin, gst)
             lax.fori_loop(0, CHUNK // 16, top_rows, 0)
             gather_start(gtop, zs2, zr2)
@@ -395,13 +497,24 @@
 
         features(proj)
         scatter_start()
-        forward_w(l, 1)
+        stage_w(l, 1)
+
+        @pl.when(l == 0)
+        def _():
+            direct_w(1, 0)
+
         scatter_wait()
         norm_forward(
             l, 1, x2.at[l], lambda rows: st[rows, :] + received(rows) + vector(6 * l + 4)
         )
         gather_start(x2.at[l])
-        forward_w(l, 2)
+        close_w(l, 1)
+        stage_w(l, 2)
+
+        @pl.when(l == 0)
+        def _():
+            direct_w(1, 1)
+
         need_w(l, 1)
         gather_wait(x2.at[l])
 
@@ -417,44 +530,21 @@
                 slope[l, h, :, lanes] = (cdf + before * density).astype(slope.dtype)
 
             tiles(3, up)
+        close_w(l, 2)
         need_w(l, 2)
 
         @pl.when(l == 0)
         def _():
             features(down(l, part))
             scatter_start()
-            forward_w(1, 0)
+            stage_w(1, 0)
+            direct_w(1, 2)
             scatter_wait()
             lax.fori_loop(0, CHUNK // 16, settle(l, recv), 0)
 
         return 0
 
     lax.fori_loop(0, LAYERS, forward, 0)
-
-    def give(src, dst, ssem, rsem, start):
-        for k in range(N):
-            for cs in range(N):
-                size = STEP if cs < N - 1 else CHUNK
-                source, target = src.at[k, pl.ds(0, size)], dst.at[span(cs)]
-                mine = jnp.logical_and(r == k, c == r)
-
-                @pl.when(jnp.logical_and(c == cs, mine))
-                def _():
-                    if start:
-                        pltpu.make_async_copy(source, target, rsem.at[cs]).start()
-
-                @pl.when(jnp.logical_and(c == cs, jnp.logical_not(mine)))
-                def _():
-                    copy = remote(source, target, ssem.at[k], rsem.at[cs], (d, k, r))
-                    if start:
-                        copy.start()
-                    else:
-                        copy.wait_send()
-
-    def give_wait(dst, rsem):
-        for cs in range(N):
-            rows = dst.at[span(cs)]
-            pltpu.make_async_copy(rows, rows, rsem.at[cs]).wait()
 
     def transpose(src, index):
         def body(n):
@@ -463,60 +553,94 @@
 
         tiles(D // 128, body)
 
-    def piece(k):
-        return remote(sbuf.at[k], prx.at[k], cs_s.at[k], cs_r.at[k], (other, r, c))
-
-    def block_tile(i, b, k, left, right):
+    def piece(turn, k):
+        return remote(
+            sbuf.at[lax.rem(k, 2)], prx.at[turn, k], cs_s.at[k], cs_r.at[turn, k], (other, r, c)
+        )
+
+    def block_tile(ref, i, b, k, left, right):
         rows = rblk(k)
-        if i == 0:
-            lanes = []
-            for j in range(2):
+        for j in range(2):
+            lanes = pl.ds(PAD * j, PAD)
+            if i == 0:
                 s = 2 * b + j
-                lanes.append(dot(lt[left(s), rows, :], right(s)))
-            return lanes
-        return [dot(lt[left(b), rows, :], right(b))]
-
-    def store_tile(ref, values):
-        start = 0
-        for value in values:
-            ref[:, start : start + value.shape[1]] = value.astype(BF)
-            start += value.shape[1]
-
-    def pair(i, slot, left, right, wait_credit):
-        if wait_credit is not None:
-
-            @pl.when(wait_credit)
+                value = dot(lt[left(s), rows, :], right(s))
+            else:
+                value = dot(lt[left(b), rows, :], right(b)[:, lanes])
+            ref[:, lanes] = value.astype(BF)
+
+    def strips(count, body):
+        def strip(t, _):
+            body(pl.ds(pl.multiple_of(16 * t, 16), 16))
+            return 0
+
+        lax.fori_loop(0, count // 16, strip, 0)
+
+    def make(i, slot, turn, left, right, wait_credit):
+        @pl.when(wait_credit)
+        def _():
+            pl.semaphore_wait(credit, 1)
+
+        def send_tile(k):
+            @pl.when(k >= 2)
             def _():
-                pl.semaphore_wait(credit, 1)
-
-        def send_tile(k):
-            store_tile(sbuf.at[k], block_tile(i, other, k, left, right))
-            piece(k).start()
+                piece(turn, k - 2).wait_send()
+
+            block_tile(sbuf.at[lax.rem(k, 2)], i, other, k, left, right)
+            piece(turn, k).start()
 
         tiles(N, send_tile)
 
         def keep_tile(k):
-            store_tile(keep.at[slot, k], block_tile(i, d, k, left, right))
+            block_tile(keep.at[slot, k], i, d, k, left, right)
 
         tiles(N, keep_tile)
-
-        def out_copy(k):
-            return remote(
-                keep.at[slot, near[k]], ici.at[i, k], gis.at[i, k], gir.at[i, k], (d, near[k], c)
-            )
-
+        for k in (2, 3):
+            piece(turn, k).wait_send()
+
+    def half_copy(i, slot, k):
+        half = pl.ds(k * (BLK // 2), BLK // 2)
+        return remote(
+            keep.at[slot, near[2], half], hop.at[i, k], hs.at[i, k], hr.at[i, k], (d, near[k], c)
+        )
+
+    def block_copy(i, slot, k):
+        return remote(
+            keep.at[slot, near[k]], ici.at[i, k], gis.at[i, k], gir.at[i, k], (d, near[k], c)
+        )
+
+    def merge(i, slot, turn):
         def add(k):
-            rows = prx.at[k]
-            pltpu.make_async_copy(rows, rows, cs_r.at[k]).wait()
-            keep[slot, k] = (keep[slot, k].astype(F32) + prx[k].astype(F32)).astype(BF)
-
-        for k in range(3):
-            add(near[k])
-            out_copy(k).start()
-        add(r)
-        for k in range(N):
-            piece(k).wait_send()
+            rows = prx.at[turn, k]
+            pltpu.make_async_copy(rows, rows, cs_r.at[turn, k]).wait()
+
+            def strip(rows):
+                value = keep[slot, k, rows, :].astype(F32) + prx[turn, k, rows, :].astype(F32)
+                keep[slot, k, rows, :] = value.astype(BF)
+
+            strips(BLK, strip)
+
+        add(near[2])
+        for k in range(2):
+            half_copy(i, slot, k).start()
+        for k in (near[0], near[1], r):
+            add(k)
         pl.semaphore_signal(credit, inc=1, device_id=(other, r, c), device_id_type=MESH)
+
+    def relay(i, slot):
+        for k in range(2):
+            pltpu.make_async_copy(hop.at[i, k], hop.at[i, k], hr.at[i, k]).wait()
+            block = near[1 - k]
+
+            def strip(t, _):
+                rows = pl.ds(pl.multiple_of(16 * t, 16), 16)
+                half = pl.ds(pl.multiple_of(k * (BLK // 2) + 16 * t, 16), 16)
+                value = keep[slot, block, half, :].astype(F32) + hop[i, k, rows, :].astype(F32)
+                keep[slot, block, half, :] = value.astype(BF)
+                return 0
+
+            lax.fori_loop(0, BLK // 32, strip, 0)
+            block_copy(i, slot, 1 - k).start()
 
     def result(i, which, j):
         if i == 0:
@@ -525,14 +649,14 @@
         return (gu_hbm if i == 1 else gd_hbm).at[:, lanes]
 
     def finish(l, i, slot):
-        for k in range(3):
+        for k in range(2):
             arrived = ici.at[i, k]
             pltpu.make_async_copy(arrived, arrived, gir.at[i, k]).wait()
 
         def body(t, _):
             rows = pl.ds(pl.multiple_of(16 * t, 16), 16)
             total = keep[slot, r, rows, :].astype(F32)
-            for k in range(3):
+            for k in range(2):
                 total = total + ici[i, k, rows, :].astype(F32)
             fin[0, rows, :] = total[:, 0:PAD]
             fin[1, rows, :] = total[:, PAD : 2 * PAD]
@@ -561,10 +685,9 @@
             for copy in copies:
                 copy.wait_send()
 
-        for k in range(3):
-            remote(
-                keep.at[slot, near[k]], ici.at[i, k], gis.at[i, k], gir.at[i, k], (d, near[k], c)
-            ).wait_send()
+        for k in range(2):
+            half_copy(i, slot, k).wait_send()
+            block_copy(i, slot, k).wait_send()
 
     def attend_back(l):
         for s in range(3):
@@ -599,7 +722,8 @@
         @pl.when(step > 0)
         def _():
             gather_start(gtop)
-            finish(l + 1, 0, 0)
+            merge(0, 0, lax.rem(step + 1, 2))
+            finish(l + 1, 1, 1)
             gather_wait(gtop)
 
         for h in range(2):
@@ -615,6 +739,11 @@
 
             tiles(3, hidden)
 
+        @pl.when(step > 0)
+        def _():
+            relay(0, 0)
+            go_pass(2, out_hbm)
+
         def back_up(start, size):
             rows = pl.ds(start, size)
             value = dot_t(gb[0], wm[l, 0, rows, :]) + dot_t(gb[1], wm[l, 1, rows, :])
@@ -623,24 +752,34 @@
         features(back_up)
         scatter_start()
         transpose(gtop, 0)
-        pair(2, 0, lambda b: 0, lambda b: hid[l, b], step > 0)
+
+        @pl.when(step > 0)
+        def _():
+            finish(l + 1, 0, 0)
+
+        make(2, 0, lax.rem(step, 2), lambda b: 0, lambda b: hid.at[l, b], step > 0)
         scatter_wait()
         norm_backward(l, 1, gmid, 6 * l + 4)
         gather_start(gmid)
+        merge(2, 0, lax.rem(step, 2))
         transpose(x2.at[l], 1)
-        pair(1, 1, lambda b: 1, lambda b: gb[b], step >= 0)
+        make(1, 1, lax.rem(step + 1, 2), lambda b: 1, lambda b: gb.at[b], step > 0)
+
         @pl.when(step == 0)
         def _():
-            features(down(l, part2))
-
+            features(down(l, x2.at[LAYERS - 1]))
+
+        relay(2, 0)
         gather_wait(gmid)
 
         @pl.when(step == 0)
         def _():
             scatter_start(side)
 
+        merge(1, 1, lax.rem(step + 1, 2))
         da[...] = dot(gmid[...], wa[l, 3]).astype(BF)
         attend_back(l)
+        relay(1, 1)
         for s in range(3):
             if s != 1:
                 csum[l, s // 2 : s // 2 + 1, 0:PAD] = jnp.sum(
@@ -657,10 +796,9 @@
         features(back_qkv)
         scatter_start()
         finish(l, 2, 0)
-        finish(l, 1, 1)
         transpose(x1.at[l], 0)
         transpose(gmid, 1)
-        pair(0, 0, lambda s: s // 3, lambda s: g3[s], step >= 0)
+        make(0, 0, lax.rem(step, 2), lambda s: s // 3, lambda s: g3[s], step >= 0)
         scatter_wait()
         norm_backward(l, 0, gtop, jnp.where(l > 0, 6 * l - 1, 12))
 
@@ -669,18 +807,19 @@
             scatter_wait(side)
             lax.fori_loop(0, CHUNK // 16, settle(l, recv2), 0)
             for k in range(N):
-                oblk[k] = st[:, BLK * k : BLK * (k + 1)]
-            give(oblk, out_hbm, outs, outr, True)
+                oblk[k] = st[:, BLK * k : BLK * (k + 1)].astype(BF)
+            go_start(2)
 
         return 0
 
     lax.fori_loop(0, LAYERS, backward, 0)
 
-    give(oblk, out_hbm, outs, outr, False)
-    give_wait(out_hbm, outr)
+    merge(0, 0, (LAYERS - 1) % 2)
+    go_wait(2, out_hbm)
+    sent(2)
     for k in range(N):
-        oblk[k] = gst[:, BLK * k : BLK * (k + 1)]
-    give(oblk, tg_hbm, tgs, tgr, True)
+        oblk[k] = gst[:, BLK * k : BLK * (k + 1)].astype(BF)
+    go_start(3)
 
     def c_copy(k):
         return remote(csum, cx.at[k], cxs.at[k], cxr.at[k], (d, near[k], c))
@@ -698,6 +837,8 @@
     for k in range(3):
         v_copy(k).start()
         c_copy(k).start()
+    go_pass(3, tg_hbm)
+    relay(0, 0)
     total = vb[r]
     for k in range(3):
         v_copy(k).wait_recv()
@@ -723,6 +864,7 @@
     vd[0] = total
     v_half = remote(vd.at[0], vd.at[1], vds.at[0], vds.at[1], (other, r, c))
     v_half.start()
+    finish(0, 1, 1)
     finish(0, 0, 0)
     c_half.wait()
     cout[...] = csum[d] + cd[...]
@@ -732,11 +874,10 @@
         v_copy(k).wait_send()
         z_copy(k).wait_send()
 
-    pl.semaphore_wait(credit, 1)
-    give(oblk, tg_hbm, tgs, tgr, False)
-    give_wait(tg_hbm, tgr)
-    spread(tok_hbm, tin, toks, tokr, False)
-    spread(cot_hbm, cin, cots, cotr, False)
+    pl.semaphore_wait(credit, 2)
+    go_wait(3, tg_hbm)
+    for u in (0, 1, 3):
+        sent(u)
     for i in range(3):
         for j in range(2):
             arrived = result(i, other, j)
@@ -745,8 +886,10 @@
         remote(vec_ref, pin.at[r], vs.at[k], vr.at[k], (d, near[k], c)).wait_send()
     for l in range(LAYERS):
         for i in range(3):
+            for k in range(2):
+                send_w(l, i, k).wait_send()
+                pass_w(l, i, k).wait_send()
             for k in range(3):
-                send_w(l, i, k).wait_send()
                 share_w(l, i, k).wait_send()
 
 
@@ -776,19 +919,20 @@
         vmem((CHUNK, D), F32),
         vmem((N, CHUNK, BLK), BF),
         vmem((N, CHUNK, BLK), BF),
-        vmem((N, CHUNK, BLK), F32),
+        vmem((N, CHUNK, BLK), BF),
+        vmem((4, N, CHUNK, BLK), BF),
         vmem((N, 16, BLK), F32),
         vmem((16, D), F32),
         vmem((2, ROWS, HALF), BF),
         vmem((ROWS, PAD), BF),
         vmem((4, ROWS, PAD), BF),
         vmem((3, ROWS, PAD), F32),
-        vmem((N, BLK, HALF), BF),
-        vmem((N, BLK, HALF), BF),
+        vmem((2, BLK, HALF), BF),
         vmem((2, N, BLK, HALF), BF),
-        vmem((3, 3, BLK, HALF), BF),
+        vmem((2, N, BLK, HALF), BF),
+        vmem((3, 2, BLK, HALF), BF),
         vmem((2, BLK, PAD), F32),
-        vmem((ROWS, D), BF),
+        vmem((3, 2, BLK // 2, HALF), BF),
         vmem((N, CHUNK, D), BF),
         vmem((16, D), F32),
         vmem((LAYERS, 4, HALF), F32),
@@ -799,14 +943,15 @@
         vmem((3, LAYERS, 4, HALF), F32),
         vmem((4, HALF), F32),
         dma((LAYERS, 3, 2)),
-        dma((LAYERS, 3, 3)), dma((LAYERS, 3, 3)),
+        dma((LAYERS, 3, 2)), dma((LAYERS, 3, 2)),
+        dma((LAYERS, 3, 2)), dma((LAYERS, 3, 2)),
         dma((LAYERS, 3, 3)), dma((LAYERS, 3, 3)),
         dma((3,)), dma((4,)),
+        dma((4, N)), dma((4, N)), dma((4, N)), dma((4, N)),
         dma((N,)), dma((N,)), dma((N,)), dma((N,)),
-        dma((N,)), dma((N,)), dma((N,)), dma((N,)),
-        dma((N,)), dma((N,)), dma((N,)), dma((N,)),
-        dma((N,)), dma((N,)), pltpu.SemaphoreType.REGULAR,
-        dma((3, 3)), dma((3, 3)), dma((2,)), dma((3, 2)),
+        dma((N,)), dma((2, N)), pltpu.SemaphoreType.REGULAR,
+        dma((3, 2)), dma((3, 2)), dma((2,)), dma((3, 2)),
+        dma((3, 2)), dma((3, 2)),
         dma((N,)), dma((N,)), dma((N,)), dma((N,)),
         dma((3,)), dma((3,)), dma((3,)), dma((N,)), dma((2,)),
         dma((3,)), dma((3,)), dma((2,)),
@@ -815,8 +960,8 @@
     return pl.pallas_call(
         kernel,
         out_shape=(
-            shape((ROWS, BLK), F32),
-            shape((ROWS, BLK), F32),
+            shape((ROWS, BLK), BF),
+            shape((ROWS, BLK), BF),
             shape((4, BLK, PAD), F32),
             shape((BLK, 2 * HALF), F32),
             shape((BLK, 2 * HALF), F32),
@@ -861,8 +1006,8 @@
     both = vout[:12].reshape(LAYERS, 6, BLK)
     layer = lax.dynamic_slice(both, (dp, 0, 0), (1, 6, BLK))
     return (
-        out[None, :SEQ],
-        tg[None, :SEQ],
+        out[None, :SEQ].astype(F32),
+        tg[None, :SEQ].astype(F32),
         ga[:3, :, :BLK].transpose(1, 0, 2)[None],
         cout[None, 0:2, :BLK],
         ga[3, :, :BLK].T[None],

time: 426 us -> 387 us (0.908)
  Pallas kernels: 401 us -> 361 us
    pallas_call x1, Pallas kernels: 401 us -> 361 us  [fused(): pl.pallas_call(kernel, out_shape=(shape((ROWS, BLK), BF), shape((ROWS, BL...]
where the time goes in v3:
time: 387 us; the launch traced here: 385 us
  Pallas kernels  361 us (93%)
  local copies, waits for them, and re-layouts  18.8 us (5%)
  other arithmetic  4.46 us (1%)
    pallas_call x1, Pallas kernels, fused(): pl.pallas_call(kernel, out_shape=(shape((ROWS, BLK), BF), shape((ROWS, BL...  361 us
    unnamed x30, local copies, waits for them, and re-layouts  9.06 us

profile of v3, /device:TPU:0, one launch (start us, length us, event | category | flops | bytes accessed | tf_op | source)
XLA Modules:
  0.0 384.7 jit_solution(12394160343396385408)
XLA Ops:
  0.6 0.8 fusion.4
  1.4 0.1 pad.25.clone
  1.5 0.1 pad_maximum_fusion.1
  1.6 0.6 pad.23.qb_ref
  2.2 1.3 copy.28
  3.5 0.0 copy-start.2
  3.5 0.0 copy-start.3
  3.5 0.0 copy-start.9
  3.6 0.0 copy-start.10
  3.6 0.0 copy-start.7
  3.6 0.0 copy-start.8
  3.6 0.0 copy-start.5
  3.6 3.3 fusion.2.wa_hbm
  6.9 0.0 copy-done.2
  6.9 0.7 pad.19.tok_hbm
  7.6 0.0 copy-done.3
  7.6 0.7 pad.20.cot_hbm
  8.3 0.0 copy-done.9
  8.3 0.0 copy-done.10
  8.3 0.0 copy-done.7
  8.3 0.0 copy-done.8
  8.4 0.6 pad.22.vec_ref
  9.0 0.0 copy-done.5
  9.0 0.6 reshape.41.ub_ref
  9.6 360.6 %shard_map.211 = (bf16[272,352]{1,0:T(8,128)(2,1)}, bf16[272,352]{1,0:T(8,128)(2,1)}, f32[4,352,384]{2,1,0:T(8,128)}, f32[352,1536]{1,0:T(8,128)}, f32[352,1536]...) custom-call(bf16[272,352]{1,0:T(8,128)(2,1)} %pad.19.tok_hbm, bf16[272,352]{1,0:T(8,128)(2,1)} %pad.20.cot_hbm, ...), custom_call_target="tpu_custom_call" | custom-call | tf_op jit(solution)/shard_map/pallas_call | solution.py:960
  370.2 0.0 copy-start.4
  370.2 1.1 bitcast_convert_fusion
  371.3 1.2 copy.31
  372.5 1.2 copy.32
  373.6 0.0 copy-done.4
  373.6 0.6 dynamic-slice_bitcast_fusion
  374.2 0.6 fusion.3
  374.8 0.0 copy-start.6
  374.8 0.0 copy-start.1
  374.8 2.8 slice_bitcast_fusion
  377.7 1.1 slice_bitcast_fusion.1
  378.7 1.0 copy.33
  379.8 0.0 copy-done.6
  379.8 0.6 copy.34
  380.4 0.6 slice_bitcast_fusion.3
  381.0 0.0 copy-done.1
  381.0 0.0 copy-start
  381.0 1.3 copy.37
  382.3 1.0 copy-done
  383.3 1.3 copy.38
  (6 shorter events, 0.0 us)
Async XLA Ops:
  3.5 3.4 copy-start.2
  3.5 4.1 %copy-start.3 = (bf16[1,257,352]{2,1,0:T(8,128)(2,1)S(1)}, bf16[1,257,352]{2,1,0:T(8,128)(2,1)}, u32[]{:S(2)}) copy-start(bf16[1,257,352]{2,1,0:T(8,128)(2,1)} %param.13) | copy-start | bytes 542788
  3.5 4.8 %copy-start.9 = (f32[2,352]{1,0:T(2,128)S(1)}, f32[2,352]{1,0:T(2,128)}, u32[]{:S(2)}) copy-start(f32[2,352]{1,0:T(2,128)} %param.17) | copy-start | bytes 8452
  3.6 4.8 %copy-start.10 = (f32[2,352]{1,0:T(2,128)S(1)}, f32[2,352]{1,0:T(2,128)}, u32[]{:S(2)}) copy-start(f32[2,352]{1,0:T(2,128)} %param.21) | copy-start | bytes 8452
  3.6 4.8 %copy-start.7 = (f32[2,2,352]{2,1,0:T(2,128)S(1)}, f32[2,2,352]{2,1,0:T(2,128)}, u32[]{:S(2)}) copy-start(f32[2,2,352]{2,1,0:T(2,128)} %param.23) | copy-start | bytes 16900
  3.6 4.8 %copy-start.8 = (f32[2,2,352]{2,1,0:T(2,128)S(1)}, f32[2,2,352]{2,1,0:T(2,128)}, u32[]{:S(2)}) copy-start(f32[2,2,352]{2,1,0:T(2,128)} %param.22) | copy-start | bytes 16900
  3.6 5.4 %copy-start.5 = (f32[2,1536]{1,0:T(2,128)S(1)}, f32[2,1536]{1,0:T(2,128)}, u32[]{:S(2)}) copy-start(f32[2,1536]{1,0:T(2,128)} %param.19) | copy-start | bytes 36868
  370.2 3.4 copy-start.4
  374.8 5.0 %copy-start.6 = (f32[4,768]{1,0:T(4,128)S(1)}, f32[4,768]{1,0:T(4,128)}, u32[]{:S(2)}) copy-start(f32[4,768]{1,0:T(4,128)} %get-tuple-element.22) | copy-start | bytes 36868
  374.8 6.1 %copy-start.1 = (f32[352,1536]{1,0:T(8,128)S(1)}, f32[352,1536]{1,0:T(8,128)}, u32[]{:S(2)}) copy-start(f32[352,1536]{1,0:T(8,128)} %get-tuple-element.24) | copy-start | bytes 6488068
  381.0 2.4 copy-start

commit v4 on v3

--- a/solution.py
+++ b/solution.py
@@ -52,11 +52,11 @@
     out_hbm, tg_hbm, ga_hbm, gu_hbm, gd_hbm, vout, cout,
     wa, wm, x1, x2, triple, att, lse, hid, slope, std, inv,
     gtop, gmid, lt, part, recv, st, gst, tin, cin, oblk, mid, pin, pv,
-    gb, da, g3, acc, sbuf, prx, keep, ici, fin, hop, recv2,
+    gb, da, g3, acc, sbuf, prx, keep, ici, fin, hop, rb, rb2, recv2,
     vsum, csum, vb, vx, vz, vd, cx, cd,
     wloc, wsend, wrecv, fsend, frecv, psend, precv, vs, vr, m1s, m1r, m2s, m2r,
-    zs, zr, rss, rsr, cs_s, cs_r, credit, gis, gir, fins, finr, hs, hr,
-    zs2, zr2, rss2, rsr2, vxs, vxr, vzs, vzr, vds, cxs, cxr, cds,
+    zs, zr, rss, rsr, lr, cs_s, cs_r, credit, gis, gir, fins, finr, hs, hr,
+    zs2, zr2, rss2, rsr2, lr2, vxs, vxr, vzs, vzr, vds, cxs, cxr, cds,
 ):
     d, r, c = lax.axis_index("dp"), lax.axis_index("row"), lax.axis_index("col")
     other = 1 - d
@@ -210,11 +210,11 @@
 
     come_start(0, tok_hbm)
 
-    def source_w(l, i, which):
+    def source_w(l, i, which, rows):
         if i == 0:
-            return wa_hbm.at[l, pl.ds(2 * which, 2)]
+            return wa_hbm.at[l, pl.ds(2 * which, 2), rows, :]
         lanes = pl.ds(pl.multiple_of(HALF * which, 128), HALF)
-        return (up_hbm if i == 1 else down_hbm).at[l, :, lanes]
+        return (up_hbm if i == 1 else down_hbm).at[l, rows, lanes]
 
     def rows_w(l, i, which, block):
         if i == 0:
@@ -223,13 +223,13 @@
 
     def local_w(l, i, which):
         return pltpu.make_async_copy(
-            source_w(l, i, which), rows_w(l, i, which, rblk(r)), wloc.at[l, i, which]
+            source_w(l, i, which, pl.ds(0, BLK)), rows_w(l, i, which, rblk(r)), wloc.at[l, i, which]
         )
 
-    def send_w(l, i, k):
+    def send_w(l, i, k, h):
         return remote(
-            source_w(l, i, d), rows_w(l, i, d, rblk(r)), wsend.at[l, i, k], wrecv.at[l, i, k],
-            (d, near[k], c),
+            source_w(l, i, d, pl.ds(h * (BLK // 2), BLK // 2)), rows_w(l, i, d, rhalf(r, h)),
+            wsend.at[l, i, k, h], wrecv.at[l, i, k, h], (d, near[k], c),
         )
 
     def pass_w(l, i, k):
@@ -240,15 +240,17 @@
         rows = rows_w(l, i, d, rblk(near[k]))
         return remote(rows, rows, psend.at[l, i, k], precv.at[l, i, k], (other, r, c))
 
-    def direct_w(l, i):
-        for k in range(2):
-            send_w(l, i, k).start()
+    def direct_w(l, i, parts=(0, 1)):
+        for part_ in parts:
+            for k in range(2):
+                send_w(l, i, k, k if part_ == 0 else 1 - k).start()
 
     def stage_w(l, i):
         for k in range(2):
-            send_w(l, i, k).wait_recv()
+            send_w(l, i, k, k).wait_recv()
             pass_w(l, i, k).start()
         for k in range(2):
+            send_w(l, i, k, 1 - k).wait_recv()
             share_w(l, i, k).start()
 
     def close_w(l, i):
@@ -264,77 +266,175 @@
             rows = rows_w(l, i, other, rblk(near[k]))
             pltpu.make_async_copy(rows, rows, precv.at[l, i, k]).wait()
 
-    direct_w(0, 0)
+    direct_w(0, 0, (0,))
+    come_pass(0, tin)
+    direct_w(0, 0, (1,))
     come_start(1, cot_hbm)
-    come_pass(0, tin)
     for l in range(LAYERS):
         for i in range(3):
             for which in range(2):
                 local_w(l, i, which).start()
 
-    def gather_start(x, zs=zs, zr=zr):
+    def half_rows(cs, h):
+        return pl.ds(STEP * cs + 32 * h, 32 if h == 0 or cs < N - 1 else LAST - 32)
+
+    halves = ((0, 0), (1, 0), (0, 1), (1, 1))
+    targets = ((2, 1), (2, 0), (1, 3), (1, 2))
+    relays = ((1, 0, [(2 + far, h) for far, h in halves]), (2, 3, [(1 - far, h) for far, h in halves]))
+
+    first_z, second_z = (zs, zr), (zs2, zr2)
+
+    def gather_start(x, sems=first_z):
+        zs, zr = sems
+        for c0 in range(N):
+
+            @pl.when(c == c0)
+            def _():
+                for n in range(4):
+                    rows = x.at[half_rows(c0, n % 2)]
+                    remote(
+                        rows, rows, zs.at[n], zr.at[c0, n % 2], (d, r, targets[c0][n // 2])
+                    ).start()
+
+    def gather_pass(x, *steps, sems=first_z):
+        zs, zr = sems
+        for c0, far, order in relays:
+
+            @pl.when(c == c0)
+            def _():
+                for n in steps:
+                    cs, h = order[n]
+                    rows = x.at[half_rows(cs, h)]
+                    pltpu.make_async_copy(rows, rows, zr.at[cs, h]).wait()
+                    remote(rows, rows, zs.at[4 + n], zr.at[cs, h], (d, r, far)).start()
+
+    def gather_wait(x, sems=first_z):
+        zs, zr = sems
+        for c0 in range(N):
+            passed = [order for at, _, order in relays if at == c0]
+
+            @pl.when(c == c0)
+            def _():
+                for cs in range(N):
+                    for h in range(2):
+                        if cs != c0 and not (passed and (cs, h) in passed[0]):
+                            rows = x.at[half_rows(cs, h)]
+                            pltpu.make_async_copy(rows, rows, zr.at[cs, h]).wait()
+                for n in range(4):
+                    rows = x.at[half_rows(c0, n % 2)]
+                    remote(rows, rows, zs.at[n], zr.at[c0, 0], (d, r, targets[c0][0])).wait_send()
+                if passed:
+                    for n, (cs, h) in enumerate(passed[0]):
+                        rows = x.at[half_rows(cs, h)]
+                        remote(rows, rows, zs.at[4 + n], zr.at[cs, h], (d, r, 0)).wait_send()
+
+    sides = ((0, 1, (3, 2)), (3, 2, (0, 1)))
+    inner = ((1, 0), (2, 3))
+
+    def size_of(cs):
+        return STEP if cs < N - 1 else LAST
+
+    def cols(h):
+        return pl.ds(0, HALF) if h == 0 else pl.ds(HALF, D - HALF)
+
+    main = (part, rb, recv, rss, rsr, lr)
+    side = (x2.at[LAYERS - 1], rb2, recv2, rss2, rsr2, lr2)
+
+    def end_copy(n, h, middle, dest, path):
+        part, rb, recv, rss, rsr, lr = path
+        return remote(
+            part.at[span(dest), cols(h)], rb.at[n, pl.ds(0, size_of(dest)), cols(h)],
+            rss.at[2 * n + h], lr.at[n, h], (d, r, middle),
+        )
+
+    def single_copy(dest, h, path):
+        part, rb, recv, rss, rsr, lr = path
+        return remote(
+            part.at[span(dest), cols(h)], recv.at[1, pl.ds(0, size_of(dest)), cols(h)],
+            rss.at[4 + h], rsr.at[h], (d, r, dest),
+        )
+
+    def sum_copy(n, h, dest, path):
+        part, rb, recv, rss, rsr, lr = path
+        rows = pl.ds(0, size_of(dest))
+        return remote(
+            rb.at[n, rows, cols(h)], recv.at[2, rows, cols(h)], rss.at[6 + 2 * n + h],
+            rsr.at[2 + h], (d, r, dest),
+        )
+
+    def add_start(h, path=main):
+        for end, middle, dests in sides:
+
+            @pl.when(c == end)
+            def _():
+                for n in range(2):
+                    end_copy(n, h, middle, dests[n], path).start()
+                single_copy(middle, h, path).start()
+
+        for middle, end in inner:
+
+            @pl.when(c == middle)
+            def _():
+                single_copy(end, h, path).start()
+
         for cs in range(N):
 
             @pl.when(c == cs)
             def _():
-                for ct in range(N):
-                    if ct != cs:
-                        rows = x.at[span(cs)]
-                        remote(rows, rows, zs.at[ct], zr.at[cs], (d, r, ct)).start()
-
-    def gather_wait(x, zs=zs, zr=zr):
+                path[2][0, 0 : size_of(cs), cols(h)] = path[0][span(cs), cols(h)]
+
+    def add_pass(*steps, path=main):
+        part, rb, recv, rss, rsr, lr = path
+        for end, middle, dests in sides:
+
+            @pl.when(c == middle)
+            def _():
+                for step in steps:
+                    h, n = step // 2, step % 2
+                    dest = dests[n]
+                    size = size_of(dest)
+                    rows = rb.at[n, pl.ds(0, size), cols(h)]
+                    pltpu.make_async_copy(rows, rows, lr.at[n, h]).wait()
+                    for start in range(0, size, 16):
+                        width = min(16, size - start)
+                        mine = part[pl.ds(STEP * dest + start, width), cols(h)]
+                        value = rb[n, start : start + width, cols(h)].astype(F32)
+                        rb[n, start : start + width, cols(h)] = (
+                            value + mine.astype(F32)
+                        ).astype(BF)
+                    sum_copy(n, h, dest, path).start()
+
+    def add_wait(path=main):
+        part, rb, recv, rss, rsr, lr = path
         for cs in range(N):
-            rows = x.at[span(cs)]
-
-            @pl.when(c != cs)
-            def _():
-                pltpu.make_async_copy(rows, rows, zr.at[cs]).wait()
 
             @pl.when(c == cs)
             def _():
-                for ct in range(N):
-                    if ct != cs:
-                        remote(rows, rows, zs.at[ct], zr.at[cs], (d, r, ct)).wait_send()
-
-    def scatter_copy(ct, part, recv, rss, rsr):
-        size = STEP if ct < N - 1 else LAST
-        return remote(
-            part.at[span(ct)], recv.at[c, pl.ds(0, size)], rss.at[ct], rsr.at[c], (d, r, ct)
-        )
-
-    main = (part, recv, rss, rsr)
-    side = (x2.at[LAYERS - 1], recv2, rss2, rsr2)
-
-    def scatter_start(path=main):
-        for ct in range(N):
-
-            @pl.when(c != ct)
+                for k in (1, 2):
+                    for h in range(2):
+                        rows = recv.at[k, pl.ds(0, size_of(cs)), cols(h)]
+                        pltpu.make_async_copy(rows, rows, rsr.at[2 * (k - 1) + h]).wait()
+
+        for end, middle, dests in sides:
+
+            @pl.when(c == end)
             def _():
-                scatter_copy(ct, *path).start()
-
-            @pl.when(c == ct)
+                for h in range(2):
+                    for n in range(2):
+                        end_copy(n, h, middle, dests[n], path).wait_send()
+                    single_copy(middle, h, path).wait_send()
+
+            @pl.when(c == middle)
             def _():
-                size = STEP if ct < N - 1 else LAST
-                path[1][ct, 0:size, :] = path[0][span(ct), :]
-
-    def scatter_wait(path=main):
-        for cs in range(N):
-            for big in (False, True):
-                size = LAST if big else STEP
-                rows = path[1].at[cs, pl.ds(0, size)]
-
-                @pl.when(jnp.logical_and(c != cs, last if big else jnp.logical_not(last)))
-                def _():
-                    pltpu.make_async_copy(rows, rows, path[3].at[cs]).wait()
-
-            @pl.when(c != cs)
-            def _():
-                scatter_copy(cs, *path).wait_send()
+                for h in range(2):
+                    single_copy(end, h, path).wait_send()
+                    for n in range(2):
+                        sum_copy(n, h, dests[n], path).wait_send()
 
     def received(rows, recv=recv):
         total = recv[0, rows, :].astype(F32)
-        for cs in range(1, N):
-            total = total + recv[cs, rows, :].astype(F32)
+        for k in range(1, recv.shape[0]):
+            total = total + recv[k, rows, :].astype(F32)
         return total
 
     def vector(row):
@@ -395,9 +495,14 @@
     def tiles(count, body):
         lax.fori_loop(0, count, lambda n, _: (body(n), 0)[1], 0)
 
-    def features(body):
-        tiles(5, lambda n: body(pl.multiple_of(n * 256, 256), 256))
+    def features(body, start=None):
+        tiles(3, lambda n: body(pl.multiple_of(n * 256, 256), 256))
+        if start is not None:
+            start(0)
+        tiles(2, lambda n: body(pl.multiple_of(HALF + n * 256, 256), 256))
         body(1280, 128)
+        if start is not None:
+            start(1)
 
     def assemble(src, dst):
         for k in range(N):
@@ -470,9 +575,13 @@
         def _():
             stage_w(0, 0)
             direct_w(0, 1)
-            direct_w(0, 2)
-
-        close_w(l, 0)
+
+        gather_pass(x1.at[l], 0, 1, 2, 3)
+
+        @pl.when(l == 0)
+        def _():
+            close_w(0, 0)
+
         gather_wait(x1.at[l])
 
         @pl.when(l == 0)
@@ -480,7 +589,7 @@
             come_wait(1, cin)
             assemble(cin, gst)
             lax.fori_loop(0, CHUNK // 16, top_rows, 0)
-            gather_start(gtop, zs2, zr2)
+            gather_start(gtop, second_z)
 
         need_w(l, 0)
 
@@ -490,33 +599,37 @@
 
         tiles(3, qkv)
         attend(l)
+        stage_w(l, 1)
+        direct_w(l, 2)
 
         def proj(start, size):
             value = dot_t(att[l], wa[l, 3, pl.ds(start, size), :])
             part[:, pl.ds(start, size)] = value.astype(BF)
 
-        features(proj)
-        scatter_start()
-        stage_w(l, 1)
-
-        @pl.when(l == 0)
-        def _():
-            direct_w(1, 0)
-
-        scatter_wait()
+        features(proj, add_start)
+        add_pass(0, 1, 2, 3)
+        close_w(l, 1)
+        add_wait()
         norm_forward(
             l, 1, x2.at[l], lambda rows: st[rows, :] + received(rows) + vector(6 * l + 4)
         )
         gather_start(x2.at[l])
-        close_w(l, 1)
+        gather_pass(x2.at[l], 0, 1)
         stage_w(l, 2)
 
         @pl.when(l == 0)
         def _():
-            direct_w(1, 1)
-
+            direct_w(1, 0)
+
+        gather_pass(x2.at[l], 2, 3)
+        gather_wait(x2.at[l])
+        close_w(l, 2)
         need_w(l, 1)
-        gather_wait(x2.at[l])
+
+        @pl.when(l == 0)
+        def _():
+            gather_pass(gtop, 0, 1, 2, 3, sems=second_z)
+
 
         for h in range(2):
 
@@ -530,16 +643,16 @@
                 slope[l, h, :, lanes] = (cdf + before * density).astype(slope.dtype)
 
             tiles(3, up)
-        close_w(l, 2)
         need_w(l, 2)
 
         @pl.when(l == 0)
         def _():
-            features(down(l, part))
-            scatter_start()
+            features(down(l, part), add_start)
             stage_w(1, 0)
-            direct_w(1, 2)
-            scatter_wait()
+            direct_w(1, 1)
+            add_pass(0, 1, 2, 3)
+            close_w(1, 0)
+            add_wait()
             lax.fori_loop(0, CHUNK // 16, settle(l, recv), 0)
 
         return 0
@@ -576,7 +689,7 @@
 
         lax.fori_loop(0, count // 16, strip, 0)
 
-    def make(i, slot, turn, left, right, wait_credit):
+    def make_send(i, turn, left, right, wait_credit):
         @pl.when(wait_credit)
         def _():
             pl.semaphore_wait(credit, 1)
@@ -591,12 +704,14 @@
 
         tiles(N, send_tile)
 
+    def make_keep(i, slot, turn, left, right, first):
         def keep_tile(k):
-            block_tile(keep.at[slot, k], i, d, k, left, right)
-
-        tiles(N, keep_tile)
-        for k in (2, 3):
-            piece(turn, k).wait_send()
+            block_tile(keep.at[slot, 2 * first + k], i, d, 2 * first + k, left, right)
+
+        tiles(2, keep_tile)
+        if first == 1:
+            for k in (2, 3):
+                piece(turn, k).wait_send()
 
     def half_copy(i, slot, k):
         half = pl.ds(k * (BLK // 2), BLK // 2)
@@ -717,14 +832,16 @@
 
         @pl.when(step == 0)
         def _():
-            gather_wait(gtop, zs2, zr2)
+            gather_wait(gtop, second_z)
 
         @pl.when(step > 0)
         def _():
             gather_start(gtop)
-            merge(0, 0, lax.rem(step + 1, 2))
+            gather_pass(gtop, 0, 1, 2, 3)
+            relay(0, 0)
             finish(l + 1, 1, 1)
             gather_wait(gtop)
+            add_pass(0, 1, 2, 3, path=side)
 
         for h in range(2):
 
@@ -739,44 +856,58 @@
 
             tiles(3, hidden)
 
-        @pl.when(step > 0)
-        def _():
-            relay(0, 0)
-            go_pass(2, out_hbm)
-
         def back_up(start, size):
             rows = pl.ds(start, size)
             value = dot_t(gb[0], wm[l, 0, rows, :]) + dot_t(gb[1], wm[l, 1, rows, :])
             part[:, pl.ds(start, size)] = value.astype(BF)
 
-        features(back_up)
-        scatter_start()
+        features(back_up, add_start)
         transpose(gtop, 0)
+        down_pair = (lax.rem(step, 2), lambda b: 0, lambda b: hid.at[l, b])
+        make_send(2, *down_pair, step > 0)
+        add_pass(0, 1)
 
         @pl.when(step > 0)
         def _():
             finish(l + 1, 0, 0)
 
-        make(2, 0, lax.rem(step, 2), lambda b: 0, lambda b: hid.at[l, b], step > 0)
-        scatter_wait()
+        make_keep(2, 0, *down_pair, 0)
+        add_pass(2)
+        make_keep(2, 0, *down_pair, 1)
+        add_pass(3)
+        merge(2, 0, lax.rem(step, 2))
+        add_wait()
         norm_backward(l, 1, gmid, 6 * l + 4)
         gather_start(gmid)
-        merge(2, 0, lax.rem(step, 2))
         transpose(x2.at[l], 1)
-        make(1, 1, lax.rem(step + 1, 2), lambda b: 1, lambda b: gb.at[b], step > 0)
+        gather_pass(gmid, 0, 1)
+        up_pair = (lax.rem(step + 1, 2), lambda b: 1, lambda b: gb.at[b])
+        make_send(1, *up_pair, step > 0)
+        gather_pass(gmid, 2, 3)
+        relay(2, 0)
+        make_keep(1, 1, *up_pair, 0)
+        make_keep(1, 1, *up_pair, 1)
 
         @pl.when(step == 0)
         def _():
             features(down(l, x2.at[LAYERS - 1]))
 
-        relay(2, 0)
+        merge(1, 1, lax.rem(step + 1, 2))
         gather_wait(gmid)
 
         @pl.when(step == 0)
         def _():
-            scatter_start(side)
-
-        merge(1, 1, lax.rem(step + 1, 2))
+            for h in range(2):
+                add_start(h, side)
+
+        @pl.when(step > 0)
+        def _():
+            add_wait(side)
+            lax.fori_loop(0, CHUNK // 16, settle(LAYERS - 1, recv2), 0)
+            for k in range(N):
+                oblk[k] = st[:, BLK * k : BLK * (k + 1)].astype(BF)
+            go_start(2)
+
         da[...] = dot(gmid[...], wa[l, 3]).astype(BF)
         attend_back(l)
         relay(1, 1)
@@ -793,28 +924,30 @@
             value = value + dot_t(g3[2], wa[l, 2, rows, :])
             part[:, pl.ds(start, size)] = value.astype(BF)
 
-        features(back_qkv)
-        scatter_start()
-        finish(l, 2, 0)
+        features(back_qkv, add_start)
         transpose(x1.at[l], 0)
         transpose(gmid, 1)
-        make(0, 0, lax.rem(step, 2), lambda s: s // 3, lambda s: g3[s], step >= 0)
-        scatter_wait()
+        add_pass(0)
+        head_pair = (lax.rem(step, 2), lambda s: s // 3, lambda s: g3[s])
+        make_send(0, *head_pair, step >= 0)
+        add_pass(1, 2)
+        finish(l, 2, 0)
+        make_keep(0, 0, *head_pair, 0)
+        add_pass(3)
+        make_keep(0, 0, *head_pair, 1)
+
+        @pl.when(step > 0)
+        def _():
+            go_pass(2, out_hbm)
+
+        merge(0, 0, lax.rem(step, 2))
+        add_wait()
         norm_backward(l, 0, gtop, jnp.where(l > 0, 6 * l - 1, 12))
 
-        @pl.when(step == 0)
-        def _():
-            scatter_wait(side)
-            lax.fori_loop(0, CHUNK // 16, settle(l, recv2), 0)
-            for k in range(N):
-                oblk[k] = st[:, BLK * k : BLK * (k + 1)].astype(BF)
-            go_start(2)
-
         return 0
 
     lax.fori_loop(0, LAYERS, backward, 0)
 
-    merge(0, 0, (LAYERS - 1) % 2)
     go_wait(2, out_hbm)
     sent(2)
     for k in range(N):
@@ -887,7 +1020,8 @@
     for l in range(LAYERS):
         for i in range(3):
             for k in range(2):
-                send_w(l, i, k).wait_send()
+                for h in range(2):
+                    send_w(l, i, k, h).wait_send()
                 pass_w(l, i, k).wait_send()
             for k in range(3):
                 share_w(l, i, k).wait_send()
@@ -914,7 +1048,7 @@
         vmem((ROWS, D), BF),
         vmem((2, D, ROWS), BF),
         vmem((ROWS, D), BF),
-        vmem((N, CHUNK, D), BF),
+        vmem((3, CHUNK, D), BF),
         vmem((CHUNK, D), F32),
         vmem((CHUNK, D), F32),
         vmem((N, CHUNK, BLK), BF),
@@ -933,7 +1067,9 @@
         vmem((3, 2, BLK, HALF), BF),
         vmem((2, BLK, PAD), F32),
         vmem((3, 2, BLK // 2, HALF), BF),
-        vmem((N, CHUNK, D), BF),
+        vmem((2, LAST, D), BF),
+        vmem((2, LAST, D), BF),
+        vmem((3, CHUNK, D), BF),
         vmem((16, D), F32),
         vmem((LAYERS, 4, HALF), F32),
         vmem((N, 16, BLK), F32),
@@ -943,16 +1079,16 @@
         vmem((3, LAYERS, 4, HALF), F32),
         vmem((4, HALF), F32),
         dma((LAYERS, 3, 2)),
-        dma((LAYERS, 3, 2)), dma((LAYERS, 3, 2)),
+        dma((LAYERS, 3, 2, 2)), dma((LAYERS, 3, 2, 2)),
         dma((LAYERS, 3, 2)), dma((LAYERS, 3, 2)),
         dma((LAYERS, 3, 3)), dma((LAYERS, 3, 3)),
         dma((3,)), dma((4,)),
         dma((4, N)), dma((4, N)), dma((4, N)), dma((4, N)),
-        dma((N,)), dma((N,)), dma((N,)), dma((N,)),
+        dma((8,)), dma((N, 2)), dma((10,)), dma((4,)), dma((2, 2)),
         dma((N,)), dma((2, N)), pltpu.SemaphoreType.REGULAR,
         dma((3, 2)), dma((3, 2)), dma((2,)), dma((3, 2)),
         dma((3, 2)), dma((3, 2)),
-        dma((N,)), dma((N,)), dma((N,)), dma((N,)),
+        dma((8,)), dma((N, 2)), dma((10,)), dma((4,)), dma((2, 2)),
         dma((3,)), dma((3,)), dma((3,)), dma((N,)), dma((2,)),
         dma((3,)), dma((3,)), dma((2,)),
     ]

time: 387 us -> 342 us (0.88)
  Pallas kernels: 361 us -> 317 us
    pallas_call x1, Pallas kernels: 361 us -> 317 us  [fused(): pl.pallas_call(kernel, out_shape=(shape((ROWS, BLK), BF), shape((ROWS, BL...]
where the time goes in v4:
time: 342 us; the launch traced here: 341 us
  Pallas kernels  317 us (93%)
  local copies, waits for them, and re-layouts  18.8 us (5%)
  other arithmetic  4.46 us (1%)
    pallas_call x1, Pallas kernels, fused(): pl.pallas_call(kernel, out_shape=(shape((ROWS, BLK), BF), shape((ROWS, BL...  317 us
    unnamed x30, local copies, waits for them, and re-layouts  9.06 us

profile of v4, /device:TPU:0, one launch (start us, length us, event | category | flops | bytes accessed | tf_op | source)
XLA Modules:
  0.0 340.7 jit_solution(17228987196687571079)
XLA Ops:
  0.6 0.8 fusion.4
  1.4 0.1 pad.25.clone
  1.5 0.1 pad_maximum_fusion.1
  1.6 0.6 pad.23.qb_ref
  2.2 1.3 copy.28
  3.5 0.0 copy-start.2
  3.5 0.0 copy-start.3
  3.5 0.0 copy-start.9
  3.6 0.0 copy-start.10
  3.6 0.0 copy-start.7
  3.6 0.0 copy-start.8
  3.6 0.0 copy-start.5
  3.6 3.3 fusion.2.wa_hbm
  6.9 0.0 copy-done.2
  6.9 0.7 pad.19.tok_hbm
  7.6 0.0 copy-done.3
  7.6 0.7 pad.20.cot_hbm
  8.3 0.0 copy-done.9
  8.3 0.0 copy-done.10
  8.3 0.0 copy-done.7
  8.3 0.0 copy-done.8
  8.4 0.6 pad.22.vec_ref
  9.0 0.0 copy-done.5
  9.0 0.6 reshape.41.ub_ref
  9.6 316.6 %shard_map.211 = (bf16[272,352]{1,0:T(8,128)(2,1)}, bf16[272,352]{1,0:T(8,128)(2,1)}, f32[4,352,384]{2,1,0:T(8,128)}, f32[352,1536]{1,0:T(8,128)}, f32[352,1536]...) custom-call(bf16[272,352]{1,0:T(8,128)(2,1)} %pad.19.tok_hbm, bf16[272,352]{1,0:T(8,128)(2,1)} %pad.20.cot_hbm, ...), custom_call_target="tpu_custom_call" | custom-call | tf_op jit(solution)/shard_map/pallas_call | solution.py:1096
  326.2 0.0 copy-start.4
  326.2 1.1 bitcast_convert_fusion
  327.3 1.2 copy.31
  328.5 1.2 copy.32
  329.6 0.0 copy-done.4
  329.6 0.6 dynamic-slice_bitcast_fusion
  330.2 0.6 fusion.3
  330.8 0.0 copy-start.6
  330.8 0.0 copy-start.1
  330.8 2.8 slice_bitcast_fusion
  333.7 1.1 slice_bitcast_fusion.1
  334.7 1.0 copy.33
  335.8 0.0 copy-done.6
  335.8 0.6 copy.34
  336.4 0.6 slice_bitcast_fusion.3
  337.0 0.0 copy-done.1
  337.0 0.0 copy-start
  337.0 1.3 copy.37
  338.3 1.0 copy-done
  339.3 1.3 copy.38
  (6 shorter events, 0.0 us)
Async XLA Ops:
  3.5 3.4 copy-start.2
  3.5 4.1 %copy-start.3 = (bf16[1,257,352]{2,1,0:T(8,128)(2,1)S(1)}, bf16[1,257,352]{2,1,0:T(8,128)(2,1)}, u32[]{:S(2)}) copy-start(bf16[1,257,352]{2,1,0:T(8,128)(2,1)} %param.13) | copy-start | bytes 542788
  3.5 4.8 %copy-start.9 = (f32[2,352]{1,0:T(2,128)S(1)}, f32[2,352]{1,0:T(2,128)}, u32[]{:S(2)}) copy-start(f32[2,352]{1,0:T(2,128)} %param.17) | copy-start | bytes 8452
  3.6 4.8 %copy-start.10 = (f32[2,352]{1,0:T(2,128)S(1)}, f32[2,352]{1,0:T(2,128)}, u32[]{:S(2)}) copy-start(f32[2,352]{1,0:T(2,128)} %param.21) | copy-start | bytes 8452
  3.6 4.8 %copy-start.7 = (f32[2,2,352]{2,1,0:T(2,128)S(1)}, f32[2,2,352]{2,1,0:T(2,128)}, u32[]{:S(2)}) copy-start(f32[2,2,352]{2,1,0:T(2,128)} %param.23) | copy-start | bytes 16900
  3.6 4.8 %copy-start.8 = (f32[2,2,352]{2,1,0:T(2,128)S(1)}, f32[2,2,352]{2,1,0:T(2,128)}, u32[]{:S(2)}) copy-start(f32[2,2,352]{2,1,0:T(2,128)} %param.22) | copy-start | bytes 16900
  3.6 5.4 %copy-start.5 = (f32[2,1536]{1,0:T(2,128)S(1)}, f32[2,1536]{1,0:T(2,128)}, u32[]{:S(2)}) copy-start(f32[2,1536]{1,0:T(2,128)} %param.19) | copy-start | bytes 36868
  326.2 3.4 %copy-start.4 = (f32[16,352]{1,0:T(8,128)S(1)}, f32[16,352]{1,0:T(8,128)}, u32[]{:S(2)}) copy-start(f32[16,352]{1,0:T(8,128)} %get-tuple-element.23) | copy-start | bytes 67588
  330.8 5.0 %copy-start.6 = (f32[4,768]{1,0:T(4,128)S(1)}, f32[4,768]{1,0:T(4,128)}, u32[]{:S(2)}) copy-start(f32[4,768]{1,0:T(4,128)} %get-tuple-element.22) | copy-start | bytes 36868
  330.8 6.1 %copy-start.1 = (f32[352,1536]{1,0:T(8,128)S(1)}, f32[352,1536]{1,0:T(8,128)}, u32[]{:S(2)}) copy-start(f32[352,1536]{1,0:T(8,128)} %get-tuple-element.24) | copy-start | bytes 6488068
  337.0 2.4 copy-start

commit v5 on v4

--- a/solution.py
+++ b/solution.py
@@ -48,12 +48,12 @@
 
 
 def kernel(
-    tok_hbm, cot_hbm, wa_hbm, up_hbm, down_hbm, vec_ref, qb_ref, ub_ref,
+    io_hbm, wa_hbm, up_hbm, down_hbm, gain_ref, shift_ref, pb_ref, db_ref, qv_ref, ub_ref,
     out_hbm, tg_hbm, ga_hbm, gu_hbm, gd_hbm, vout, cout,
     wa, wm, x1, x2, triple, att, lse, hid, slope, std, inv,
     gtop, gmid, lt, part, recv, st, gst, tin, cin, oblk, mid, pin, pv,
     gb, da, g3, acc, sbuf, prx, keep, ici, fin, hop, rb, rb2, recv2,
-    vsum, csum, vb, vx, vz, vd, cx, cd,
+    vec_ref, qb_ref, vsum, csum, vb, vx, vz, vd, cx, cd,
     wloc, wsend, wrecv, fsend, frecv, psend, precv, vs, vr, m1s, m1r, m2s, m2r,
     zs, zr, rss, rsr, lr, cs_s, cs_r, credit, gis, gir, fins, finr, hs, hr,
     zs2, zr2, rss2, rsr2, lr2, vxs, vxr, vzs, vzr, vds, cxs, cxr, cds,
@@ -82,6 +82,15 @@
     cin[...] = jnp.zeros_like(cin)
     vsum[...] = jnp.zeros_like(vsum)
     csum[...] = jnp.zeros_like(csum)
+    vec_ref[...] = jnp.zeros_like(vec_ref)
+    qb_ref[...] = jnp.zeros_like(qb_ref)
+    for l in range(LAYERS):
+        for j in range(2):
+            vec_ref[6 * l + j : 6 * l + j + 1, :] = gain_ref[l, j : j + 1, :]
+            vec_ref[6 * l + 2 + j : 6 * l + 3 + j, :] = shift_ref[l, j : j + 1, :]
+            qb_ref[l, 2 * j : 2 * j + 1, 0:BLK] = qv_ref[l, j : j + 1, :]
+        vec_ref[6 * l + 4 : 6 * l + 5, :] = pb_ref[l : l + 1, :]
+        vec_ref[6 * l + 5 : 6 * l + 6, :] = db_ref[l : l + 1, :]
     barrier = pltpu.get_barrier_semaphore()
     for k in range(N * N):
         pl.semaphore_signal(
@@ -208,7 +217,7 @@
 
             by_size(second)
 
-    come_start(0, tok_hbm)
+    come_start(0, io_hbm.at[0])
 
     def source_w(l, i, which, rows):
         if i == 0:
@@ -269,7 +278,7 @@
     direct_w(0, 0, (0,))
     come_pass(0, tin)
     direct_w(0, 0, (1,))
-    come_start(1, cot_hbm)
+    come_start(1, io_hbm.at[1])
     for l in range(LAYERS):
         for i in range(3):
             for which in range(2):
@@ -284,13 +293,13 @@
 
     first_z, second_z = (zs, zr), (zs2, zr2)
 
-    def gather_start(x, sems=first_z):
+    def gather_start(x, sems=first_z, steps=(0, 1, 2, 3)):
         zs, zr = sems
         for c0 in range(N):
 
             @pl.when(c == c0)
             def _():
-                for n in range(4):
+                for n in steps:
                     rows = x.at[half_rows(c0, n % 2)]
                     remote(
                         rows, rows, zs.at[n], zr.at[c0, n % 2], (d, r, targets[c0][n // 2])
@@ -451,6 +460,12 @@
         index = lax.broadcasted_iota(jnp.int32, (16, 1), 0) + 16 * t
         return jnp.where(index < valid, value, 0.0)
 
+    def early(x, body):
+        lax.fori_loop(0, 2, body, 0)
+        gather_start(x, steps=(0,))
+        lax.fori_loop(2, CHUNK // 16, body, 0)
+        gather_start(x, steps=(1, 2, 3))
+
     def norm_forward(l, j, x, extra):
         def body(t, _):
             rows = pl.ds(pl.multiple_of(16 * t, 16), 16)
@@ -466,7 +481,7 @@
             own_rows(x, t, value.astype(BF))
             return 0
 
-        lax.fori_loop(0, CHUNK // 16, body, 0)
+        early(x, body)
 
     def norm_backward(l, j, x, bias_row):
         def body(t, _):
@@ -490,17 +505,26 @@
                 )
             return 0
 
-        lax.fori_loop(0, CHUNK // 16, body, 0)
+        if j == 1:
+            early(x, body)
+        else:
+
+            @pl.when(l > 0)
+            def _():
+                early(x, body)
+
+            @pl.when(l == 0)
+            def _():
+                lax.fori_loop(0, CHUNK // 16, body, 0)
 
     def tiles(count, body):
         lax.fori_loop(0, count, lambda n, _: (body(n), 0)[1], 0)
 
     def features(body, start=None):
-        tiles(3, lambda n: body(pl.multiple_of(n * 256, 256), 256))
+        body(0, 768)
         if start is not None:
             start(0)
-        tiles(2, lambda n: body(pl.multiple_of(HALF + n * 256, 256), 256))
-        body(1280, 128)
+        body(HALF, 640)
         if start is not None:
             start(1)
 
@@ -569,7 +593,6 @@
             return st[rows, :]
 
         norm_forward(l, 0, x1.at[l], take)
-        gather_start(x1.at[l])
 
         @pl.when(l == 0)
         def _():
@@ -613,7 +636,6 @@
         norm_forward(
             l, 1, x2.at[l], lambda rows: st[rows, :] + received(rows) + vector(6 * l + 4)
         )
-        gather_start(x2.at[l])
         gather_pass(x2.at[l], 0, 1)
         stage_w(l, 2)
 
@@ -634,15 +656,15 @@
         for h in range(2):
 
             def up(n):
-                lanes = pl.ds(pl.multiple_of(n * 256, 256), 256)
-                before = dot(x2[l], wm[l, h, :, lanes]) + ub_ref[l, pl.ds(h, 1), lanes]
+                lanes = pl.ds(pl.multiple_of(n * 768, 128), 768)
+                before = dot(x2[l], wm[l, h, :, lanes]) + ub_ref[pl.ds(l, 1), HALF * h : HALF * (h + 1)]
                 half = before * (0.5**0.5)
                 cdf = 0.5 + 0.5 * lax.erf(half)
                 hid[l, h, :, lanes] = (before * cdf).astype(BF)
                 density = jnp.exp(-half * half) * 0.3989422804014327
                 slope[l, h, :, lanes] = (cdf + before * density).astype(slope.dtype)
 
-            tiles(3, up)
+            tiles(1, up)
         need_w(l, 2)
 
         @pl.when(l == 0)
@@ -666,9 +688,9 @@
 
         tiles(D // 128, body)
 
-    def piece(turn, k):
+    def piece(turn, n):
         return remote(
-            sbuf.at[lax.rem(k, 2)], prx.at[turn, k], cs_s.at[k], cs_r.at[turn, k], (other, r, c)
+            sbuf.at[n % 2], prx.at[turn, n], cs_s.at[n], cs_r.at[turn, n], (other, r, c)
         )
 
     def block_tile(ref, i, b, k, left, right):
@@ -682,36 +704,7 @@
                 value = dot(lt[left(b), rows, :], right(b)[:, lanes])
             ref[:, lanes] = value.astype(BF)
 
-    def strips(count, body):
-        def strip(t, _):
-            body(pl.ds(pl.multiple_of(16 * t, 16), 16))
-            return 0
-
-        lax.fori_loop(0, count // 16, strip, 0)
-
-    def make_send(i, turn, left, right, wait_credit):
-        @pl.when(wait_credit)
-        def _():
-            pl.semaphore_wait(credit, 1)
-
-        def send_tile(k):
-            @pl.when(k >= 2)
-            def _():
-                piece(turn, k - 2).wait_send()
-
-            block_tile(sbuf.at[lax.rem(k, 2)], i, other, k, left, right)
-            piece(turn, k).start()
-
-        tiles(N, send_tile)
-
-    def make_keep(i, slot, turn, left, right, first):
-        def keep_tile(k):
-            block_tile(keep.at[slot, 2 * first + k], i, d, 2 * first + k, left, right)
-
-        tiles(2, keep_tile)
-        if first == 1:
-            for k in (2, 3):
-                piece(turn, k).wait_send()
+    order = (near[2], near[0], near[1], r)
 
     def half_copy(i, slot, k):
         half = pl.ds(k * (BLK // 2), BLK // 2)
@@ -719,28 +712,49 @@
             keep.at[slot, near[2], half], hop.at[i, k], hs.at[i, k], hr.at[i, k], (d, near[k], c)
         )
 
-    def block_copy(i, slot, k):
+    def block_copy(i, slot, k, h):
+        half = pl.ds(h * (BLK // 2), BLK // 2)
         return remote(
-            keep.at[slot, near[k]], ici.at[i, k], gis.at[i, k], gir.at[i, k], (d, near[k], c)
+            keep.at[slot, near[k], half], ici.at[i, k, half], gis.at[i, k, h], gir.at[i, k, h],
+            (d, near[k], c),
         )
 
-    def merge(i, slot, turn):
-        def add(k):
-            rows = prx.at[turn, k]
-            pltpu.make_async_copy(rows, rows, cs_r.at[turn, k]).wait()
-
-            def strip(rows):
-                value = keep[slot, k, rows, :].astype(F32) + prx[turn, k, rows, :].astype(F32)
-                keep[slot, k, rows, :] = value.astype(BF)
-
-            strips(BLK, strip)
-
-        add(near[2])
-        for k in range(2):
-            half_copy(i, slot, k).start()
-        for k in (near[0], near[1], r):
-            add(k)
-        pl.semaphore_signal(credit, inc=1, device_id=(other, r, c), device_id_type=MESH)
+    def merge(i, slot, turn, n):
+        rows = prx.at[turn, n]
+        pltpu.make_async_copy(rows, rows, cs_r.at[turn, n]).wait()
+
+        def strip(t, _):
+            rows = pl.ds(pl.multiple_of(16 * t, 16), 16)
+            value = keep[slot, order[n], rows, :].astype(F32) + prx[turn, n, rows, :].astype(F32)
+            keep[slot, order[n], rows, :] = value.astype(BF)
+            return 0
+
+        lax.fori_loop(0, BLK // 16, strip, 0)
+        if n == 0:
+            for k in range(2):
+                half_copy(i, slot, k).start()
+        elif n < 3:
+            block_copy(i, slot, n - 1, n - 1).start()
+
+    def make(i, slot, turn, left, right, first, n):
+        if n == 0:
+
+            @pl.when(first)
+            def _():
+                pl.semaphore_wait(credit, 1)
+
+        if n >= 2:
+            piece(turn, n - 2).wait_send()
+        block_tile(sbuf.at[n % 2], i, other, order[n], left, right)
+        piece(turn, n).start()
+        block_tile(keep.at[slot, order[n]], i, d, order[n], left, right)
+        if n > 0:
+            merge(i, slot, turn, n - 1)
+        if n == 3:
+            merge(i, slot, turn, 3)
+            for k in (2, 3):
+                piece(turn, k).wait_send()
+            pl.semaphore_signal(credit, inc=1, device_id=(other, r, c), device_id_type=MESH)
 
     def relay(i, slot):
         for k in range(2):
@@ -755,7 +769,7 @@
                 return 0
 
             lax.fori_loop(0, BLK // 32, strip, 0)
-            block_copy(i, slot, 1 - k).start()
+            block_copy(i, slot, 1 - k, k).start()
 
     def result(i, which, j):
         if i == 0:
@@ -765,8 +779,9 @@
 
     def finish(l, i, slot):
         for k in range(2):
-            arrived = ici.at[i, k]
-            pltpu.make_async_copy(arrived, arrived, gir.at[i, k]).wait()
+            for h in range(2):
+                arrived = ici.at[i, k, pl.ds(h * (BLK // 2), BLK // 2)]
+                pltpu.make_async_copy(arrived, arrived, gir.at[i, k, h]).wait()
 
         def body(t, _):
             rows = pl.ds(pl.multiple_of(16 * t, 16), 16)
@@ -802,7 +817,8 @@
 
         for k in range(2):
             half_copy(i, slot, k).wait_send()
-            block_copy(i, slot, k).wait_send()
+            for h in range(2):
+                block_copy(i, slot, k, h).wait_send()
 
     def attend_back(l):
         for s in range(3):
@@ -836,7 +852,6 @@
 
         @pl.when(step > 0)
         def _():
-            gather_start(gtop)
             gather_pass(gtop, 0, 1, 2, 3)
             relay(0, 0)
             finish(l + 1, 1, 1)
@@ -846,7 +861,7 @@
         for h in range(2):
 
             def hidden(n):
-                lanes = pl.ds(pl.multiple_of(n * 256, 256), 256)
+                lanes = pl.ds(pl.multiple_of(n * 768, 128), 768)
                 value = dot(gtop[...], wm[l, 2 + h, :, lanes]) * slope[l, h, :, lanes].astype(F32)
                 low = value.astype(BF)
                 gb[h, :, lanes] = low
@@ -854,7 +869,7 @@
                     low.astype(F32), axis=0, keepdims=True
                 )
 
-            tiles(3, hidden)
+            tiles(1, hidden)
 
         def back_up(start, size):
             rows = pl.ds(start, size)
@@ -863,36 +878,36 @@
 
         features(back_up, add_start)
         transpose(gtop, 0)
-        down_pair = (lax.rem(step, 2), lambda b: 0, lambda b: hid.at[l, b])
-        make_send(2, *down_pair, step > 0)
+        down_pair = (2, 0, lax.rem(step, 2), lambda b: 0, lambda b: hid.at[l, b], step > 0)
+
+        @pl.when(step > 0)
+        def _():
+            finish(l + 1, 0, 0)
+
+        make(*down_pair, 0)
         add_pass(0, 1)
-
-        @pl.when(step > 0)
-        def _():
-            finish(l + 1, 0, 0)
-
-        make_keep(2, 0, *down_pair, 0)
+        make(*down_pair, 1)
         add_pass(2)
-        make_keep(2, 0, *down_pair, 1)
+        make(*down_pair, 2)
         add_pass(3)
-        merge(2, 0, lax.rem(step, 2))
+        make(*down_pair, 3)
         add_wait()
         norm_backward(l, 1, gmid, 6 * l + 4)
-        gather_start(gmid)
         transpose(x2.at[l], 1)
+        up_pair = (1, 1, lax.rem(step + 1, 2), lambda b: 1, lambda b: gb.at[b], step > 0)
+        make(*up_pair, 0)
         gather_pass(gmid, 0, 1)
-        up_pair = (lax.rem(step + 1, 2), lambda b: 1, lambda b: gb.at[b])
-        make_send(1, *up_pair, step > 0)
+        make(*up_pair, 1)
         gather_pass(gmid, 2, 3)
         relay(2, 0)
-        make_keep(1, 1, *up_pair, 0)
-        make_keep(1, 1, *up_pair, 1)
+        make(*up_pair, 2)
+        make(*up_pair, 3)
+        transpose(x1.at[l], 0)
 
         @pl.when(step == 0)
         def _():
             features(down(l, x2.at[LAYERS - 1]))
 
-        merge(1, 1, lax.rem(step + 1, 2))
         gather_wait(gmid)
 
         @pl.when(step == 0)
@@ -925,22 +940,21 @@
             part[:, pl.ds(start, size)] = value.astype(BF)
 
         features(back_qkv, add_start)
-        transpose(x1.at[l], 0)
         transpose(gmid, 1)
+        finish(l, 2, 0)
+        head_pair = (0, 0, lax.rem(step, 2), lambda s: s // 3, lambda s: g3[s], step >= 0)
+        make(*head_pair, 0)
         add_pass(0)
-        head_pair = (lax.rem(step, 2), lambda s: s // 3, lambda s: g3[s])
-        make_send(0, *head_pair, step >= 0)
+        make(*head_pair, 1)
         add_pass(1, 2)
-        finish(l, 2, 0)
-        make_keep(0, 0, *head_pair, 0)
+        make(*head_pair, 2)
         add_pass(3)
-        make_keep(0, 0, *head_pair, 1)
+        make(*head_pair, 3)
 
         @pl.when(step > 0)
         def _():
             go_pass(2, out_hbm)
 
-        merge(0, 0, lax.rem(step, 2))
         add_wait()
         norm_backward(l, 0, gtop, jnp.where(l > 0, 6 * l - 1, 12))
 
@@ -1070,6 +1084,8 @@
         vmem((2, LAST, D), BF),
         vmem((2, LAST, D), BF),
         vmem((3, CHUNK, D), BF),
+        vmem((16, BLK), F32),
+        vmem((LAYERS, 3, PAD), F32),
         vmem((16, D), F32),
         vmem((LAYERS, 4, HALF), F32),
         vmem((N, 16, BLK), F32),
@@ -1086,7 +1102,7 @@
         dma((4, N)), dma((4, N)), dma((4, N)), dma((4, N)),
         dma((8,)), dma((N, 2)), dma((10,)), dma((4,)), dma((2, 2)),
         dma((N,)), dma((2, N)), pltpu.SemaphoreType.REGULAR,
-        dma((3, 2)), dma((3, 2)), dma((2,)), dma((3, 2)),
+        dma((3, 2, 2)), dma((3, 2, 2)), dma((2,)), dma((3, 2)),
         dma((3, 2)), dma((3, 2)),
         dma((8,)), dma((N, 2)), dma((10,)), dma((4,)), dma((2, 2)),
         dma((3,)), dma((3,)), dma((3,)), dma((N,)), dma((2,)),
@@ -1104,7 +1120,7 @@
             shape((16, BLK), F32),
             shape((4, HALF), F32),
         ),
-        in_specs=[anywhere] * 5 + [whole] * 3,
+        in_specs=[anywhere] * 4 + [whole] * 6,
         out_specs=(anywhere,) * 5 + (whole, whole),
         scratch_shapes=scratch,
         compiler_params=pltpu.CompilerParams(
@@ -1125,20 +1141,15 @@
     up_weight, up_bias, down_weight, down_bias, norm_gain, norm_shift,
 ):
     dp = lax.axis_index("dp")
-    tok = widen(tokens[0], 0, ROWS)
-    cot = widen(cotangent[0], 0, ROWS)
+    both_in = widen(jnp.concatenate([tokens, cotangent]), 1, ROWS)
     heads = jnp.concatenate(
         [qkv_weight.transpose(0, 2, 1, 3), proj_weight.transpose(0, 2, 1)[:, None]], axis=1
     )
-    vec = jnp.concatenate(
-        [norm_gain, norm_shift, proj_bias[:, None], down_bias[:, None]], axis=1
-    ).reshape(12, BLK)
-    vec = widen(vec, 0, 16)
-    zero = jnp.zeros_like(qv_bias[:, 0])
-    qb = widen(jnp.stack([qv_bias[:, 0], zero, qv_bias[:, 1]], axis=1))
-    ub = up_bias.reshape(LAYERS, 2, HALF)
     down = down_weight.transpose(0, 2, 1)
-    out, tg, ga, gu, gd, vout, cout = fused(tok, cot, widen(heads), up_weight, down, vec, qb, ub)
+    out, tg, ga, gu, gd, vout, cout = fused(
+        both_in, widen(heads), up_weight, down,
+        norm_gain, norm_shift, proj_bias, down_bias, qv_bias, up_bias,
+    )
     both = vout[:12].reshape(LAYERS, 6, BLK)
     layer = lax.dynamic_slice(both, (dp, 0, 0), (1, 6, BLK))
     return (

time: 342 us -> 326 us (0.953)
  Pallas kernels: 317 us -> 307 us
  local copies, waits for them, and re-layouts: 18.8 us -> 12.8 us
    pallas_call x1, Pallas kernels: 317 us -> 307 us  [fused(): pl.pallas_call(kernel, out_shape=(shape((ROWS, BLK), BF), shape((ROWS, BL...]
    unnamed x30 -> x20, local copies, waits for them, and re-layouts: 9.06 us -> 9.03 us
where the time goes in v5:
time: 326 us
  Pallas kernels  307 us (94%)
  local copies, waits for them, and re-layouts  12.8 us (4%)
  other arithmetic  5.11 us (2%)
    pallas_call x1, Pallas kernels, fused(): pl.pallas_call(kernel, out_shape=(shape((ROWS, BLK), BF), shape((ROWS, BL...  307 us
    unnamed x20, local copies, waits for them, and re-layouts  9.03 us

profile of v5, /device:TPU:0, one launch (start us, length us, event | category | flops | bytes accessed | tf_op | source)
XLA Modules:
  0.0 325.8 jit_solution(2598420329616747997)
XLA Ops:
  0.6 1.3 copy.28
  2.0 0.0 copy-start.3
  2.0 0.0 copy-start.4
  2.0 3.1 fusion.2.wa_hbm
  5.2 0.0 copy-done.3
  5.2 0.0 copy-done.4
  5.2 0.8 fusion.5.io_hbm
  6.0 307.2 %shard_map.211 = (bf16[272,352]{1,0:T(8,128)(2,1)}, bf16[272,352]{1,0:T(8,128)(2,1)}, f32[4,352,384]{2,1,0:T(8,128)}, f32[352,1536]{1,0:T(8,128)}, f32[352,1536]...) custom-call(bf16[2,272,352]{2,1,0:T(8,128)(2,1)} %fusion.5.io_hbm, bf16[2,4,352,384]{3,2,1,0:T(8,128)(2,1)} %fusion.2.wa_hbm, ...), custom_call_target="tpu_custom_call" | custom-call | tf_op jit(solution)/shard_map/pallas_call | solution.py:1112
  313.1 0.7 reshape.34
  313.9 0.0 copy-start.2
  313.9 0.6 dynamic-slice_bitcast_fusion
  314.5 1.2 bitcast_convert_fusion
  315.6 1.2 copy.29
  316.8 1.2 copy.30
  317.9 0.6 fusion.6
  318.5 0.0 copy-done.2
  318.5 0.0 copy-start.5
  318.5 0.0 copy-start.1
  318.5 1.3 slice_bitcast_fusion
  319.8 1.0 copy.31
  320.9 0.0 copy-done.5
  320.9 0.6 copy.32
  321.5 0.6 slice_bitcast_fusion.3
  322.1 0.0 copy-done.1
  322.1 0.0 copy-start
  322.1 1.3 copy.35
  323.4 1.0 copy-done
  324.4 1.3 copy.36
  (2 shorter events, 0.0 us)
Async XLA Ops:
  2.0 3.2 copy-start.3
  2.0 3.2 copy-start.4
  313.9 4.6 %copy-start.2 = (f32[4,352,384]{2,1,0:T(8,128)S(1)}, f32[4,352,384]{2,1,0:T(8,128)}, u32[]{:S(2)}) copy-start(f32[4,352,384]{2,1,0:T(8,128)} %get-tuple-element.21) | copy-start | bytes 6488068
  318.5 2.3 copy-start.5
  318.5 3.5 %copy-start.1 = (f32[352,1536]{1,0:T(8,128)S(1)}, f32[352,1536]{1,0:T(8,128)}, u32[]{:S(2)}) copy-start(f32[352,1536]{1,0:T(8,128)} %get-tuple-element.24) | copy-start | bytes 6488068
  322.1 2.4 copy-start

commit v6 on v5

--- a/solution.py
+++ b/solution.py
@@ -17,9 +17,11 @@
 F32 = jnp.float32
 
 ROWS = 272
-STEP = 64
-CHUNK = 80
-LAST = 72
+START = (0, 80, 128, 176)
+SIZE = (80, 48, 48, 88)
+FIRST = (40, 24, 24, 40)
+CHUNK = 96
+LAST = 88
 BLK = 352
 PAD = 384
 HALF = 768
@@ -39,7 +41,7 @@
 
 
 def span(index):
-    return pl.ds(STEP * index, STEP if index < N - 1 else LAST)
+    return pl.ds(START[index], SIZE[index])
 
 
 def head_span(head):
@@ -106,17 +108,25 @@
     own_vec.start()
 
     def by_size(body):
+        @pl.when(c == 0)
+        def _():
+            body(SIZE[0])
+
+        @pl.when(jnp.logical_and(c > 0, c < N - 1))
+        def _():
+            body(SIZE[1])
+
         @pl.when(last)
         def _():
-            body(LAST)
-
-        @pl.when(jnp.logical_not(last))
-        def _():
-            body(STEP)
+            body(SIZE[N - 1])
+
+    begin = jnp.where(c < 2, 80 * c, 48 * c + 32)
+    count = jnp.where(c == 0, 5, jnp.where(last, 6, 3))
+    ahead = jnp.where(jnp.logical_or(c == 0, last), 3, 2)
 
     def come_start(u, src):
         for ct in range(N):
-            size = STEP if ct < N - 1 else LAST
+            size = SIZE[ct]
             source, target = src.at[span(ct)], mid.at[u, c, pl.ds(0, size)]
 
             @pl.when(c == ct)
@@ -172,7 +182,7 @@
         def sized(size):
             for p in range(N):
                 source = mid.at[u, p, pl.ds(0, size)]
-                target = dst.at[pl.ds(pl.multiple_of(STEP * c, 16), size)]
+                target = dst.at[pl.ds(pl.multiple_of(begin, 16), size)]
                 pltpu.make_async_copy(source, source, m1r.at[u, p]).wait()
 
                 @pl.when(c == p)
@@ -192,7 +202,7 @@
 
     def sent(u):
         for ct in range(N):
-            size = STEP if ct < N - 1 else LAST
+            size = SIZE[ct]
             rows = mid.at[u, 0, pl.ds(0, size)]
 
             if u < 2:
@@ -285,7 +295,7 @@
                 local_w(l, i, which).start()
 
     def half_rows(cs, h):
-        return pl.ds(STEP * cs + 32 * h, 32 if h == 0 or cs < N - 1 else LAST - 32)
+        return pl.ds(START[cs] + FIRST[cs] * h, FIRST[cs] if h == 0 else SIZE[cs] - FIRST[cs])
 
     halves = ((0, 0), (1, 0), (0, 1), (1, 1))
     targets = ((2, 1), (2, 0), (1, 3), (1, 2))
@@ -341,7 +351,7 @@
     inner = ((1, 0), (2, 3))
 
     def size_of(cs):
-        return STEP if cs < N - 1 else LAST
+        return SIZE[cs]
 
     def cols(h):
         return pl.ds(0, HALF) if h == 0 else pl.ds(HALF, D - HALF)
@@ -406,7 +416,7 @@
                     pltpu.make_async_copy(rows, rows, lr.at[n, h]).wait()
                     for start in range(0, size, 16):
                         width = min(16, size - start)
-                        mine = part[pl.ds(STEP * dest + start, width), cols(h)]
+                        mine = part[pl.ds(START[dest] + start, width), cols(h)]
                         value = rb[n, start : start + width, cols(h)].astype(F32)
                         rb[n, start : start + width, cols(h)] = (
                             value + mine.astype(F32)
@@ -450,20 +460,18 @@
         return pv[pl.ds(row, 1), :]
 
     def own_rows(x, t, value):
-        @pl.when(jnp.logical_or(t < 4, last))
-        def _():
-            x[pl.ds(pl.multiple_of(STEP * c + 16 * t, 16), 16), :] = value
-
-    valid = jnp.where(last, SEQ - STEP * (N - 1), STEP)
+        x[pl.ds(pl.multiple_of(begin + 16 * t, 16), 16), :] = value
+
+    valid = jnp.where(last, SEQ - START[N - 1], 16 * count)
 
     def masked(t, value):
         index = lax.broadcasted_iota(jnp.int32, (16, 1), 0) + 16 * t
         return jnp.where(index < valid, value, 0.0)
 
     def early(x, body):
-        lax.fori_loop(0, 2, body, 0)
+        lax.fori_loop(0, ahead, body, 0)
         gather_start(x, steps=(0,))
-        lax.fori_loop(2, CHUNK // 16, body, 0)
+        lax.fori_loop(ahead, count, body, 0)
         gather_start(x, steps=(1, 2, 3))
 
     def norm_forward(l, j, x, extra):
@@ -475,7 +483,7 @@
             spread_ = jnp.sum(v * v, axis=1, keepdims=True) / D - centre * centre
             scale = lax.rsqrt(spread_ + EPSILON)
             standard = (v - centre) * scale
-            std[l, j, rows, :] = standard
+            std[l, j, rows, :] = standard.astype(BF)
             inv[l, j, rows, :] = jnp.broadcast_to(scale, (16, 128))
             value = standard * vector(6 * l + j) + vector(6 * l + 2 + j)
             own_rows(x, t, value.astype(BF))
@@ -487,7 +495,7 @@
         def body(t, _):
             rows = pl.ds(pl.multiple_of(16 * t, 16), 16)
             e = received(rows)
-            standard = std[l, j, rows, :]
+            standard = std[l, j, rows, :].astype(F32)
             gain_term = masked(t, e * standard)
             vsum[pl.ds(6 * l + j, 1), :] += jnp.sum(gain_term, axis=0, keepdims=True)
             vsum[pl.ds(6 * l + 2 + j, 1), :] += jnp.sum(masked(t, e), axis=0, keepdims=True)
@@ -515,7 +523,7 @@
 
             @pl.when(l == 0)
             def _():
-                lax.fori_loop(0, CHUNK // 16, body, 0)
+                lax.fori_loop(0, count, body, 0)
 
     def tiles(count, body):
         lax.fori_loop(0, count, lambda n, _: (body(n), 0)[1], 0)
@@ -611,7 +619,7 @@
         def _():
             come_wait(1, cin)
             assemble(cin, gst)
-            lax.fori_loop(0, CHUNK // 16, top_rows, 0)
+            lax.fori_loop(0, count, top_rows, 0)
             gather_start(gtop, second_z)
 
         need_w(l, 0)
@@ -675,7 +683,7 @@
             add_pass(0, 1, 2, 3)
             close_w(1, 0)
             add_wait()
-            lax.fori_loop(0, CHUNK // 16, settle(l, recv), 0)
+            lax.fori_loop(0, count, settle(l, recv), 0)
 
         return 0
 
@@ -918,9 +926,9 @@
         @pl.when(step > 0)
         def _():
             add_wait(side)
-            lax.fori_loop(0, CHUNK // 16, settle(LAYERS - 1, recv2), 0)
+            lax.fori_loop(0, count, settle(LAYERS - 1, recv2), 0)
             for k in range(N):
-                oblk[k] = st[:, BLK * k : BLK * (k + 1)].astype(BF)
+                oblk[k] = st[0:LAST, BLK * k : BLK * (k + 1)].astype(BF)
             go_start(2)
 
         da[...] = dot(gmid[...], wa[l, 3]).astype(BF)
@@ -965,7 +973,7 @@
     go_wait(2, out_hbm)
     sent(2)
     for k in range(N):
-        oblk[k] = gst[:, BLK * k : BLK * (k + 1)].astype(BF)
+        oblk[k] = gst[0:LAST, BLK * k : BLK * (k + 1)].astype(BF)
     go_start(3)
 
     def c_copy(k):
@@ -1056,7 +1064,7 @@
         vmem((LAYERS, ROWS, 128), F32),
         vmem((LAYERS, 2, ROWS, HALF), BF),
         vmem((LAYERS, 2, ROWS, HALF), BF),
-        vmem((LAYERS, 2, CHUNK, D), F32),
+        vmem((LAYERS, 2, CHUNK, D), BF),
         vmem((LAYERS, 2, CHUNK, 128), F32),
         vmem((ROWS, D), BF),
         vmem((ROWS, D), BF),
@@ -1067,8 +1075,8 @@
         vmem((CHUNK, D), F32),
         vmem((N, CHUNK, BLK), BF),
         vmem((N, CHUNK, BLK), BF),
-        vmem((N, CHUNK, BLK), BF),
-        vmem((4, N, CHUNK, BLK), BF),
+        vmem((N, LAST, BLK), BF),
+        vmem((4, N, LAST, BLK), BF),
         vmem((N, 16, BLK), F32),
         vmem((16, D), F32),
         vmem((2, ROWS, HALF), BF),

time: 326 us -> 334 us (1.025)
  Pallas kernels: 307 us -> 315 us
    pallas_call x1, Pallas kernels: 307 us -> 315 us  [fused(): pl.pallas_call(kernel, out_shape=(shape((ROWS, BLK), BF), shape((ROWS, BL...]
where the time goes in v6:
time: 334 us; the launch traced here: 333 us
  Pallas kernels  315 us (94%)
  local copies, waits for them, and re-layouts  12.8 us (4%)
  other arithmetic  5.11 us (2%)
    pallas_call x1, Pallas kernels, fused(): pl.pallas_call(kernel, out_shape=(shape((ROWS, BLK), BF), shape((ROWS, BL...  315 us
    unnamed x20, local copies, waits for them, and re-layouts  9.03 us

profile of v6, /device:TPU:0, one launch (start us, length us, event | category | flops | bytes accessed | tf_op | source)
XLA Modules:
  0.0 333.5 jit_solution(7664519615204532139)
XLA Ops:
  0.6 1.3 copy.28
  2.0 0.0 copy-start.3
  2.0 0.0 copy-start.4
  2.0 3.1 fusion.2.wa_hbm
  5.2 0.0 copy-done.3
  5.2 0.0 copy-done.4
  5.2 0.8 fusion.5.io_hbm
  6.0 314.8 %shard_map.211 = (bf16[272,352]{1,0:T(8,128)(2,1)}, bf16[272,352]{1,0:T(8,128)(2,1)}, f32[4,352,384]{2,1,0:T(8,128)}, f32[352,1536]{1,0:T(8,128)}, f32[352,1536]...) custom-call(bf16[2,272,352]{2,1,0:T(8,128)(2,1)} %fusion.5.io_hbm, bf16[2,4,352,384]{3,2,1,0:T(8,128)(2,1)} %fusion.2.wa_hbm, ...), custom_call_target="tpu_custom_call" | custom-call | tf_op jit(solution)/shard_map/pallas_call | solution.py:1120
  320.8 0.7 reshape.34
  321.6 0.0 copy-start.2
  321.6 0.6 dynamic-slice_bitcast_fusion
  322.1 1.2 bitcast_convert_fusion
  323.3 1.2 copy.29
  324.5 1.2 copy.30
  325.6 0.6 fusion.6
  326.2 0.0 copy-done.2
  326.2 0.0 copy-start.5
  326.2 0.0 copy-start.1
  326.2 1.3 slice_bitcast_fusion
  327.5 1.0 copy.31
  328.5 0.0 copy-done.5
  328.6 0.6 copy.32
  329.2 0.6 slice_bitcast_fusion.3
  329.7 0.0 copy-done.1
  329.7 0.0 copy-start
  329.7 1.3 copy.35
  331.1 1.0 copy-done
  332.1 1.3 copy.36
  (2 shorter events, 0.0 us)
Async XLA Ops:
  2.0 3.2 copy-start.3
  2.0 3.2 copy-start.4
  321.6 4.6 %copy-start.2 = (f32[4,352,384]{2,1,0:T(8,128)S(1)}, f32[4,352,384]{2,1,0:T(8,128)}, u32[]{:S(2)}) copy-start(f32[4,352,384]{2,1,0:T(8,128)} %get-tuple-element.21) | copy-start | bytes 6488068
  326.2 2.3 copy-start.5
  326.2 3.5 %copy-start.1 = (f32[352,1536]{1,0:T(8,128)S(1)}, f32[352,1536]{1,0:T(8,128)}, u32[]{:S(2)}) copy-start(f32[352,1536]{1,0:T(8,128)} %get-tuple-element.24) | copy-start | bytes 6488068
  329.7 2.4 copy-start
